TPU v7x, 32 devices: a whole 2x2x4 slice. The times are simulated.
32 devices in a mesh: ctx: 8 (over y, x, core), fsdp: 4 (over z).
Axes of the slice: x: 2, y: 2, z: 4, core: 2. Of those that a mesh axis runs over, the one named last changes fastest.
Arguments:
- tokens: bfloat16 [4, 2048, 1024], P('fsdp', 'ctx'), may hold values from -6 to 6
- cotangent: bfloat16 [4, 2048, 1024], P('fsdp', 'ctx'), may hold values from -6 to 6
- block_map: int32 [4, 16], P('fsdp'), may hold values from 0 to 15, as said below
- attn_gain: bfloat16 [1024], P(('ctx', 'fsdp')), may hold values from 0.5 to 1.5
- query_weight: bfloat16 [1024, 2048], P(('ctx', 'fsdp')), may hold values from -0.1875 to 0.1875
- key_weight: bfloat16 [1024, 1024], P(('ctx', 'fsdp')), may hold values from -0.1875 to 0.1875
- value_weight: bfloat16 [1024, 1024], P(('ctx', 'fsdp')), may hold values from -0.1875 to 0.1875
- query_gain: bfloat16 [128], P(('ctx', 'fsdp')), may hold values from 0.5 to 1.5
- key_gain: bfloat16 [128], P(('ctx', 'fsdp')), may hold values from 0.5 to 1.5
- output_weight: bfloat16 [2048, 1024], P(('ctx', 'fsdp')), may hold values from -4 to 4
- mlp_gain: bfloat16 [1024], P(('ctx', 'fsdp')), may hold values from 0.5 to 1.5
- gate_weight: bfloat16 [1024, 3072], P(('ctx', 'fsdp')), may hold values from -0.1875 to 0.1875
- up_weight: bfloat16 [1024, 3072], P(('ctx', 'fsdp')), may hold values from -0.1875 to 0.1875
- down_weight: bfloat16 [3072, 1024], P(('ctx', 'fsdp')), may hold values from -0.109375 to 0.109375
Outputs:
- output: bfloat16 [4, 2048, 1024], P('fsdp', 'ctx')
- grad_tokens: bfloat16 [4, 2048, 1024], P('fsdp', 'ctx')
- grad_attn_gain: float32 [1024], P(('ctx', 'fsdp'))
- grad_query_weight: float32 [1024, 2048], P(('ctx', 'fsdp'))
- grad_key_weight: float32 [1024, 1024], P(('ctx', 'fsdp'))
- grad_value_weight: float32 [1024, 1024], P(('ctx', 'fsdp'))
- grad_query_gain: float32 [128], P(('ctx', 'fsdp'))
- grad_key_gain: float32 [128], P(('ctx', 'fsdp'))
- grad_output_weight: float32 [2048, 1024], P(('ctx', 'fsdp'))
- grad_mlp_gain: float32 [1024], P(('ctx', 'fsdp'))
- grad_gate_weight: float32 [1024, 3072], P(('ctx', 'fsdp'))
- up_projection_gradient: float32 [1024, 3072], P(('ctx', 'fsdp'))
- grad_down_weight: float32 [3072, 1024], P(('ctx', 'fsdp'))
Inputs may be any that keep to these rules, and one draw needn't show every extreme that they name: Each row of block_map holds every block number of its sequence once, and the two slots 2c and 2c + 1 of one index c of ctx hold blocks b and 15 - b.
All inputs are finite; a program needn't handle non-finite values.
Results may differ from a plain program's by a relative error of at most 0.018.
Values may be sent and summed in bfloat16 or wider, within the bound.
A program may use at most 256 MiB of HBM per device.

v0:
```python
import math

import jax
import jax.numpy as jnp
from jax import lax
from jax.sharding import PartitionSpec as P

H = 16
KVH = 8
HD = 128
BLK = 128


EPSILON = 1e-06
ROPE_BASE = 1000000.0


def rope_tables(positions):
    half = HD // 2
    freqs = jnp.exp(jnp.arange(half, dtype=jnp.float32) * (-2.0 * math.log(ROPE_BASE) / HD))
    angles = positions.astype(jnp.float32)[..., None] * freqs
    cosine = jnp.cos(angles)
    sine = jnp.sin(angles)
    return (jnp.concatenate([cosine, cosine], axis=-1), jnp.concatenate([sine, sine], axis=-1))


def rotate(value_vectors):
    half = value_vectors.shape[-1] // 2
    return jnp.concatenate([-value_vectors[..., half:], value_vectors[..., :half]], axis=-1)


def unrotate(value_vectors):
    half = value_vectors.shape[-1] // 2
    return jnp.concatenate([value_vectors[..., half:], -value_vectors[..., :half]], axis=-1)


def left_dot(left, right):
    return lax.dot_general(
        left, right, (((0,), (0,)), ((), ())), preferred_element_type=jnp.float32
    )


def right_dot(left, right):
    return lax.dot_general(
        left, right, (((1,), (1,)), ((), ())), preferred_element_type=jnp.float32
    )


def plain_dot(left, right):
    return jnp.dot(left, right, preferred_element_type=jnp.float32)


def norm_back(grad_normed, unit, inverse, gain):
    scaled = grad_normed * gain
    return inverse * (scaled - unit * jnp.mean(scaled * unit, axis=-1, keepdims=True))


def on_device(
    tokens,
    cotangent,
    block_map,
    attn_gain,
    query_weight,
    key_weight,
    value_weight,
    query_gain,
    key_gain,
    output_weight,
    mlp_gain,
    gate_weight,
    up_weight,
    down_weight,
):
    groups, pair_rows, width = tokens.shape
    rows_all = groups * pair_rows
    context_length = pair_rows * lax.axis_size("ctx")
    key_rows = min(512, context_length)
    key_steps = context_length // key_rows
    ratio = H // KVH
    scale = HD ** (-0.5)
    attn_full = (
        lax.all_gather(attn_gain, ("ctx", "fsdp"), axis=0, tiled=True),
        lax.all_gather(query_weight, ("ctx", "fsdp"), axis=0, tiled=True),
        lax.all_gather(key_weight, ("ctx", "fsdp"), axis=0, tiled=True),
        lax.all_gather(value_weight, ("ctx", "fsdp"), axis=0, tiled=True),
        lax.all_gather(query_gain, ("ctx", "fsdp"), axis=0, tiled=True),
        lax.all_gather(key_gain, ("ctx", "fsdp"), axis=0, tiled=True),
        lax.all_gather(output_weight, ("ctx", "fsdp"), axis=0, tiled=True),
    )
    mlp_full = (
        lax.all_gather(mlp_gain, ("ctx", "fsdp"), axis=0, tiled=True),
        lax.all_gather(gate_weight, ("ctx", "fsdp"), axis=0, tiled=True),
        lax.all_gather(up_weight, ("ctx", "fsdp"), axis=0, tiled=True),
        lax.all_gather(down_weight, ("ctx", "fsdp"), axis=0, tiled=True),
    )
    gain_one = attn_full[0].astype(jnp.float32)
    full_query, full_key, full_value = (attn_full[1], attn_full[2], attn_full[3])
    query_scale = attn_full[4].astype(jnp.float32)
    key_scale = attn_full[5].astype(jnp.float32)
    full_output = attn_full[6]
    gain_two = mlp_full[0].astype(jnp.float32)
    full_gate, full_up, full_down = (mlp_full[1], mlp_full[2], mlp_full[3])
    offsets = jnp.arange(BLK, dtype=jnp.int32)
    own_blocks = lax.dynamic_slice_in_dim(block_map, 2 * lax.axis_index("ctx"), 2, 1)
    query_spots = (own_blocks[:, :, None] * BLK + offsets).reshape(groups, pair_rows)
    key_spots = (block_map[:, :, None] * BLK + offsets).reshape(groups, context_length)
    cosine, sine = rope_tables(query_spots)
    cosine = cosine.reshape(rows_all, 1, HD)
    sine = sine.reshape(rows_all, 1, HD)
    inputs = tokens.reshape(rows_all, width).astype(jnp.float32)
    inverse_one = lax.rsqrt(jnp.mean(inputs * inputs, axis=-1, keepdims=True) + EPSILON)
    normal_one = inputs * inverse_one
    normed = (normal_one * gain_one).astype(jnp.bfloat16)
    query_raw = plain_dot(normed, full_query).reshape(rows_all, H, HD)
    key_raw = plain_dot(normed, full_key).reshape(rows_all, KVH, HD)
    value_low = plain_dot(normed, full_value).astype(jnp.bfloat16)
    query_inverse = lax.rsqrt(jnp.mean(query_raw * query_raw, axis=-1, keepdims=True) + EPSILON)
    query_unit = query_raw * query_inverse
    query_normed = query_unit * query_scale
    query_low = (query_normed * cosine + rotate(query_normed) * sine).astype(jnp.bfloat16)
    key_inverse = lax.rsqrt(jnp.mean(key_raw * key_raw, axis=-1, keepdims=True) + EPSILON)
    key_unit_vector = key_raw * key_inverse
    key_normed = key_unit_vector * key_scale
    key_low = (key_normed * cosine + rotate(key_normed) * sine).astype(jnp.bfloat16)
    key_slab = key_low.reshape(groups, pair_rows, KVH * HD)
    value_slab = value_low.reshape(groups, pair_rows, KVH * HD)
    key_all, value_all = (
        lax.all_gather(key_slab, "ctx", axis=1, tiled=True),
        lax.all_gather(value_slab, "ctx", axis=1, tiled=True),
    )
    query_grouped = query_low.reshape(groups, pair_rows, KVH, ratio, HD)

    def block_inputs(key_source, value_source, start):
        keys_block = lax.dynamic_slice_in_dim(key_source, start, key_rows, 1).reshape(
            groups, key_rows, KVH, HD
        )
        values_block = lax.dynamic_slice_in_dim(value_source, start, key_rows, 1).reshape(
            groups, key_rows, KVH, HD
        )
        spots_block = lax.dynamic_slice_in_dim(key_spots, start, key_rows, 1)
        scores = (
            jnp.einsum(
                "gqkrd,gtkd->gkrqt", query_grouped, keys_block, preferred_element_type=jnp.float32
            )
            * scale
        )
        allowed = spots_block[:, None, None, None, :] <= query_spots[:, None, None, :, None]
        weights = jnp.where(allowed, jnp.exp(scores), 0.0)
        return (keys_block, values_block, weights)

    def forward_block(carry, block_index):
        summed, totals = carry
        keys_block, values_block, weights = block_inputs(key_all, value_all, block_index * key_rows)
        totals = totals + jnp.sum(weights, axis=-1)
        summed = summed + jnp.einsum(
            "gkrqt,gtkd->gqkrd",
            weights.astype(jnp.bfloat16),
            values_block,
            preferred_element_type=jnp.float32,
        )
        return ((summed, totals), None)

    start_sum = jnp.zeros((groups, pair_rows, KVH, ratio, HD), jnp.float32)
    start_total = jnp.zeros((groups, KVH, ratio, pair_rows), jnp.float32)
    (summed, totals), unused = lax.scan(
        forward_block, (start_sum, start_total), jnp.arange(key_steps)
    )
    row_totals = jnp.transpose(totals, (0, 3, 1, 2))[..., None]
    attended = summed / row_totals
    attended_low = attended.reshape(rows_all, H * HD).astype(jnp.bfloat16)
    middle = inputs + plain_dot(attended_low, full_output)
    inverse_two = lax.rsqrt(jnp.mean(middle * middle, axis=-1, keepdims=True) + EPSILON)
    normal_two = middle * inverse_two
    normed_two = (normal_two * gain_two).astype(jnp.bfloat16)
    gate = plain_dot(normed_two, full_gate)
    upper = plain_dot(normed_two, full_up)
    sigmoid_gate = jax.nn.sigmoid(gate)
    activated = gate * sigmoid_gate
    hidden = (activated * upper).astype(jnp.bfloat16)
    result = middle + plain_dot(hidden, full_down)
    output = result.astype(jnp.bfloat16).reshape(groups, pair_rows, width)
    attn_back = (
        lax.all_gather(attn_gain, ("ctx", "fsdp"), axis=0, tiled=True),
        lax.all_gather(query_weight, ("ctx", "fsdp"), axis=0, tiled=True),
        lax.all_gather(key_weight, ("ctx", "fsdp"), axis=0, tiled=True),
        lax.all_gather(value_weight, ("ctx", "fsdp"), axis=0, tiled=True),
        lax.all_gather(query_gain, ("ctx", "fsdp"), axis=0, tiled=True),
        lax.all_gather(key_gain, ("ctx", "fsdp"), axis=0, tiled=True),
        lax.all_gather(output_weight, ("ctx", "fsdp"), axis=0, tiled=True),
    )
    mlp_back = (
        lax.all_gather(mlp_gain, ("ctx", "fsdp"), axis=0, tiled=True),
        lax.all_gather(gate_weight, ("ctx", "fsdp"), axis=0, tiled=True),
        lax.all_gather(up_weight, ("ctx", "fsdp"), axis=0, tiled=True),
        lax.all_gather(down_weight, ("ctx", "fsdp"), axis=0, tiled=True),
    )
    full_query, full_key, full_value = (attn_back[1], attn_back[2], attn_back[3])
    full_output = attn_back[6]
    full_gate, full_up, full_down = (mlp_back[1], mlp_back[2], mlp_back[3])
    upstream = cotangent.reshape(rows_all, width)
    grad_down = left_dot(hidden, upstream)
    grad_hidden = right_dot(upstream, full_down)
    grad_gate = (grad_hidden * upper * sigmoid_gate * (1.0 + gate * (1.0 - sigmoid_gate))).astype(
        jnp.bfloat16
    )
    grad_upper = (grad_hidden * activated).astype(jnp.bfloat16)
    gate_matrix_gradient = left_dot(normed_two, grad_gate)
    grad_wup = left_dot(normed_two, grad_upper)
    grad_normed_two = right_dot(grad_gate, full_gate) + right_dot(grad_upper, full_up)
    grad_gaintwo = jnp.sum(grad_normed_two * normal_two, axis=0)
    grad_middle = upstream.astype(jnp.float32) + norm_back(
        grad_normed_two, normal_two, inverse_two, gain_two
    )
    mlp_sums = (
        lax.psum_scatter(grad_gaintwo, ("ctx", "fsdp"), scatter_dimension=0, tiled=True),
        lax.psum_scatter(gate_matrix_gradient, ("ctx", "fsdp"), scatter_dimension=0, tiled=True),
        lax.psum_scatter(grad_wup, ("ctx", "fsdp"), scatter_dimension=0, tiled=True),
        lax.psum_scatter(grad_down, ("ctx", "fsdp"), scatter_dimension=0, tiled=True),
    )
    branch_grad = grad_middle.astype(jnp.bfloat16)
    grad_woutput = left_dot(attended_low, branch_grad)
    grad_attended = right_dot(branch_grad, full_output).reshape(groups, pair_rows, KVH, ratio, HD)
    grad_summed = (grad_attended / row_totals).astype(jnp.bfloat16)
    drift_rows = jnp.sum(grad_attended * attended, axis=-1) / row_totals[..., 0]
    drift = jnp.transpose(drift_rows, (0, 2, 3, 1))
    key_all, value_all = (
        lax.all_gather(key_slab, "ctx", axis=1, tiled=True),
        lax.all_gather(value_slab, "ctx", axis=1, tiled=True),
    )

    def backward_block(carry, block_index):
        grad_query, grad_keys, grad_values = carry
        start = block_index * key_rows
        keys_block, values_block, weights = block_inputs(key_all, value_all, start)
        through = jnp.einsum(
            "gqkrd,gtkd->gkrqt", grad_summed, values_block, preferred_element_type=jnp.float32
        )
        grad_scores = (weights * (through - drift[..., None])).astype(jnp.bfloat16)
        grad_query = grad_query + jnp.einsum(
            "gkrqt,gtkd->gqkrd", grad_scores, keys_block, preferred_element_type=jnp.float32
        )
        key_part = (
            jnp.einsum(
                "gkrqt,gqkrd->gtkd", grad_scores, query_grouped, preferred_element_type=jnp.float32
            )
            * scale
        )
        value_part = jnp.einsum(
            "gkrqt,gqkrd->gtkd",
            weights.astype(jnp.bfloat16),
            grad_summed,
            preferred_element_type=jnp.float32,
        )
        grad_keys = lax.dynamic_update_slice_in_dim(
            grad_keys, key_part.reshape(groups, key_rows, KVH * HD), start, 1
        )
        grad_values = lax.dynamic_update_slice_in_dim(
            grad_values, value_part.reshape(groups, key_rows, KVH * HD), start, 1
        )
        return ((grad_query, grad_keys, grad_values), None)

    start_keys = jnp.zeros((groups, context_length, KVH * HD), jnp.float32)
    (grad_query, grad_keys, grad_values), unused = lax.scan(
        backward_block, (start_sum, start_keys, start_keys), jnp.arange(key_steps)
    )
    own_keys, own_values = (
        lax.psum_scatter(
            grad_keys.astype(jnp.bfloat16), "ctx", scatter_dimension=1, tiled=True
        ).astype(jnp.float32),
        lax.psum_scatter(
            grad_values.astype(jnp.bfloat16), "ctx", scatter_dimension=1, tiled=True
        ).astype(jnp.float32),
    )
    grad_qrot = (grad_query * scale).reshape(rows_all, H, HD)
    grad_qnormed = grad_qrot * cosine + unrotate(grad_qrot) * sine
    grad_qscale = jnp.sum(grad_qnormed * query_unit, axis=(0, 1))
    grad_qraw = (
        norm_back(grad_qnormed, query_unit, query_inverse, query_scale)
        .reshape(rows_all, H * HD)
        .astype(jnp.bfloat16)
    )
    grad_krot = own_keys.reshape(rows_all, KVH, HD)
    key_normalized_gradient = grad_krot * cosine + unrotate(grad_krot) * sine
    key_rescale_gradient = jnp.sum(key_normalized_gradient * key_unit_vector, axis=(0, 1))
    grad_kraw = (
        norm_back(key_normalized_gradient, key_unit_vector, key_inverse, key_scale)
        .reshape(rows_all, KVH * HD)
        .astype(jnp.bfloat16)
    )
    grad_vraw = own_values.reshape(rows_all, KVH * HD).astype(jnp.bfloat16)
    grad_wquery = left_dot(normed, grad_qraw)
    grad_wkey = left_dot(normed, grad_kraw)
    grad_wvalue = left_dot(normed, grad_vraw)
    grad_normed = (
        right_dot(grad_qraw, full_query)
        + right_dot(grad_kraw, full_key)
        + right_dot(grad_vraw, full_value)
    )
    grad_gainone = jnp.sum(grad_normed * normal_one, axis=0)
    grad_inputs = grad_middle + norm_back(grad_normed, normal_one, inverse_one, gain_one)
    attn_sums = (
        lax.psum_scatter(grad_gainone, ("ctx", "fsdp"), scatter_dimension=0, tiled=True),
        lax.psum_scatter(grad_wquery, ("ctx", "fsdp"), scatter_dimension=0, tiled=True),
        lax.psum_scatter(grad_wkey, ("ctx", "fsdp"), scatter_dimension=0, tiled=True),
        lax.psum_scatter(grad_wvalue, ("ctx", "fsdp"), scatter_dimension=0, tiled=True),
        lax.psum_scatter(grad_qscale, ("ctx", "fsdp"), scatter_dimension=0, tiled=True),
        lax.psum_scatter(key_rescale_gradient, ("ctx", "fsdp"), scatter_dimension=0, tiled=True),
        lax.psum_scatter(grad_woutput, ("ctx", "fsdp"), scatter_dimension=0, tiled=True),
    )
    return (
        output,
        grad_inputs.astype(jnp.bfloat16).reshape(groups, pair_rows, width),
        attn_sums[0],
        attn_sums[1],
        attn_sums[2],
        attn_sums[3],
        attn_sums[4],
        attn_sums[5],
        attn_sums[6],
        mlp_sums[0],
        mlp_sums[1],
        mlp_sums[2],
        mlp_sums[3],
    )


def solution(mesh):
    return jax.shard_map(
        on_device,
        mesh=mesh,
        in_specs=(
            P("fsdp", "ctx", None),
            P("fsdp", "ctx", None),
            P("fsdp", None),
            P(("ctx", "fsdp")),
            P(("ctx", "fsdp"), None),
            P(("ctx", "fsdp"), None),
            P(("ctx", "fsdp"), None),
            P(("ctx", "fsdp")),
            P(("ctx", "fsdp")),
            P(("ctx", "fsdp"), None),
            P(("ctx", "fsdp")),
            P(("ctx", "fsdp"), None),
            P(("ctx", "fsdp"), None),
            P(("ctx", "fsdp"), None),
        ),
        out_specs=(
            P("fsdp", "ctx", None),
            P("fsdp", "ctx", None),
            P(("ctx", "fsdp")),
            P(("ctx", "fsdp"), None),
            P(("ctx", "fsdp"), None),
            P(("ctx", "fsdp"), None),
            P(("ctx", "fsdp")),
            P(("ctx", "fsdp")),
            P(("ctx", "fsdp"), None),
            P(("ctx", "fsdp")),
            P(("ctx", "fsdp"), None),
            P(("ctx", "fsdp"), None),
            P(("ctx", "fsdp"), None),
        ),
        check_vma=False,
    )
```

profile of v0, /device:TPU:0, one launch (start us, length us, event | category | flops | bytes accessed | tf_op | source)
XLA Modules:
  0.0 1933.9 jit_solution(4478477780481027640)
XLA Ops:
  12.9 42.2 %all-reduce.9 = (bf16[1024]{0:T(1024)(128)(2,1)S(1)}, bf16[128]{0:T(256)(128)(2,1)S(1)}, bf16[128]{0:T(256)(128)(2,1)S(1)}, bf16[1024]{0:T(1024)(128)(2,1)S(1)}) all-reduce(bf16[1024]{0:T(1024)(128)(2,1)S(1)} %dynamic-update-slice, bf16[128]{0:T(256)(128)(2,1)S(1)} %dynamic-update-slice.1, ...), channel_id=1, replica_groups=mesh['ctx'=8,'fsdp'=4] {'ctx','fsdp'}, use_global_device_ids=true, to_apply=%add | all-reduce | flops 2304 | bytes 9216
  56.3 13.9 all-gather.11.cloned.1.call-done
  74.2 54.2 %all-gather.13.cloned.1.call-done = bf16[1024,1024]{1,0:T(8,128)(2,1)} async-done(((bf16[32,1024]{1,0:T(8,128)(2,1)}), bf16[1024,1024]{1,0:T(8,128)(2,1)}) %all-gather.13.cloned.1.call-update) | async-done | bytes 2097168 | tf_op jit(solution)/shard_map/all_gather | solution.py:84
  139.4 52.5 %all-gather.17.cloned.1.call-done = bf16[1024,2048]{1,0:T(8,128)(2,1)} async-done(((bf16[32,2048]{1,0:T(8,128)(2,1)}), bf16[1024,2048]{1,0:T(8,128)(2,1)}) %all-gather.17.cloned.1.call-update) | async-done | bytes 4194320 | tf_op jit(solution)/shard_map/all_gather | solution.py:83
  205.5 24.1 %all-gather.27.cloned.1.call-done = bf16[2048,1024]{1,0:T(8,128)(2,1)} async-done(((bf16[256,1024]{1,0:T(8,128)(2,1)}), bf16[2048,1024]{1,0:T(8,128)(2,1)}) %all-gather.27.cloned.1.call-update) | async-done | bytes 4194320 | tf_op jit(solution)/shard_map/all_gather | solution.py:129
  236.1 33.1 %all-gather.15.cloned.1.call-done = bf16[1,2048,1024]{1,2,0:T(8,128)(2,1)} async-done(((bf16[1,256,1024]{1,2,0:T(8,128)(2,1)}), bf16[1,2048,1024]{1,2,0:T(8,128)(2,1)}) %all-gather.15.cloned.1.call-update) | async-done | bytes 4194320 | tf_op jit(solution)/shard_map/all_gather | solution.py:128
  269.3 61.5 %while.28 = (s32[]{:T(128)}, f32[1,256,8,2,128]{1,4,3,2,0:T(8,128)}, f32[1,8,2,256]{3,2,1,0:T(2,128)S(1)}, s32[4]{0:T(128)S(1)}, bf16[1,2048,1024]{1,2,0:T(8,128...) while((s32[]{:T(128)}, ...), condition=%wide.region_5.6_spmd.clone, body=%wide.region_3.5_spmd.clone.sunk | while | flops 1087508736 | bytes 32973044 | solution.py:165
  338.8 65.9 %all-gather.21.cloned.1.call-done = bf16[1024,3072]{1,0:T(8,128)(2,1)} async-done(((bf16[32,3072]{1,0:T(8,128)(2,1)}), bf16[1024,3072]{1,0:T(8,128)(2,1)}) %all-gather.21.cloned.1.call-update) | async-done | bytes 6291472 | tf_op jit(solution)/shard_map/all_gather | solution.py:92
  411.0 64.5 %all-gather.23.cloned.1.call-done = bf16[1024,3072]{1,0:T(8,128)(2,1)} async-done(((bf16[32,3072]{1,0:T(8,128)(2,1)}), bf16[1024,3072]{1,0:T(8,128)(2,1)}) %all-gather.23.cloned.1.call-update) | async-done | bytes 6291472 | tf_op jit(solution)/shard_map/all_gather | solution.py:93
  481.7 64.4 %all-gather.25.cloned.1.call-done = bf16[3072,1024]{1,0:T(8,128)(2,1)} async-done(((bf16[96,1024]{1,0:T(8,128)(2,1)}), bf16[3072,1024]{1,0:T(8,128)(2,1)}) %all-gather.25.cloned.1.call-update) | async-done | bytes 6291472 | tf_op jit(solution)/shard_map/all_gather | solution.py:94
  546.1 9.9 multiply_convert_fusion
  574.0 92.3 %while.29 = (s32[]{:T(128)}, f32[1,256,8,2,128]{1,4,3,2,0:T(8,128)S(1)}, bf16[1,2048,1024]{1,2,0:T(8,128)(2,1)}, bf16[1,2048,1024]{1,2,0:T(8,128)(2,1)}, s32[4]{...) while((s32[]{:T(128)}, ...), condition=%wide.region_10.11_spmd.clone, body=%wide.region_9.10_spmd.clone.sunk | while | flops 2703360256 | bytes 156656048 | solution.py:263
  667.0 48.9 %reduce-scatter.10.cloned.1.call-done = bf16[1,256,1024]{1,2,0:T(8,128)(2,1)} async-done(((bf16[1,2048,1024]{1,2,0:T(8,128)(2,1)}), bf16[1,256,1024]{1,2,0:T(8,128)(2,1)}) %reduce-scatter.10.cloned.1.call-update) | async-done | bytes 524304 | tf_op jit(solution)/shard_map/reduce_scatter | solution.py:267
  723.4 47.0 %reduce-scatter.12.cloned.1.call-done = bf16[1,256,1024]{1,2,0:T(8,128)(2,1)} async-done(((bf16[1,2048,1024]{1,2,0:T(8,128)(2,1)}), bf16[1,256,1024]{1,2,0:T(8,128)(2,1)}) %reduce-scatter.12.cloned.1.call-update) | async-done | bytes 524304 | tf_op jit(solution)/shard_map/reduce_scatter | solution.py:270
  791.0 7.8 fusion.98
  807.7 7.9 fusion.67
  828.9 40.4 %all-reduce.8 = (f32[1024]{0:T(1024)S(1)}, f32[128]{0:T(128)S(1)}, f32[128]{0:T(128)S(1)}, f32[1024]{0:T(1024)S(1)}) all-reduce(f32[1024]{0:T(1024)S(1)} %get-tuple-element.262, f32[128]{0:T(128)S(1)} %get-tuple-element.256, f32[128]{0:T(128)S(1)} %get-tuple-element.258, ...), channel_id=5, replica_groups=mesh['ctx'=8,'fsdp'=4] {'ctx','fsdp'}, use_global_device_ids=true, to_apply=%region_17.18.clone | all-reduce | flops 2304 | bytes 18432
  872.8 50.2 %reduce-scatter.16.cloned.1.call-done = f32[32,1024]{1,0:T(8,128)} async-done(((f32[1024,1024]{1,0:T(8,128)}), f32[32,1024]{1,0:T(8,128)}) %reduce-scatter.16.cloned.1.call-update) | async-done | bytes 131088 | tf_op jit(solution)/shard_map/reduce_scatter | solution.py:304
  923.0 150.8 %reduce-scatter.18.cloned.1.call-done = f32[32,1024]{1,0:T(8,128)} async-done(((f32[1024,1024]{1,0:T(8,128)}), f32[32,1024]{1,0:T(8,128)}) %reduce-scatter.18.cloned.1.call-update) | async-done | bytes 131088 | tf_op jit(solution)/shard_map/reduce_scatter | solution.py:305
  1073.8 187.3 %reduce-scatter.14.cloned.1.call-done = f32[32,2048]{1,0:T(8,128)} async-done(((f32[1024,2048]{1,0:T(8,128)}), f32[32,2048]{1,0:T(8,128)}) %reduce-scatter.14.cloned.1.call-update) | async-done | bytes 262160 | tf_op jit(solution)/shard_map/reduce_scatter | solution.py:303
  1261.1 186.2 %reduce-scatter.20.cloned.1.call-done = f32[64,1024]{1,0:T(8,128)} async-done(((f32[2048,1024]{1,0:T(8,128)}), f32[64,1024]{1,0:T(8,128)}) %reduce-scatter.20.cloned.1.call-update) | async-done | bytes 262160 | tf_op jit(solution)/shard_map/reduce_scatter | solution.py:308
  1447.2 159.0 %reduce-scatter.22.cloned.1.call-done = f32[32,3072]{1,0:T(8,128)} async-done(((f32[1024,3072]{1,0:T(8,128)}), f32[32,3072]{1,0:T(8,128)}) %reduce-scatter.22.cloned.1.call-update) | async-done | bytes 393232 | tf_op jit(solution)/shard_map/reduce_scatter | solution.py:216
  1606.3 160.3 %reduce-scatter.24.cloned.1.call-done = f32[32,3072]{1,0:T(8,128)} async-done(((f32[1024,3072]{1,0:T(8,128)}), f32[32,3072]{1,0:T(8,128)}) %reduce-scatter.24.cloned.1.call-update) | async-done | bytes 393232 | tf_op jit(solution)/shard_map/reduce_scatter | solution.py:217
  1766.5 160.3 %reduce-scatter.26.cloned.1.call-done = f32[96,1024]{1,0:T(8,128)} async-done(((f32[3072,1024]{1,0:T(8,128)}), f32[96,1024]{1,0:T(8,128)}) %reduce-scatter.26.cloned.1.call-update) | async-done | bytes 393232 | tf_op jit(solution)/shard_map/reduce_scatter | solution.py:218
  (354 shorter events, 281.7 us)
Async XLA Ops:
  7.2 63.0 %all-gather.11.cloned.1.call-start = ((), (), s32[]{:S(2)}) async-start(), calls=%async_computation.9 | async-start | bytes 2162688 | tf_op jit(solution)/shard_map/all_gather | solution.py:85
  7.9 120.4 %all-gather.13.cloned.1.call-start = ((), (), s32[]{:S(2)}) async-start(), calls=%async_computation.10 | async-start | bytes 2162688 | tf_op jit(solution)/shard_map/all_gather | solution.py:84
  8.7 183.2 %all-gather.17.cloned.1.call-start = ((), (), s32[]{:S(2)}) async-start(), calls=%async_computation.12 | async-start | bytes 4325376 | tf_op jit(solution)/shard_map/all_gather | solution.py:83
  9.4 220.2 %all-gather.27.cloned.1.call-start = ((), (), s32[]{:S(2)}) async-start(), calls=%async_computation.26 | async-start | bytes 4718592 | tf_op jit(solution)/shard_map/all_gather | solution.py:129
  55.0 143.3 %copy-start.41 = (f32[1024]{0:T(1024)}, f32[1024]{0:T(1024)S(1)}, u32[]{:S(2)}) copy-start(f32[1024]{0:T(1024)S(1)} %convert_element_type.134) | copy-start | bytes 12292
  56.3 142.0 %copy-start.45 = (f32[256]{0:T(256)}, f32[256]{0:T(256)S(1)}, u32[]{:S(2)}) copy-start(f32[256]{0:T(256)S(1)} %add_rsqrt_fusion.3) | copy-start | bytes 3076
  73.5 195.7 %all-gather.15.cloned.1.call-start = ((), (), s32[]{:S(2)}) async-start(), calls=%async_computation.11 | async-start | bytes 4718592 | tf_op jit(solution)/shard_map/all_gather | solution.py:128
  74.1 128.7 %copy-start.22 = (f32[256,128]{0,1:T(8,128)}, f32[256,128]{0,1:T(8,128)S(1)}, u32[]{:S(2)}) copy-start(f32[256,128]{0,1:T(8,128)S(1)} %get-tuple-element.342) | copy-start | bytes 393220
  74.1 128.7 %copy-start.24 = (f32[256,128]{0,1:T(8,128)}, f32[256,128]{0,1:T(8,128)S(1)}, u32[]{:S(2)}) copy-start(f32[256,128]{0,1:T(8,128)S(1)} %get-tuple-element.343) | copy-start | bytes 393220
  136.2 197.6 %all-gather.19.cloned.1.call-start = ((), (), s32[]{:S(2)}) async-start(), calls=%async_computation.13 | async-start | bytes 4325376 | tf_op jit(solution)/shard_map/all_gather | solution.py:88
  136.7 268.0 %all-gather.21.cloned.1.call-start = ((), (), s32[]{:S(2)}) async-start(), calls=%async_computation.14 | async-start | bytes 6488064 | tf_op jit(solution)/shard_map/all_gather | solution.py:92
  137.5 337.9 %all-gather.23.cloned.1.call-start = ((), (), s32[]{:S(2)}) async-start(), calls=%async_computation.15 | async-start | bytes 6488064 | tf_op jit(solution)/shard_map/all_gather | solution.py:93
  138.2 407.9 %all-gather.25.cloned.1.call-start = ((), (), s32[]{:S(2)}) async-start(), calls=%async_computation.16 | async-start | bytes 6488064 | tf_op jit(solution)/shard_map/all_gather | solution.py:94
  139.0 577.0 %reduce-scatter.10.cloned.1.call-start = ((), (), s32[]{:S(2)}) async-start(), calls=%async_computation.17 | async-start | bytes 4718592 | tf_op jit(solution)/shard_map/reduce_scatter | solution.py:267
  338.8 136.7 %copy-start.20 = (bf16[256,1024]{1,0:T(8,128)(2,1)}, bf16[256,1024]{1,0:T(8,128)(2,1)S(1)}, u32[]{:S(2)}) copy-start(bf16[256,1024]{1,0:T(8,128)(2,1)S(1)} %multiply_convert_fusion.5) | copy-start | bytes 1572868
  410.9 135.2 %copy-start.33 = (bf16[1,256,1024]{2,1,0:T(8,128)(2,1)S(1)}, bf16[1,256,1024]{2,1,0:T(8,128)(2,1)}, u32[]{:S(2)}) copy-start(bf16[1,256,1024]{2,1,0:T(8,128)(2,1)} %param.19) | copy-start | bytes 1572868
  666.3 104.2 %reduce-scatter.12.cloned.1.call-start = ((), (), s32[]{:S(2)}) async-start(), calls=%async_computation.18 | async-start | bytes 4718592 | tf_op jit(solution)/shard_map/reduce_scatter | solution.py:270
  667.0 256.0 %reduce-scatter.16.cloned.1.call-start = ((), (), s32[]{:S(2)}) async-start(), calls=%async_computation.20 | async-start | bytes 4325376 | tf_op jit(solution)/shard_map/reduce_scatter | solution.py:304
  723.4 350.4 %reduce-scatter.18.cloned.1.call-start = ((), (), s32[]{:S(2)}) async-start(), calls=%async_computation.21 | async-start | bytes 4325376 | tf_op jit(solution)/shard_map/reduce_scatter | solution.py:305
  774.4 486.7 %reduce-scatter.14.cloned.1.call-start = ((), (), s32[]{:S(2)}) async-start(), calls=%async_computation.19 | async-start | bytes 8650752 | tf_op jit(solution)/shard_map/reduce_scatter | solution.py:303
  783.8 663.4 %reduce-scatter.20.cloned.1.call-start = ((), (), s32[]{:S(2)}) async-start(), calls=%async_computation.22 | async-start | bytes 8650752 | tf_op jit(solution)/shard_map/reduce_scatter | solution.py:308
  790.0 816.3 %reduce-scatter.22.cloned.1.call-start = ((), (), s32[]{:S(2)}) async-start(), calls=%async_computation.23 | async-start | bytes 12976128 | tf_op jit(solution)/shard_map/reduce_scatter | solution.py:216
  798.8 967.7 %reduce-scatter.24.cloned.1.call-start = ((), (), s32[]{:S(2)}) async-start(), calls=%async_computation.24 | async-start | bytes 12976128 | tf_op jit(solution)/shard_map/reduce_scatter | solution.py:217
  806.7 1120.1 %reduce-scatter.26.cloned.1.call-start = ((), (), s32[]{:S(2)}) async-start(), calls=%async_computation.25 | async-start | bytes 12976128 | tf_op jit(solution)/shard_map/reduce_scatter | solution.py:218
  (70 other events, 672.8 us)
Sparse Core Ops, SparseCore 0:
  10.9 59.1 all-gather.10
  73.1 55.1 all-gather.12
  131.3 60.4 all-gather.16
  194.2 35.3 all-gather.26
  231.9 37.3 all-gather.14
  272.1 61.6 all-gather.18
  336.7 68.0 all-gather.20
  407.6 67.7 all-gather.22
  478.3 67.7 all-gather.24
  666.4 49.5 reduce-scatter.9
  719.3 51.0 reduce-scatter.11
  773.1 149.7 reduce-scatter.15
  925.8 147.9 reduce-scatter.17
  1076.5 184.4 reduce-scatter.13
  1263.8 183.4 reduce-scatter.19
  1453.7 152.5 reduce-scatter.21
  1612.7 153.7 reduce-scatter.23
  1773.0 153.7 reduce-scatter.25
where the time goes:
time: 1940 us; the launch traced here: 1930 us
  waiting for transfers between devices  1530 us (79%)
  matrix products  197 us (10%)
  local copies, waits for them, and re-layouts  85.6 us (4%)
  blocking collectives  82.6 us (4%)
    reduce_scatter x1, waiting for transfers between devices, on_device(): lax.psum_scatter(grad_wquery, ('ctx', 'fsdp'), scatter_dimension=0, tiled...  187 us
    reduce_scatter x1, waiting for transfers between devices, on_device(): lax.psum_scatter(grad_woutput, ('ctx', 'fsdp'), scatter_dimension=0, tile...  186 us
    reduce_scatter x1, waiting for transfers between devices, on_device(): lax.psum_scatter(grad_down, ('ctx', 'fsdp'), scatter_dimension=0, tiled=T...  160 us
    reduce_scatter x1, waiting for transfers between devices, on_device(): lax.psum_scatter(grad_wup, ('ctx', 'fsdp'), scatter_dimension=0, tiled=True)  160 us
    reduce_scatter x1, waiting for transfers between devices, on_device(): lax.psum_scatter(gate_matrix_gradient, ('ctx', 'fsdp'), scatter_dimension...  159 us
    reduce_scatter x1, waiting for transfers between devices, on_device(): lax.psum_scatter(grad_wvalue, ('ctx', 'fsdp'), scatter_dimension=0, tiled...  151 us
    unnamed x2, blocking collectives  82.6 us
    all_gather x1, waiting for transfers between devices, on_device(): lax.all_gather(gate_weight, ('ctx', 'fsdp'), axis=0, tiled=True)  65.9 us
  transfers between devices with their start and end apart: 18, of which 18 were waited for; matrix products, arithmetic and copies ran while one was open for 9% of the time, Pallas kernels for 0%

commit v1 on v0

v1 whole, which is shorter than its diff:
```python
import functools
import math

import jax
import jax.numpy as jnp
from jax import lax
from jax.experimental import pallas as pl
from jax.experimental.pallas import tpu as pltpu
from jax.sharding import PartitionSpec as P

MESH = pl.DeviceIdType.MESH
ANY = pl.BlockSpec(memory_space=pl.ANY)


H = 16
KVH = 8
HD = 128
BLK = 128


EPSILON = 1e-06
ROPE_BASE = 1000000.0


def rope_tables(positions):
    half = HD // 2
    freqs = jnp.exp(jnp.arange(half, dtype=jnp.float32) * (-2.0 * math.log(ROPE_BASE) / HD))
    angles = positions.astype(jnp.float32)[..., None] * freqs
    cosine = jnp.cos(angles)
    sine = jnp.sin(angles)
    return (jnp.concatenate([cosine, cosine], axis=-1), jnp.concatenate([sine, sine], axis=-1))


def rotate(value_vectors):
    half = value_vectors.shape[-1] // 2
    return jnp.concatenate([-value_vectors[..., half:], value_vectors[..., :half]], axis=-1)


def unrotate(value_vectors):
    half = value_vectors.shape[-1] // 2
    return jnp.concatenate([value_vectors[..., half:], -value_vectors[..., :half]], axis=-1)


def left_dot(left, right):
    return lax.dot_general(
        left, right, (((0,), (0,)), ((), ())), preferred_element_type=jnp.float32
    )


def right_dot(left, right):
    return lax.dot_general(
        left, right, (((1,), (1,)), ((), ())), preferred_element_type=jnp.float32
    )


def plain_dot(left, right):
    return jnp.dot(left, right, preferred_element_type=jnp.float32)


def norm_back(grad_normed, unit, inverse, gain):
    scaled = grad_normed * gain
    return inverse * (scaled - unit * jnp.mean(scaled * unit, axis=-1, keepdims=True))


class Grid:
    def __init__(self, ctx, fsdp):
        self.sizes = {"a": ctx // 4, "b": 2, "core": 2, "f": fsdp}
        self.stride = {"a": 4, "b": 2, "core": 1}

    def enter(self):
        self.c = lax.axis_index("ctx")
        self.at = {
            "a": self.c // 4,
            "b": (self.c // 2) % 2,
            "core": self.c % 2,
            "f": lax.axis_index("fsdp"),
        }

    def peer(self, axis, place):
        if axis == "f":
            return {"fsdp": place}
        return {"ctx": self.c + (place - self.at[axis]) * self.stride[axis]}

    def sources(self, axis):
        n, p = self.sizes[axis], self.at[axis]
        if n == 2:
            return [(None, 1 - p, None, None)]
        found = []
        for step in range(1, n):
            for way in (1, -1):
                origin = p - way * step
                onward = p + way
                found.append(
                    (
                        jnp.logical_and(origin >= 0, origin < n),
                        origin,
                        onward,
                        jnp.logical_and(
                            jnp.logical_and(origin >= 0, origin < n),
                            jnp.logical_and(onward >= 0, onward < n),
                        ),
                    )
                )
        return found

    def around(self, axis):
        n, p = self.sizes[axis], self.at[axis]
        if n == 2:
            return [(None, 1 - p)]
        return [(p + 1 < n, p + 1), (p >= 1, p - 1)]

    def nearest(self, axis):
        n, p = self.sizes[axis], self.at[axis]
        if n == 2:
            return [p, 1 - p]
        order = [0]
        for step in range(1, n):
            for way in (step, n - step):
                if way not in order:
                    order.append(way)
        return [lax.rem(p + s, n) for s in order]


class Pool:
    def __init__(self, ref):
        self.ref, self.used = ref, 0

    def take(self, count):
        first = self.used
        self.used += count
        return self.ref.at[pl.ds(first, count)]


def guarded(cond, body):
    if cond is None:
        body()
    else:
        pl.when(cond)(body)


class Gather:
    def __init__(self, grid, order, src, dst, columns, send_sem, recv_sem, layout_axes):
        self.grid, self.order, self.src, self.dst = grid, order, src, dst
        self.columns, self.send_sem, self.recv_sem = columns, send_sem, recv_sem
        self.layout_axes = layout_axes
        self.sends = 0
        self.pending = []

    @staticmethod
    def semaphores(grid, order):
        near = {x: 1 if grid.sizes[x] == 2 else 2 for x in order}
        far = {x: 0 if grid.sizes[x] == 2 else 2 * (grid.sizes[x] - 1) for x in order}
        sends = near[order[0]] + far[order[0]] + sum(near[x] for x in order[1:])
        inner = 1
        for level in range(1, len(order)):
            axis = order[level]
            onward = sum(near[x] for x in order[level + 1 :])
            sends += inner * (far[axis] + max(far[axis], 1) * onward)
            inner *= grid.sizes[axis]
        return sends, grid.sizes[order[0]] + inner

    def view(self, places):
        idx = tuple(places.get(x, slice(None)) for x in self.layout_axes)
        return self.dst.at[idx + (slice(None), self.columns)]

    def unit_number(self, places):
        number = 0
        for x in self.order[1:]:
            number = number * self.grid.sizes[x] + places[x]
        return number

    def start(self, cond, view, axis, place, sem):
        slot = self.sends
        self.sends += 1

        def make():
            return pltpu.make_async_remote_copy(
                src_ref=view[0],
                dst_ref=view[1],
                send_sem=self.send_sem.at[slot],
                recv_sem=self.recv_sem.at[sem],
                device_id=self.grid.peer(axis, place),
                device_id_type=MESH,
            )

        guarded(cond, lambda: make().start())
        self.pending.append((cond, make))

    def wait_recv(self, view, sem):
        pltpu.make_async_remote_copy(
            src_ref=view,
            dst_ref=view,
            send_sem=self.send_sem.at[0],
            recv_sem=self.recv_sem.at[sem],
            device_id={},
            device_id_type=MESH,
        ).wait_recv()

    def own_places(self):
        return {x: self.grid.at[x] for x in self.order}

    def open(self):
        axis = self.order[0]
        own = self.view(self.own_places())
        src = self.src.at[:, self.columns]
        for cond, place in self.grid.around(axis):
            self.start(cond, (src, own), axis, place, self.grid.at[axis])

    def first(self):
        axis = self.order[0]
        for cond, origin, onward, more in self.grid.sources(axis):
            view = self.view({**self.own_places(), axis: origin})
            guarded(cond, lambda: self.wait_recv(view, origin))
            if onward is not None:
                self.start(more, (view, view), axis, onward, origin)
        self.pass_on(None, 1, {x: self.grid.at[x] for x in self.order[1:]})

    def pass_on(self, cond, level, places):
        n1 = self.grid.sizes[self.order[0]]
        sem = n1 + self.unit_number(places)
        view = self.view(places)
        for axis in self.order[level:]:
            for near, place in self.grid.around(axis):
                both = near if cond is None else cond if near is None else jnp.logical_and(cond, near)
                self.start(both, (view, view), axis, place, sem)

    def arrivals(self, level):
        n1 = self.grid.sizes[self.order[0]]
        axis = self.order[level]
        inner = [{}]
        for x in self.order[1:level]:
            inner = [{**places, x: j} for places in inner for j in self.grid.nearest(x)]
        fixed = {x: self.grid.at[x] for x in self.order[level + 1 :]}
        for places in inner:
            for cond, origin, onward, more in self.grid.sources(axis):
                unit = {**places, **fixed, axis: origin}
                view = self.view(unit)
                sem = n1 + self.unit_number(unit)
                guarded(cond, lambda: self.wait_recv(view, sem))
                if onward is not None:
                    self.start(more, (view, view), axis, onward, sem)
                self.pass_on(cond, level + 1, unit)

    def close(self):
        for cond, make in self.pending:
            guarded(cond, lambda: make().wait_send())


def add_into(total, term, out=None):
    shape = total.shape
    rows = min(16, shape[-2])
    steps = shape[-2] // rows
    lead = math.prod(shape[:-2])

    def body(i, carry):
        index = ()
        rest = i // steps
        for n in reversed(shape[:-2]):
            index = (lax.rem(rest, n),) + index
            rest = rest // n
        at = index + (pl.ds(pl.multiple_of(lax.rem(i, steps) * rows, rows), rows), slice(None))
        value = total[at].astype(jnp.float32)
        if term is not None:
            value = value + term[at].astype(jnp.float32)
        if out is None:
            total[at] = value.astype(total.dtype)
        else:
            out[at] = value.astype(out.dtype)
        return carry

    lax.fori_loop(0, lead * steps, body, 0)


class Scatter:
    def __init__(self, grid, order, src, columns, own, recvs, load_sem, send_sem, recv_sem, out, layout_axes):
        self.grid, self.order, self.src, self.columns = grid, order, src, columns
        self.own, self.recvs, self.out = own, recvs, out
        self.load_sem, self.send_sem, self.recv_sem = load_sem, send_sem, recv_sem
        self.layout_axes = layout_axes
        self.sends = 0
        self.pending = []
        self.base = {}
        number = 0
        for level in range(len(order) - 1, -1, -1):
            self.base[level] = number
            number += self.slots(grid, order, level)

    @staticmethod
    def inner(grid, order, level):
        return [grid.sizes[x] for x in order[1:level]]

    @staticmethod
    def slots(grid, order, level):
        n = grid.sizes[order[level]]
        lines = 1 if n == 2 else 2 * n
        return lines * math.prod(Scatter.inner(grid, order, level))

    @staticmethod
    def scratch(grid, order, rows, columns, dtype):
        n1 = grid.sizes[order[0]]
        own = tuple(grid.sizes[x] for x in order[1:-1]) + (n1, rows, columns)
        recvs = []
        for level in range(len(order)):
            n = grid.sizes[order[level]]
            lead = () if n == 2 else (2, n)
            block = (rows, columns) if level == 0 else (n1, rows, columns)
            recvs.append(lead + tuple(Scatter.inner(grid, order, level)) + block)
        return [pltpu.VMEM(s, dtype) for s in [own] + recvs]

    @staticmethod
    def semaphores(grid, order):
        loads = math.prod(grid.sizes[x] for x in order[1:-1])
        slots = [Scatter.slots(grid, order, level) for level in range(len(order))]
        sends = [
            (1 if grid.sizes[x] == 2 else 2 * (grid.sizes[x] - 1))
            * math.prod(Scatter.inner(grid, order, level))
            for level, x in enumerate(order)
        ]
        return loads, sum(sends), sum(slots)

    def hbm(self, places):
        idx = tuple(places.get(x, slice(None)) for x in self.layout_axes)
        return self.src.at[idx + (slice(None), self.columns)]

    def units(self, level, first=None):
        found = [{}]
        for x in self.order[1:level]:
            found = [{**places, x: j} for places in found for j in reversed(self.grid.nearest(x))]
        return found

    def mine(self, places):
        idx = tuple(places.get(x, self.grid.at[x]) for x in self.order[1:-1])
        return self.own.at[idx]

    def number(self, places, axes):
        value = 0
        for x in axes:
            value = value * self.grid.sizes[x] + places[x]
        return value

    def slot(self, level, places, way=None, target=None):
        axes = self.order[1:level]
        idx = tuple(places[x] for x in axes)
        inner = math.prod(self.grid.sizes[x] for x in axes)
        number = self.number(places, axes)
        if way is not None:
            idx = (way, target) + idx
            number = (way * self.grid.sizes[self.order[level]] + target) * inner + number
        ref = self.recvs[level]
        return (ref.at[idx] if idx else ref), self.recv_sem.at[self.base[level] + number]

    def send(self, cond, view, landing, axis, place):
        slot = self.sends
        self.sends += 1
        ref, sem = landing

        def make():
            return pltpu.make_async_remote_copy(
                src_ref=view,
                dst_ref=ref,
                send_sem=self.send_sem.at[slot],
                recv_sem=sem,
                device_id=self.grid.peer(axis, place),
                device_id_type=MESH,
            )

        guarded(cond, lambda: make().start())
        self.pending.append((cond, make))

    def take(self, cond, landing, total, out=None):
        ref, sem = landing

        def body():
            pltpu.make_async_remote_copy(
                src_ref=ref,
                dst_ref=ref,
                send_sem=self.send_sem.at[0],
                recv_sem=sem,
                device_id={},
                device_id_type=MESH,
            ).wait_recv()
            add_into(total, ref, out)

        guarded(cond, body)

    def load(self, places):
        axes = self.order[1:-1]
        here = {**places, self.order[-1]: self.grid.at[self.order[-1]]}
        return pltpu.make_async_copy(
            self.hbm(here), self.mine(places), self.load_sem.at[self.number(places, axes)]
        )

    def open(self):
        top = len(self.order) - 1
        axis = self.order[top]
        there = 1 - self.grid.at[axis]
        for places in self.units(top):
            self.send(None, self.hbm({**places, axis: there}), self.slot(top, places), axis, there)
            self.load(places).start()

    def settle(self, level, places):
        above = level + 1
        top = len(self.order) - 1
        total = self.mine(places)
        if above == top:
            self.load(places).wait()
            self.take(None, self.slot(above, places), total)
            return
        axis = self.order[above]
        n, p = self.grid.sizes[axis], self.grid.at[axis]
        if n == 2:
            self.take(None, self.slot(above, places), total)
        else:
            self.take(p >= 1, self.slot(above, places, 0, p), total)
            self.take(p + 1 < n, self.slot(above, places, 1, p), total)

    def step(self, level):
        axis = self.order[level]
        n, p = self.grid.sizes[axis], self.grid.at[axis]
        if level == 0:
            self.settle(0, {})
            whole = self.mine({})
            self.along(level, {}, lambda t: whole.at[t])
            return
        for places in self.units(level):
            self.along(level, places, lambda t: self.mine({**places, axis: t}))
            self.settle(level, {**places, axis: p})

    def along(self, level, places, view):
        axis = self.order[level]
        n, p = self.grid.sizes[axis], self.grid.at[axis]
        if n == 2:
            if level:
                self.settle(level, {**places, axis: 1 - p})
            self.send(None, view(1 - p), self.slot(level, places), axis, 1 - p)
            return
        for s in range(n - 1):
            for way, t in ((0, n - 1 - s), (1, s)):
                wanted = (t > p) if way == 0 else (t < p)
                behind = (p >= 1) if way == 0 else (p + 1 < n)
                if level:
                    pl.when(wanted)(lambda: self.settle(level, {**places, axis: t}))
                self.take(jnp.logical_and(wanted, behind), self.slot(level, places, way, t), view(t))
                self.send(wanted, view(t), self.slot(level, places, way, t), axis, p + (1 if way == 0 else -1))

    def finish(self):
        axis = self.order[0]
        n, p = self.grid.sizes[axis], self.grid.at[axis]
        total = self.mine({}).at[p]
        if n == 2:
            self.take(None, self.slot(0, {}), total, self.out)
            return
        self.take(p >= 1, self.slot(0, {}, 0, p), total)
        self.take(p + 1 < n, self.slot(0, {}, 1, p), total)
        add_into(total, None, self.out)

    def close(self):
        for cond, make in self.pending:
            guarded(cond, lambda: make().wait_send())


def half_pairs(ref, s):
    rows = pl.ds(s * BLK, BLK)
    return jnp.concatenate([ref[rows, :HD], ref[rows, HD:]], axis=0)


def items(table, pairs):
    high_slot, high = table[pairs * 2], table[pairs * 2 + 1]
    low_block = 2 * pairs - 1 - high
    split = high // 2
    found = []
    for w in range(pairs - 1):
        upper = w < split
        found.append((jnp.where(upper, high_slot, 1 - high_slot), jnp.where(upper, w, w - split), None))
    found.append((high_slot, split, high))
    found.append((1 - high_slot, low_block // 2, low_block))
    return found


def chunk_of(ref, table, c):
    return jnp.concatenate(
        [ref[pl.ds(pl.multiple_of(table[2 * c + i] * BLK, BLK), BLK), :] for i in range(2)], axis=0
    )


def row_contract(left, right):
    return lax.dot_general(left, right, (((1,), (1,)), ((), ())), preferred_element_type=jnp.float32)


def attention_kernel(pairs, table, q_ref, k_ref, v_ref, o_ref, low_ref, t_ref, qs, acc, tot):
    for s in range(2):
        qs[s] = half_pairs(q_ref, s)
    acc[...] = jnp.zeros_like(acc)
    tot[...] = jnp.zeros_like(tot)
    for s, c, block in items(table, pairs):
        keys = chunk_of(k_ref, table, c)
        vals = chunk_of(v_ref, table, c)
        scores = row_contract(qs[s], keys) * (HD ** (-0.5) * math.log2(math.e))
        weights = jnp.exp2(scores)
        if block is not None:
            rows = lax.broadcasted_iota(jnp.int32, (2 * BLK, 2 * BLK), 0)
            cols = lax.broadcasted_iota(jnp.int32, (2 * BLK, 2 * BLK), 1)
            allowed = cols <= lax.rem(rows, BLK) + (block - 2 * c) * BLK
            weights = jnp.where(allowed, weights, 0.0)
        tot[s] += weights[:, :HD] + weights[:, HD:]
        acc[s] += jnp.dot(weights.astype(jnp.bfloat16), vals, preferred_element_type=jnp.float32)
    for s in range(2):
        total = tot[s]
        value = acc[s] / jnp.sum(total, axis=1, keepdims=True)
        rows = pl.ds(s * BLK, BLK)
        for i in range(2):
            part = value[i * BLK : (i + 1) * BLK]
            o_ref[rows, i * HD : (i + 1) * HD] = part
            low_ref[rows, i * HD : (i + 1) * HD] = part.astype(jnp.bfloat16)
        t_ref[0, s : s + 1, :] = jnp.sum(total.T, axis=0, keepdims=True)


def attention(table, pairs, queries, keys, values):
    rows, length = queries.shape[0], keys.shape[0]
    head = pl.BlockSpec((rows, 2 * HD), lambda h, t: (0, h))
    side = pl.BlockSpec((length, HD), lambda h, t: (0, h))
    stats = pl.BlockSpec((1, 2, 2 * BLK), lambda h, t: (h, 0, 0))
    return pl.pallas_call(
        functools.partial(attention_kernel, pairs),
        grid_spec=pltpu.PrefetchScalarGridSpec(
            num_scalar_prefetch=1,
            grid=(KVH,),
            in_specs=[head, side, side],
            out_specs=[head, head, stats],
            scratch_shapes=[
                pltpu.VMEM((2, 2 * BLK, HD), jnp.bfloat16),
                pltpu.VMEM((2, 2 * BLK, HD), jnp.float32),
                pltpu.VMEM((2, 2 * BLK, HD), jnp.float32),
            ],
        ),
        out_shape=[
            jax.ShapeDtypeStruct((rows, H * HD), jnp.float32),
            jax.ShapeDtypeStruct((rows, H * HD), jnp.bfloat16),
            jax.ShapeDtypeStruct((KVH, 2, 2 * BLK), jnp.float32),
        ],
        name="attention",
    )(table, queries, keys, values)


def attention_back_kernel(
    pairs, table, q_ref, k_ref, v_ref, g_ref, d_ref, dq_ref, dk_ref, dv_ref, qs, gs, dq, dk, dv
):
    scale = HD ** (-0.5)
    for s in range(2):
        qs[s] = half_pairs(q_ref, s)
        gs[s] = half_pairs(g_ref, s)
    for total in (dq, dk, dv):
        total[...] = jnp.zeros_like(total)
    for s, c, block in items(table, pairs):
        keys = chunk_of(k_ref, table, c)
        vals = chunk_of(v_ref, table, c)
        queries, grads = qs[s], gs[s]
        weights = jnp.exp2(row_contract(keys, queries) * (scale * math.log2(math.e)))
        if block is not None:
            rows = lax.broadcasted_iota(jnp.int32, (2 * BLK, 2 * BLK), 0)
            cols = lax.broadcasted_iota(jnp.int32, (2 * BLK, 2 * BLK), 1)
            allowed = rows <= lax.rem(cols, BLK) + (block - 2 * c) * BLK
            weights = jnp.where(allowed, weights, 0.0)
        through = row_contract(vals, grads)
        scores = (weights * (through - d_ref[0, pl.ds(s, 1), :])).astype(jnp.bfloat16)
        to_values = jnp.dot(weights.astype(jnp.bfloat16), grads, preferred_element_type=jnp.float32)
        to_keys = jnp.dot(scores, queries, preferred_element_type=jnp.float32)
        for i in range(2):
            at = pl.ds(pl.multiple_of(table[2 * c + i] * BLK, BLK), BLK)
            dv[at, :] += to_values[i * BLK : (i + 1) * BLK]
            dk[at, :] += to_keys[i * BLK : (i + 1) * BLK]
        dq[s] += left_dot(scores, keys)
    dk_ref[...] = (dk[...] * scale).astype(jnp.bfloat16)
    dv_ref[...] = dv[...].astype(jnp.bfloat16)
    for s in range(2):
        for i in range(2):
            dq_ref[pl.ds(s * BLK, BLK), i * HD : (i + 1) * HD] = dq[s, i * BLK : (i + 1) * BLK] * scale


def attention_back(table, pairs, queries, keys, values, grads, drift):
    rows, length = queries.shape[0], keys.shape[0]
    head = pl.BlockSpec((rows, 2 * HD), lambda h, t: (0, h))
    side = pl.BlockSpec((length, HD), lambda h, t: (0, h))
    stats = pl.BlockSpec((1, 2, 2 * BLK), lambda h, t: (h, 0, 0))
    return pl.pallas_call(
        functools.partial(attention_back_kernel, pairs),
        grid_spec=pltpu.PrefetchScalarGridSpec(
            num_scalar_prefetch=1,
            grid=(KVH,),
            in_specs=[head, side, side, head, stats],
            out_specs=[head, side, side],
            scratch_shapes=[
                pltpu.VMEM((2, 2 * BLK, HD), jnp.bfloat16),
                pltpu.VMEM((2, 2 * BLK, HD), jnp.bfloat16),
                pltpu.VMEM((2, 2 * BLK, HD), jnp.float32),
                pltpu.VMEM((length, HD), jnp.float32),
                pltpu.VMEM((length, HD), jnp.float32),
            ],
        ),
        out_shape=[
            jax.ShapeDtypeStruct((rows, H * HD), jnp.float32),
            jax.ShapeDtypeStruct((length, KVH * HD), jnp.bfloat16),
            jax.ShapeDtypeStruct((length, KVH * HD), jnp.bfloat16),
        ],
        name="attention_back",
    )(table, queries, keys, values, grads, drift)


ALL_AXES = ("a", "b", "core", "f")
SLOT_AXES = ("a", "b", "core")
BFA, AFB = ("b", "f", "a", "core"), ("a", "f", "b", "core")
FAB, FBA = ("f", "a", "b", "core"), ("f", "b", "a", "core")
AB, BA = ("a", "b", "core"), ("b", "a", "core")


def gather_kernel(grid, portions, layout, n, *refs):
    srcs, dsts, held = refs[:n], refs[n : 2 * n], refs[2 * n : 3 * n]
    send, recv, local = refs[3 * n :]
    grid.enter()
    send, recv = Pool(send), Pool(recv)
    mine = tuple(grid.at[x] for x in layout)
    for i in range(n):
        pltpu.make_async_copy(srcs[i], held[i], local.at[i]).start()
    parts = []
    for i, low, high, order in portions:
        sends, takes = Gather.semaphores(grid, order)
        columns = pl.ds(low, high - low)
        parts.append(
            Gather(grid, order, srcs[i], dsts[i], columns, send.take(sends), recv.take(takes), layout)
        )
        parts[-1].open()
    for i in range(n):
        pltpu.make_async_copy(srcs[i], held[i], local.at[i]).wait()
        pltpu.make_async_copy(held[i], dsts[i].at[mine], local.at[i]).start()
    for i in range(n):
        pltpu.make_async_copy(held[i], dsts[i].at[mine], local.at[i]).wait()
    for part in parts:
        part.first()
    for level in range(1, len(layout)):
        for part in parts:
            part.arrivals(level)
    for part in parts:
        part.close()


def gather(grid, layout, portions, name, *blocks):
    n = len(blocks)
    sends, takes = [sum(x) for x in zip(*[Gather.semaphores(grid, p[3]) for p in portions])]
    places = tuple(grid.sizes[x] for x in layout)
    total = math.prod(places)
    outs = pl.pallas_call(
        functools.partial(gather_kernel, grid, portions, layout, n),
        out_shape=[jax.ShapeDtypeStruct(places + x.shape, x.dtype) for x in blocks],
        in_specs=[ANY] * n,
        out_specs=[ANY] * n,
        scratch_shapes=[pltpu.VMEM(x.shape, x.dtype) for x in blocks]
        + [
            pltpu.SemaphoreType.DMA((sends,)),
            pltpu.SemaphoreType.DMA((takes,)),
            pltpu.SemaphoreType.DMA((n,)),
        ],
        compiler_params=pltpu.CompilerParams(has_side_effects=True),
        name=name,
    )(*blocks)
    return [x.reshape(total * x.shape[-2], x.shape[-1]) for x in outs]


def scatter_kernel(grid, portions, layout, n, *refs):
    srcs, outs, scratch = refs[:n], refs[n : 2 * n], list(refs[2 * n : -3])
    load, send, recv = [Pool(x) for x in refs[-3:]]
    grid.enter()
    parts = []
    for i, low, high, order in portions:
        loads, sends, takes = Scatter.semaphores(grid, order)
        own, *recvs = scratch[: 1 + len(order)]
        del scratch[: 1 + len(order)]
        parts.append(
            Scatter(
                grid,
                order,
                srcs[i],
                pl.ds(low, high - low),
                own,
                recvs,
                load.take(loads),
                send.take(sends),
                recv.take(takes),
                outs[i].at[:, low:high],
                layout,
            )
        )
        parts[-1].open()
    for level in range(len(layout) - 2, -1, -1):
        for part in parts:
            part.step(level)
    for part in parts:
        part.finish()
    for part in parts:
        part.close()


def scatter(grid, layout, portions, name, dtypes, *sums):
    n = len(sums)
    places = tuple(grid.sizes[x] for x in layout)
    total = math.prod(places)
    blocks = [x.reshape(places + (x.shape[0] // total, x.shape[1])) for x in sums]
    loads, sends, takes = [sum(x) for x in zip(*[Scatter.semaphores(grid, p[3]) for p in portions])]
    scratch = []
    for i, low, high, order in portions:
        scratch += Scatter.scratch(grid, order, blocks[i].shape[-2], high - low, blocks[i].dtype)
    return pl.pallas_call(
        functools.partial(scatter_kernel, grid, portions, layout, n),
        out_shape=[jax.ShapeDtypeStruct(x.shape[-2:], t) for x, t in zip(blocks, dtypes)],
        in_specs=[ANY] * n,
        out_specs=[pl.BlockSpec(memory_space=pltpu.VMEM)] * n,
        scratch_shapes=scratch
        + [
            pltpu.SemaphoreType.DMA((loads,)),
            pltpu.SemaphoreType.DMA((sends,)),
            pltpu.SemaphoreType.DMA((takes,)),
        ],
        compiler_params=pltpu.CompilerParams(has_side_effects=True, vmem_limit_bytes=60 * 2**20),
        name=name,
    )(*blocks)


def padded(x, rows):
    return jnp.pad(x, ((0, rows - x.shape[0]), (0, 128 - x.shape[1])))


def gain_rows(total, *gains):
    pieces = [x.reshape(total, 1, -1) for x in gains]
    pieces = [jnp.pad(x, ((0, 0), (0, 0), (0, 128 - x.shape[2]))) for x in pieces]
    block = jnp.concatenate(pieces, axis=1)
    return jnp.pad(block, ((0, 0), (0, 8 - len(gains)), (0, 0))).reshape(total * 8, 128)


def on_device(
    tokens,
    cotangent,
    block_map,
    attn_gain,
    query_weight,
    key_weight,
    value_weight,
    query_gain,
    key_gain,
    output_weight,
    mlp_gain,
    gate_weight,
    up_weight,
    down_weight,
):
    grid = Grid(lax.axis_size("ctx"), lax.axis_size("fsdp"))
    total = lax.axis_size("ctx") * lax.axis_size("fsdp")
    groups, rows, width = tokens.shape
    pairs = block_map.shape[1] // 2
    ratio = H // KVH
    low = jnp.bfloat16

    gains = jnp.concatenate(
        [padded(x.reshape(1, -1), 1) for x in (attn_gain, mlp_gain, query_gain, key_gain)], axis=0
    )
    hidden_width = gate_weight.shape[1]
    wqkv = jnp.concatenate([query_weight, key_weight, value_weight], axis=1)
    wgu = jnp.concatenate([gate_weight, up_weight], axis=1)
    half = wqkv.shape[1] // 2
    full_qkv, full_output, full_gu, full_down, all_gains = gather(
        grid,
        ALL_AXES,
        [
            (0, 0, half, BFA),
            (0, half, 2 * half, AFB),
            (1, 0, width // 2, FAB),
            (1, width // 2, width, FBA),
            (2, 0, hidden_width, BFA),
            (2, hidden_width, 2 * hidden_width, AFB),
            (3, 0, width // 2, FAB),
            (3, width // 2, width, FBA),
            (4, 0, 128, FAB),
        ],
        "gather_weights",
        wqkv,
        output_weight,
        wgu,
        down_weight,
        padded(gains, 16),
    )
    all_gains = all_gains.reshape(total, 16, 128)
    gain_one, gain_two, query_scale, key_scale = [
        all_gains[:, i, : x.shape[0]].reshape(-1).astype(jnp.float32)
        for i, x in enumerate((attn_gain, mlp_gain, query_gain, key_gain))
    ]

    place = lax.axis_index("ctx")
    blocks = block_map.reshape(-1)
    own_blocks = lax.dynamic_slice_in_dim(blocks, 2 * place, 2, 0)
    slots = jnp.argsort(blocks).astype(jnp.int32)
    high_slot = (own_blocks[1] > own_blocks[0]).astype(jnp.int32)
    table = jnp.concatenate([slots, high_slot[None], jnp.max(own_blocks)[None]]).astype(jnp.int32)

    spots = (own_blocks[:, None] * BLK + jnp.arange(BLK, dtype=jnp.int32)).reshape(rows)
    cosine, sine = rope_tables(spots)
    cosine = cosine.reshape(rows, 1, HD)
    sine = sine.reshape(rows, 1, HD)
    inputs = tokens.reshape(rows, width).astype(jnp.float32)
    inverse_one = lax.rsqrt(jnp.mean(inputs * inputs, axis=-1, keepdims=True) + EPSILON)
    normal_one = inputs * inverse_one
    normed = (normal_one * gain_one).astype(low)
    raw = plain_dot(normed, full_qkv)
    query_raw = raw[:, : H * HD].reshape(rows, H, HD)
    key_raw = raw[:, H * HD : (H + KVH) * HD].reshape(rows, KVH, HD)
    value_low = raw[:, (H + KVH) * HD :].astype(low)
    query_inverse = lax.rsqrt(jnp.mean(query_raw * query_raw, axis=-1, keepdims=True) + EPSILON)
    query_unit = query_raw * query_inverse
    query_normed = query_unit * query_scale
    query_low = (query_normed * cosine + rotate(query_normed) * sine).astype(low).reshape(rows, H * HD)
    key_inverse = lax.rsqrt(jnp.mean(key_raw * key_raw, axis=-1, keepdims=True) + EPSILON)
    key_unit = key_raw * key_inverse
    key_normed = key_unit * key_scale
    key_low = (key_normed * cosine + rotate(key_normed) * sine).astype(low).reshape(rows, KVH * HD)
    key_all, value_all = gather(
        grid,
        SLOT_AXES,
        [(0, 0, KVH * HD, AB), (1, 0, KVH * HD, BA)],
        "gather_keys",
        key_low,
        value_low,
    )
    attended, attended_low, totals = attention(table, pairs, query_low, key_all, value_all)
    row_totals = totals.reshape(KVH, 2, ratio, BLK).transpose(1, 3, 0, 2).reshape(rows, H, 1)
    middle = inputs + plain_dot(attended_low, full_output)
    inverse_two = lax.rsqrt(jnp.mean(middle * middle, axis=-1, keepdims=True) + EPSILON)
    normal_two = middle * inverse_two
    normed_two = (normal_two * gain_two).astype(low)
    both = plain_dot(normed_two, full_gu)
    gate, upper = both[:, :hidden_width], both[:, hidden_width:]
    sigmoid_gate = jax.nn.sigmoid(gate)
    activated = gate * sigmoid_gate
    hidden = (activated * upper).astype(low)
    output = (middle + plain_dot(hidden, full_down)).astype(low).reshape(groups, rows, width)

    upstream = cotangent.reshape(rows, width)
    grad_hidden = right_dot(upstream, full_down)
    grad_gate = (grad_hidden * upper * sigmoid_gate * (1.0 + gate * (1.0 - sigmoid_gate))).astype(low)
    grad_upper = (grad_hidden * activated).astype(low)
    grad_both = jnp.concatenate([grad_gate, grad_upper], axis=1)
    grad_down = left_dot(hidden, upstream).astype(low)
    grad_gu = left_dot(normed_two, grad_both).astype(low)
    grad_normed_two = right_dot(grad_both, full_gu)
    grad_gain_two = jnp.sum(grad_normed_two * normal_two, axis=0)
    grad_middle = upstream.astype(jnp.float32) + norm_back(grad_normed_two, normal_two, inverse_two, gain_two)
    f32 = jnp.float32
    out_gu, out_down, out_gain_two = scatter(
        grid,
        ALL_AXES,
        [
            (0, 0, hidden_width, BFA),
            (0, hidden_width, 2 * hidden_width, AFB),
            (1, 0, width // 2, FAB),
            (1, width // 2, width, FBA),
            (2, 0, 128, FAB),
        ],
        "scatter_mlp",
        (f32, f32, f32),
        grad_gu,
        grad_down,
        gain_rows(total, grad_gain_two),
    )
    branch_grad = grad_middle.astype(low)
    grad_woutput = left_dot(attended_low, branch_grad).astype(low)
    grad_attended = right_dot(branch_grad, full_output).reshape(rows, H, HD)
    grad_summed = (grad_attended / row_totals).astype(low).reshape(rows, H * HD)
    drift = jnp.sum(grad_attended * attended.reshape(rows, H, HD), axis=-1) / row_totals[..., 0]
    drift = drift.reshape(2, BLK, KVH, ratio).transpose(2, 0, 3, 1).reshape(KVH, 2, ratio * BLK)
    grad_query, grad_keys, grad_values = attention_back(
        table, pairs, query_low, key_all, value_all, grad_summed, drift
    )
    own_keys, own_values = scatter(
        grid,
        SLOT_AXES,
        [(0, 0, KVH * HD, AB), (1, 0, KVH * HD, BA)],
        "scatter_keys",
        (f32, low),
        grad_keys,
        grad_values,
    )
    grad_qrot = grad_query.reshape(rows, H, HD)
    grad_qnormed = grad_qrot * cosine + unrotate(grad_qrot) * sine
    grad_qscale = jnp.sum(grad_qnormed * query_unit, axis=(0, 1))
    grad_qraw = norm_back(grad_qnormed, query_unit, query_inverse, query_scale)
    grad_krot = own_keys.reshape(rows, KVH, HD)
    grad_knormed = grad_krot * cosine + unrotate(grad_krot) * sine
    grad_kscale = jnp.sum(grad_knormed * key_unit, axis=(0, 1))
    grad_kraw = norm_back(grad_knormed, key_unit, key_inverse, key_scale)
    grad_raw = jnp.concatenate(
        [
            grad_qraw.reshape(rows, H * HD).astype(low),
            grad_kraw.reshape(rows, KVH * HD).astype(low),
            own_values,
        ],
        axis=1,
    )
    grad_wqkv = left_dot(normed, grad_raw).astype(low)
    grad_normed = right_dot(grad_raw, full_qkv)
    grad_gain_one = jnp.sum(grad_normed * normal_one, axis=0)
    grad_inputs = grad_middle + norm_back(grad_normed, normal_one, inverse_one, gain_one)
    out_qkv, out_output, out_gains = scatter(
        grid,
        ALL_AXES,
        [
            (0, 0, half, BFA),
            (0, half, 2 * half, AFB),
            (1, 0, width // 2, FAB),
            (1, width // 2, width, FBA),
            (2, 0, 128, FAB),
        ],
        "scatter_attention",
        (f32, f32, f32),
        grad_wqkv,
        grad_woutput,
        gain_rows(total, grad_gain_one, grad_qscale, grad_kscale),
    )
    return (
        output,
        grad_inputs.astype(low).reshape(groups, rows, width),
        out_gains[0, : attn_gain.shape[0]],
        out_qkv[:, : H * HD],
        out_qkv[:, H * HD : (H + KVH) * HD],
        out_qkv[:, (H + KVH) * HD :],
        out_gains[1, : query_gain.shape[0]],
        out_gains[2, : key_gain.shape[0]],
        out_output,
        out_gain_two[0, : mlp_gain.shape[0]],
        out_gu[:, :hidden_width],
        out_gu[:, hidden_width:],
        out_down,
    )


def solution(mesh):
    return jax.shard_map(
        on_device,
        mesh=mesh,
        in_specs=(
            P("fsdp", "ctx", None),
            P("fsdp", "ctx", None),
            P("fsdp", None),
            P(("ctx", "fsdp")),
            P(("ctx", "fsdp"), None),
            P(("ctx", "fsdp"), None),
            P(("ctx", "fsdp"), None),
            P(("ctx", "fsdp")),
            P(("ctx", "fsdp")),
            P(("ctx", "fsdp"), None),
            P(("ctx", "fsdp")),
            P(("ctx", "fsdp"), None),
            P(("ctx", "fsdp"), None),
            P(("ctx", "fsdp"), None),
        ),
        out_specs=(
            P("fsdp", "ctx", None),
            P("fsdp", "ctx", None),
            P(("ctx", "fsdp")),
            P(("ctx", "fsdp"), None),
            P(("ctx", "fsdp"), None),
            P(("ctx", "fsdp"), None),
            P(("ctx", "fsdp")),
            P(("ctx", "fsdp")),
            P(("ctx", "fsdp"), None),
            P(("ctx", "fsdp")),
            P(("ctx", "fsdp"), None),
            P(("ctx", "fsdp"), None),
            P(("ctx", "fsdp"), None),
        ),
        check_vma=False,
    )
```

time: 1940 us -> 649 us (0.33)
  waiting for transfers between devices: 1530 us -> 0 us
  Pallas kernels: 0 us -> 498 us
  matrix products: 197 us -> 71 us
  blocking collectives: 82.6 us -> 0 us
  local copies, waits for them, and re-layouts: 85.6 us -> 34.3 us
    reduce_scatter x9 -> x0, waiting for transfers between devices: 1150 us -> none  [the longest x1 187 us: on_device(): lax.psum_scatter(grad_wquery, ('ctx', 'fsdp'), scatter_dimension=0, tiled...]
    pallas_call x0 -> x7, Pallas kernels: none -> 498 us  [the longest x3 267 us: scatter(): pl.pallas_call(functools.partial(scatter_kernel, grid, portions, layout,...]
    all_gather x9 -> x0, waiting for transfers between devices: 373 us -> none  [the longest x1 65.9 us: on_device(): lax.all_gather(gate_weight, ('ctx', 'fsdp'), axis=0, tiled=True)]
    dot_general x28 -> x0, matrix products: 101 us -> none  [the longest x8 31.6 us: block_inputs(): jnp.einsum('gqkrd,gtkd->gkrqt', query_grouped, keys_block, preferred_elem...]
    unnamed x2 -> x0, blocking collectives: 82.6 us -> none
    dynamic_slice x28 -> x0, local copies, waits for them, and re-layouts: 25.5 us -> none  [the longest x8 12.3 us: block_inputs(): lax.dynamic_slice_in_dim(key_source, start, key_rows, 1)]
    dot_general x7 -> x4, matrix products: 39.6 us -> 21.4 us  [left_dot(): lax.dot_general(left, right, (((0,), (0,)), ((), ())), preferred_element_...]
  transfers between devices with their start and end apart: 18 -> 0, of which waited for: 18 -> 0; matrix products, arithmetic and copies ran while one was open for 9% -> 0% of each run, Pallas kernels for 0% -> 0%
where the time goes in v1:
time: 649 us; the launch traced here: 642 us
  Pallas kernels  498 us (77%)
  matrix products  71 us (11%)
  other arithmetic  36.1 us (6%)
  local copies, waits for them, and re-layouts  34.3 us (5%)
    pallas_call x3, Pallas kernels, scatter(): pl.pallas_call(functools.partial(scatter_kernel, grid, portions, layout,...  267 us
    pallas_call x2, Pallas kernels, gather(): pl.pallas_call(functools.partial(gather_kernel, grid, portions, layout, n...  189 us
    dot_general x4, matrix products, right_dot(): lax.dot_general(left, right, (((1,), (1,)), ((), ())), preferred_element_...  28.8 us
    pallas_call x1, Pallas kernels, attention_back(): pl.pallas_call(functools.partial(attention_back_kernel, pairs), grid_spec...  28.4 us
    dot_general x4, matrix products, left_dot(): lax.dot_general(left, right, (((0,), (0,)), ((), ())), preferred_element_...  21.4 us
    dot_general x4, matrix products, plain_dot(): return jnp.dot(left, right, preferred_element_type=jnp.float32)  20.8 us

profile of v1, /device:TPU:0, one launch (start us, length us, event | category | flops | bytes accessed | tf_op | source)
XLA Modules:
  0.0 641.9 jit_solution(8506059737243474936)
XLA Ops:
  11.9 142.7 %gather_weights.1 = (bf16[2,2,2,4,32,4096]{5,4,3,2,1,0:T(8,128)(2,1)}, bf16[2,2,2,4,64,1024]{5,4,3,2,1,0:T(8,128)(2,1)}, bf16[2,2,2,4,32,6144]{5,4,3,2,1,0:T(8,1...) custom-call(bf16[32,4096]{1,0:T(8,128)(2,1)} %pad_maximum_fusion.7.refs_0_, ...), custom_call_target="tpu_custom_call" | custom-call | tf_op jit(solution)/shard_map/gather_weights/pallas_call | solution.py:651
  157.6 5.8 fusion.31
  168.6 3.0 fusion.4.q_ref
  175.2 3.0 fusion.28.refs_0_
  180.2 46.8 %gather_keys.1 = (bf16[2,2,2,256,1024]{4,3,2,1,0:T(8,128)(2,1)}, bf16[2,2,2,256,1024]{4,3,2,1,0:T(8,128)(2,1)}) custom-call(bf16[256,1024]{1,0:T(8,128)(2,1)} %fusion.28.refs_0_, bf16[256,1024]{1,0:T(8,128)(2,1)} %slice.171.refs_1_), custom_call_target="tpu_custom_call" | custom-call | tf_op jit(solution)/shard_map/gather_keys/pallas_call | solution.py:651
  227.0 12.8 %attention.1 = (f32[256,2048]{1,0:T(8,128)}, bf16[256,2048]{1,0:T(8,128)(2,1)}, f32[8,2,256]{2,1,0:T(2,128)}) custom-call(s32[18]{0:T(128)} %pad_add_fusion.table, bf16[256,2048]{1,0:T(8,128)(2,1)} %fusion.4.q_ref, bf16[2048,1024]{1,0:T(8,128)(2,1)} %bitcast.249, bf16[2048,1024]{1,0:T(8,128)(2,1)} %bitcast.251), custom_call_target="tpu_custom_call" | custom-call | tf_op jit(solution)/shard_map/attention/pallas_call | solution.py:523
  239.8 5.4 multiply_reduce_fusion.8
  246.7 6.9 %fusion.62 = f32[256,6144]{1,0:T(8,128)S(1)} fusion(bf16[1024,6144]{1,0:T(8,128)(2,1)} %bitcast.255, f32[256,1024]{1,0:T(8,128)} %get-tuple-element.99, f32[1024]{0:T(1024)S(1)} %reshape.343, f32[256]{0:T(256)S(1)} %add_rsqrt_fusion.2), kind=kOutput, calls=%fused_computation.157 | convolution fusion | flops 3222011904 | bytes 19928064 | tf_op jit(solution)/shard_map/dot_general | solution.py:57
  253.7 9.0 %multiply_convert_fusion.1 = (bf16[256,3072]{1,0:T(8,128)(2,1)S(1)}, bf16[256,3072]{1,0:T(8,128)(2,1)}, bf16[256,3072]{1,0:T(8,128)(2,1)S(1)}) fusion(f32[256,6144]{1,0:T(8,128)S(1)} %fusion.62, bf16[3072,1024]{1,0:T(8,128)(2,1)} %bitcast.286, bf16[1,256,1024]{2,1,0:T(8,128)(2,1)S(1)} %copy-done.20), kind=kOutput, calls=%fused_computation.7 | convolution fusion | flops 1622409216 | bytes 17825792 | tf_op jit(solution)/shard_map/dot_general | solution.py:51
  262.7 2.6 fusion.14
  265.3 7.7 %multiply_reduce_fusion.4 = (f32[1024]{0:T(1024)}, f32[256]{0:T(256)S(1)}, f32[256,1024]{1,0:T(8,128)S(1)}) fusion(f32[256,1024]{1,0:T(8,128)S(1)} %copy-done.6, f32[256]{0:T(256)S(1)} %add_rsqrt_fusion.2, f32[1024]{0:T(1024)S(1)} %reshape.343, bf16[1024,6144]{1,0:T(8,128)(2,1)} %bitcast.256, bf16[256,3072]{1,0:T(8,128)(2,1)} %get-tuple-element.72, ...), kind=kOutput, calls=%fused_computation.71 | convolution fusion | flops 3229088512 | bytes 17836032 | tf_op jit(solution)/shard_map/dot_general | solution.py:51
  274.3 2.9 copy.49
  277.9 6.1 multiply_reduce_fusion.2
  284.0 2.3 copy.48.g_ref
  289.0 28.4 %attention_back.1 = (f32[256,2048]{1,0:T(8,128)}, bf16[2048,1024]{1,0:T(8,128)(2,1)}, bf16[2048,1024]{1,0:T(8,128)(2,1)}) custom-call(s32[18]{0:T(128)} %pad_add_fusion.table, bf16[256,2048]{1,0:T(8,128)(2,1)} %fusion.4.q_ref, bf16[2048,1024]{1,0:T(8,128)(2,1)} %bitcast.250, bf16[2048,1024]{1,0:T(8,128)(2,1)} %bitcast.252, bf16[256,2048]{1,0:T(8,128)(2,1)} %copy.48.g_ref, ...), custom_call_target="tpu_custom_call" | custom-call | tf_op jit(solution)/shard_map/attention_back/pallas_call | solution.py:585
  317.4 50.9 %scatter_keys.1 = (f32[256,1024]{1,0:T(8,128)}, bf16[256,1024]{1,0:T(8,128)(2,1)}) custom-call(bf16[2,2,2,256,1024]{4,3,2,1,0:T(8,128)(2,1)} %bitcast.266, bf16[2,2,2,256,1024]{4,3,2,1,0:T(8,128)(2,1)} %bitcast.267), custom_call_target="tpu_custom_call" | custom-call | tf_op jit(solution)/shard_map/scatter_keys/pallas_call | solution.py:711
  380.0 4.5 multiply_reduce_fusion
  384.6 6.0 fusion.21
  391.7 5.7 convolution_convert_fusion.1
  397.4 3.3 convolution_convert_fusion.3
  401.7 95.2 %scatter_attention.1 = (f32[32,4096]{1,0:T(8,128)}, f32[64,1024]{1,0:T(8,128)}, f32[8,128]{1,0:T(8,128)}) custom-call(bf16[2,2,2,4,32,4096]{5,4,3,2,1,0:T(8,128)(2,1)} %bitcast.261, bf16[2,2,2,4,64,1024]{5,4,3,2,1,0:T(8,128)(2,1)} %bitcast.242, f32[2,2,2,4,8,128]{5,4,3,2,1,0:T(8,128)} %bitcast.274), custom_call_target="tpu_custom_call" | custom-call | tf_op jit(solution)/shard_map/scatter_attention/pallas_call | solution.py:711
  502.7 8.1 %convolution_convert_fusion = bf16[1024,6144]{1,0:T(8,128)(2,1)} fusion(bf16[256,3072]{1,0:T(8,128)(2,1)} %get-tuple-element.72, bf16[256,3072]{1,0:T(8,128)(2,1)S(1)} %copy-done.25, f32[256,1024]{1,0:T(8,128)S(1)} %copy-done.7, f32[1024]{0:T(1024)S(1)} %reshape.343, f32[256]{0:T(256)S(1)} %add_rsqrt_fusion.2), kind=kOutput, calls=%fused_computation | convolution fusion | flops 3234594816 | bytes 16782336 | tf_op jit(solution)/shard_map/dot_general | solution.py:45
  510.8 4.4 convolution_convert_fusion.2
  516.0 121.0 %scatter_mlp.1 = (f32[32,6144]{1,0:T(8,128)}, f32[96,1024]{1,0:T(8,128)}, f32[8,128]{1,0:T(8,128)}) custom-call(bf16[2,2,2,4,32,6144]{5,4,3,2,1,0:T(8,128)(2,1)} %bitcast.236, bf16[2,2,2,4,96,1024]{5,4,3,2,1,0:T(8,128)(2,1)} %bitcast.237, f32[2,2,2,4,8,128]{5,4,3,2,1,0:T(8,128)} %bitcast.273), custom_call_target="tpu_custom_call" | custom-call | tf_op jit(solution)/shard_map/scatter_mlp/pallas_call | solution.py:711
  (166 shorter events, 54.7 us)
Async XLA Ops:
  0.6 156.7 %copy-start.22 = (bf16[1,256,1024]{2,1,0:T(8,128)(2,1)S(1)}, bf16[1,256,1024]{2,1,0:T(8,128)(2,1)}, u32[]{:S(2)}) copy-start(bf16[1,256,1024]{2,1,0:T(8,128)(2,1)} %param.14) | copy-start | bytes 1572868
  155.7 12.3 %copy-start.32 = (f32[128]{0:T(128)}, f32[128]{0:T(128)S(1)}, u32[]{:S(2)}) copy-start(f32[128]{0:T(128)S(1)} %reshape.341) | copy-start | bytes 1540
  157.4 6.0 copy-start.30
  157.6 5.8 copy-start.36
  163.4 5.2 copy-start
  167.9 3.7 copy-start.2
  174.8 3.4 copy-start.9
  246.7 7.0 %copy-start.20 = (bf16[1,256,1024]{2,1,0:T(8,128)(2,1)S(1)}, bf16[1,256,1024]{2,1,0:T(8,128)(2,1)}, u32[]{:S(2)}) copy-start(bf16[1,256,1024]{2,1,0:T(8,128)(2,1)} %param.15) | copy-start | bytes 1572868
  246.7 16.0 %slice-start = ((s8[6291456]{0:T(1024)(128)(4,1)}), s8[4194304]{0:T(1024)(128)(4,1)S(1)}, s32[]{:S(2)}) async-start(s8[6291456]{0:T(1024)(128)(4,1)} %bitcast.287), calls=%async_computation | async-start | bytes 8388608
  253.6 9.0 %copy-start.6 = (f32[256,1024]{1,0:T(8,128)S(1)}, f32[256,1024]{1,0:T(8,128)}, u32[]{:S(2)}) copy-start(f32[256,1024]{1,0:T(8,128)} %get-tuple-element.99) | copy-start | bytes 3145732
  253.7 9.0 %slice-start.1 = ((s8[6291456]{0:T(1024)(128)(4,1)}), s8[2097152]{0:T(1024)(128)(4,1)S(1)}, s32[]{:S(2)}) async-start(s8[6291456]{0:T(1024)(128)(4,1)} %bitcast.287), calls=%async_computation.1 | async-start | bytes 4194304
  380.0 4.5 copy-start.23
  380.0 4.6 copy-start.31
  380.0 4.6 copy-start.37
  380.0 4.6 copy-start.39
  384.5 6.0 copy-start.8
  391.7 5.7 copy-start.17
  401.7 101.0 %copy-start.7 = (f32[256,1024]{1,0:T(8,128)S(1)}, f32[256,1024]{1,0:T(8,128)}, u32[]{:S(2)}) copy-start(f32[256,1024]{1,0:T(8,128)} %get-tuple-element.99) | copy-start | bytes 3145732
  401.7 101.0 %copy-start.25 = (bf16[256,3072]{1,0:T(8,128)(2,1)S(1)}, bf16[256,3072]{1,0:T(8,128)(2,1)}, u32[]{:S(2)}) copy-start(bf16[256,3072]{1,0:T(8,128)(2,1)} %copy-done.24) | copy-start | bytes 4718596
  502.7 8.1 %copy-start.16 = (bf16[256,3072]{1,0:T(8,128)(2,1)S(1)}, bf16[256,3072]{1,0:T(8,128)(2,1)}, u32[]{:S(2)}) copy-start(bf16[256,3072]{1,0:T(8,128)(2,1)} %copy-done.15) | copy-start | bytes 4718596
  502.7 8.1 %copy-start.21 = (bf16[1,256,1024]{2,1,0:T(8,128)(2,1)S(1)}, bf16[1,256,1024]{2,1,0:T(8,128)(2,1)}, u32[]{:S(2)}) copy-start(bf16[1,256,1024]{2,1,0:T(8,128)(2,1)} %param.15) | copy-start | bytes 1572868
  510.8 4.4 copy-start.38
  516.0 124.3 %copy-start.27 = (f32[64,1024]{1,0:T(8,128)S(1)}, f32[64,1024]{1,0:T(8,128)}, u32[]{:S(2)}) copy-start(f32[64,1024]{1,0:T(8,128)} %get-tuple-element.127) | copy-start | bytes 786436
  637.0 4.0 copy-start.26
  (18 other events, 38.9 us)

commit v2 on v1

--- a/solution.py
+++ b/solution.py
@@ -75,6 +75,18 @@
             "core": self.c % 2,
             "f": lax.axis_index("fsdp"),
         }
+
+    def barrier(self):
+        sem = pltpu.get_barrier_semaphore()
+        count = 0
+        for axis in ("core", "b", "a", "f"):
+            n, p = self.sizes[axis], self.at[axis]
+            for step in (1,) if n == 2 else (1, n - 1):
+                pl.semaphore_signal(
+                    sem, inc=1, device_id=self.peer(axis, lax.rem(p + step, n)), device_id_type=MESH
+                )
+                count += 1
+        pl.semaphore_wait(sem, count)
 
     def peer(self, axis, place):
         if axis == "f":
@@ -202,9 +214,8 @@
     def open(self):
         axis = self.order[0]
         own = self.view(self.own_places())
-        src = self.src.at[:, self.columns]
         for cond, place in self.grid.around(axis):
-            self.start(cond, (src, own), axis, place, self.grid.at[axis])
+            self.start(cond, (self.src, own), axis, place, self.grid.at[axis])
 
     def first(self):
         axis = self.order[0]
@@ -286,30 +297,34 @@
             number += self.slots(grid, order, level)
 
     @staticmethod
+    def kept(grid, order):
+        return order[1:-1] if grid.sizes[order[-1]] == 2 else order[1:]
+
+    @staticmethod
     def inner(grid, order, level):
         return [grid.sizes[x] for x in order[1:level]]
 
     @staticmethod
     def slots(grid, order, level):
         n = grid.sizes[order[level]]
-        lines = 1 if n == 2 else 2 * n
+        lines = 1 if n == 2 else n + 1
         return lines * math.prod(Scatter.inner(grid, order, level))
 
     @staticmethod
     def scratch(grid, order, rows, columns, dtype):
         n1 = grid.sizes[order[0]]
-        own = tuple(grid.sizes[x] for x in order[1:-1]) + (n1, rows, columns)
+        own = tuple(grid.sizes[x] for x in Scatter.kept(grid, order)) + (n1, rows, columns)
         recvs = []
         for level in range(len(order)):
             n = grid.sizes[order[level]]
-            lead = () if n == 2 else (2, n)
+            lead = () if n == 2 else (n + 1,)
             block = (rows, columns) if level == 0 else (n1, rows, columns)
             recvs.append(lead + tuple(Scatter.inner(grid, order, level)) + block)
         return [pltpu.VMEM(s, dtype) for s in [own] + recvs]
 
     @staticmethod
     def semaphores(grid, order):
-        loads = math.prod(grid.sizes[x] for x in order[1:-1])
+        loads = math.prod(grid.sizes[x] for x in Scatter.kept(grid, order))
         slots = [Scatter.slots(grid, order, level) for level in range(len(order))]
         sends = [
             (1 if grid.sizes[x] == 2 else 2 * (grid.sizes[x] - 1))
@@ -329,7 +344,7 @@
         return found
 
     def mine(self, places):
-        idx = tuple(places.get(x, self.grid.at[x]) for x in self.order[1:-1])
+        idx = tuple(places.get(x, self.grid.at[x]) for x in self.kept(self.grid, self.order))
         return self.own.at[idx]
 
     def number(self, places, axes):
@@ -344,8 +359,9 @@
         inner = math.prod(self.grid.sizes[x] for x in axes)
         number = self.number(places, axes)
         if way is not None:
-            idx = (way, target) + idx
-            number = (way * self.grid.sizes[self.order[level]] + target) * inner + number
+            line = target + 1 - way
+            idx = (line,) + idx
+            number = line * inner + number
         ref = self.recvs[level]
         return (ref.at[idx] if idx else ref), self.recv_sem.at[self.base[level] + number]
 
@@ -384,8 +400,8 @@
         guarded(cond, body)
 
     def load(self, places):
-        axes = self.order[1:-1]
-        here = {**places, self.order[-1]: self.grid.at[self.order[-1]]}
+        axes = self.kept(self.grid, self.order)
+        here = {self.order[-1]: self.grid.at[self.order[-1]], **places}
         return pltpu.make_async_copy(
             self.hbm(here), self.mine(places), self.load_sem.at[self.number(places, axes)]
         )
@@ -393,6 +409,10 @@
     def open(self):
         top = len(self.order) - 1
         axis = self.order[top]
+        if self.grid.sizes[axis] > 2:
+            for places in self.units(top + 1):
+                self.load(places).start()
+            return
         there = 1 - self.grid.at[axis]
         for places in self.units(top):
             self.send(None, self.hbm({**places, axis: there}), self.slot(top, places), axis, there)
@@ -402,7 +422,10 @@
         above = level + 1
         top = len(self.order) - 1
         total = self.mine(places)
-        if above == top:
+        if above > top:
+            self.load(places).wait()
+            return
+        if above == top and self.grid.sizes[self.order[top]] == 2:
             self.load(places).wait()
             self.take(None, self.slot(above, places), total)
             return
@@ -413,6 +436,10 @@
         else:
             self.take(p >= 1, self.slot(above, places, 0, p), total)
             self.take(p + 1 < n, self.slot(above, places, 1, p), total)
+
+    def levels(self):
+        top = len(self.order) - 1
+        return top if self.grid.sizes[self.order[top]] == 2 else top + 1
 
     def step(self, level):
         axis = self.order[level]
@@ -608,64 +635,223 @@
 
 ALL_AXES = ("a", "b", "core", "f")
 SLOT_AXES = ("a", "b", "core")
-BFA, AFB = ("b", "f", "a", "core"), ("a", "f", "b", "core")
-FAB, FBA = ("f", "a", "b", "core"), ("f", "b", "a", "core")
+CHIP_AXES = ("a", "b", "f")
+BFA, AFB, FAB, FBA = ("b", "f", "a"), ("a", "f", "b"), ("f", "a", "b"), ("f", "b", "a")
 AB, BA = ("a", "b", "core"), ("b", "a", "core")
-
-
-def gather_kernel(grid, portions, layout, n, *refs):
-    srcs, dsts, held = refs[:n], refs[n : 2 * n], refs[2 * n : 3 * n]
-    send, recv, local = refs[3 * n :]
+CORE = ("core",)
+
+
+FRONT_SRC = ("q", "k", "v", "o", "g", "u", "d", "gains")
+
+
+def front_kernel(grid, plan, *refs):
+    n = len(FRONT_SRC)
+    src = dict(zip(FRONT_SRC, refs[:n]))
+    tokens_ref, cosine_ref, sine_ref = refs[n : n + 3]
+    outs = refs[n + 3 : n + 15]
+    wqkv_ref, wo_ref, wgu_ref, wd_ref, allgains_ref, k_out, v_out = outs[:7]
+    normed_ref, gains_ref, raw_ref, qlow_ref, inv_ref = outs[7:]
+    scratch = refs[n + 15 :]
+    held = dict(zip(FRONT_SRC, scratch[:n]))
+    weights, klow, vlow, gbuf = scratch[n : n + 4]
+    send, recv, local, load = scratch[n + 4 :]
     grid.enter()
+    grid.barrier()
     send, recv = Pool(send), Pool(recv)
-    mine = tuple(grid.at[x] for x in layout)
-    for i in range(n):
-        pltpu.make_async_copy(srcs[i], held[i], local.at[i]).start()
-    parts = []
-    for i, low, high, order in portions:
+    width = tokens_ref.shape[1]
+    rows = tokens_ref.shape[0]
+    spans = {"q": (wqkv_ref, 0), "k": (wqkv_ref, H * HD), "v": (wqkv_ref, (H + KVH) * HD)}
+    hidden = src["g"].shape[1]
+    spans.update({"o": (wo_ref, 0), "g": (wgu_ref, 0), "u": (wgu_ref, hidden), "d": (wd_ref, 0)})
+    spans["gains"] = (allgains_ref, 0)
+    mine = tuple(grid.at[x] for x in ALL_AXES)
+
+    def own_copy(i, name):
+        dst, at = spans[name]
+        return pltpu.make_async_copy(
+            held[name], dst.at[mine + (slice(None), pl.ds(at, src[name].shape[1]))], local.at[i]
+        )
+
+    for i, name in enumerate(FRONT_SRC):
+        pltpu.make_async_copy(src[name], held[name], local.at[i]).start()
+
+    def part(name, low, high, order):
+        dst, at = spans[name]
         sends, takes = Gather.semaphores(grid, order)
-        columns = pl.ds(low, high - low)
-        parts.append(
-            Gather(grid, order, srcs[i], dsts[i], columns, send.take(sends), recv.take(takes), layout)
+        columns = pl.ds(at + low, high - low)
+        return Gather(
+            grid, order, src[name].at[:, low:high], dst, columns, send.take(sends), recv.take(takes), ALL_AXES
         )
-        parts[-1].open()
-    for i in range(n):
-        pltpu.make_async_copy(srcs[i], held[i], local.at[i]).wait()
-        pltpu.make_async_copy(held[i], dsts[i].at[mine], local.at[i]).start()
-    for i in range(n):
-        pltpu.make_async_copy(held[i], dsts[i].at[mine], local.at[i]).wait()
-    for part in parts:
-        part.first()
-    for level in range(1, len(layout)):
-        for part in parts:
-            part.arrivals(level)
-    for part in parts:
-        part.close()
-
-
-def gather(grid, layout, portions, name, *blocks):
-    n = len(blocks)
-    sends, takes = [sum(x) for x in zip(*[Gather.semaphores(grid, p[3]) for p in portions])]
-    places = tuple(grid.sizes[x] for x in layout)
-    total = math.prod(places)
+
+    early = [part(*p) for p in plan[0]]
+    late = [part(*p) for p in plan[1]]
+    for p in early:
+        p.open()
+    for p in late:
+        p.open()
+    for i, name in enumerate(FRONT_SRC):
+        pltpu.make_async_copy(src[name], held[name], local.at[i]).wait()
+        own_copy(i, name).start()
+    inputs = tokens_ref[...].astype(jnp.float32)
+    inverse = lax.rsqrt(jnp.mean(inputs * inputs, axis=-1, keepdims=True) + EPSILON)
+    inv_ref[...] = jnp.broadcast_to(inverse, (rows, 128))
+    for i, name in enumerate(FRONT_SRC):
+        own_copy(i, name).wait()
+
+    for p in early:
+        p.first()
+    for level in (1, 2):
+        for p in early:
+            p.arrivals(level)
+    pump = []
+    for p in late:
+        pump.append(p.first)
+    for level in (1, 2, 3):
+        for p in late:
+            pump.append(functools.partial(p.arrivals, level))
+
+    def step(count):
+        for _ in range(count):
+            if pump:
+                pump.pop(0)()
+
+    step(len(late))
+    for p in early:
+        p.arrivals(3)
+
+    places = math.prod(grid.sizes[x] for x in ALL_AXES)
+    copy = pltpu.make_async_copy(allgains_ref, gbuf, load.at[0])
+    copy.start()
+    big = pltpu.make_async_copy(wqkv_ref, weights, load.at[1])
+    big.start()
+    copy.wait()
+    blocks = gbuf[...].reshape((places,) + gbuf.shape[-2:]).astype(jnp.float32)
+    gains = jnp.sum(blocks, axis=0)
+    gains_ref[...] = gains
+    lanes = width // 128
+    for j in range(lanes):
+        cols = slice(j * 128, (j + 1) * 128)
+        part_of = tokens_ref[:, cols].astype(jnp.float32) * inv_ref[...] * gains_ref[j : j + 1, :]
+        normed_ref[:, cols] = part_of.astype(jnp.bfloat16)
+    big.wait()
+    step(1)
+    flat = weights.reshape(width, weights.shape[-1])
+    normed = normed_ref[...]
+    chunk = 2 * HD
+
+    def heads(low_out, gain_row, out_at, raw_at, c):
+        at = pl.ds(pl.multiple_of(raw_at + c * chunk, chunk), chunk)
+        raw = jnp.dot(normed, flat[:, at], preferred_element_type=jnp.float32)
+        raw_ref[:, at] = raw
+        done = []
+        for i in range(2):
+            one = raw[:, i * HD : (i + 1) * HD]
+            unit = one * lax.rsqrt(jnp.mean(one * one, axis=-1, keepdims=True) + EPSILON)
+            unit = unit * gains_ref[gain_row : gain_row + 1, :]
+            done.append(unit * cosine_ref[...] + pltpu.roll(unit, HD // 2, 1) * sine_ref[...])
+        to = pl.ds(pl.multiple_of(out_at + c * chunk, chunk), chunk)
+        low_out[:, to] = jnp.concatenate(done, axis=1).astype(jnp.bfloat16)
+
+    def loop(count, body):
+        def once(c, carry):
+            body(c)
+            return carry
+
+        lax.fori_loop(0, count, once, 0)
+
+    def to_values(c):
+        at = pl.ds(pl.multiple_of((H + KVH) * HD + c * chunk, chunk), chunk)
+        to = pl.ds(pl.multiple_of(c * chunk, chunk), chunk)
+        raw = jnp.dot(normed, flat[:, at], preferred_element_type=jnp.float32)
+        vlow[:, to] = raw.astype(jnp.bfloat16)
+
+    loop(KVH // 2, functools.partial(heads, klow, 2 * lanes + 1, 0, H * HD))
+    loop(KVH // 2, to_values)
+
+    def pair(source, dst, order):
+        sends, takes = Gather.semaphores(grid, order)
+        return Gather(
+            grid, order, source, dst, pl.ds(0, KVH * HD), send.take(sends), recv.take(takes), SLOT_AXES
+        )
+
+    slot = tuple(grid.at[x] for x in SLOT_AXES)
+    slabs = [pair(klow, k_out, AB), pair(vlow, v_out, BA)]
+    saves = [
+        pltpu.make_async_copy(klow, k_out.at[slot], load.at[0]),
+        pltpu.make_async_copy(vlow, v_out.at[slot], load.at[1]),
+    ]
+    for p, save in zip(slabs, saves):
+        p.open()
+        save.start()
+    step(2)
+    loop(KVH // 2, functools.partial(heads, qlow_ref, 2 * lanes, 0, 0))
+    for p, save in zip(slabs, saves):
+        save.wait()
+        p.first()
+    step(2)
+    loop(KVH // 2, functools.partial(heads, qlow_ref, 2 * lanes, H * HD // 2, H * HD // 2))
+    for p in slabs:
+        p.arrivals(1)
+    step(len(pump))
+    for p in slabs:
+        p.arrivals(2)
+    for p in early + late + slabs:
+        p.close()
+
+
+def front(grid, plan, blocks, tokens, cosine, sine):
+    n = len(FRONT_SRC)
+    rows, width = tokens.shape
+    places = tuple(grid.sizes[x] for x in ALL_AXES)
+    slots = tuple(grid.sizes[x] for x in SLOT_AXES)
+    by = dict(zip(FRONT_SRC, blocks))
+    low, f32 = jnp.bfloat16, jnp.float32
+    full = (H + 2 * KVH) * HD
+    counts = [Gather.semaphores(grid, p[3]) for p in plan[0] + plan[1]]
+    counts += [Gather.semaphores(grid, AB), Gather.semaphores(grid, BA)]
+    sends, takes = [sum(x) for x in zip(*counts)]
+    shape = jax.ShapeDtypeStruct
+    vmem = pl.BlockSpec(memory_space=pltpu.VMEM)
     outs = pl.pallas_call(
-        functools.partial(gather_kernel, grid, portions, layout, n),
-        out_shape=[jax.ShapeDtypeStruct(places + x.shape, x.dtype) for x in blocks],
-        in_specs=[ANY] * n,
-        out_specs=[ANY] * n,
+        functools.partial(front_kernel, grid, plan),
+        out_shape=[
+            shape(places + (by["q"].shape[0], full), low),
+            shape(places + by["o"].shape, low),
+            shape(places + (by["g"].shape[0], 2 * by["g"].shape[1]), low),
+            shape(places + by["d"].shape, low),
+            shape(places + by["gains"].shape, low),
+            shape(slots + (rows, KVH * HD), low),
+            shape(slots + (rows, KVH * HD), low),
+            shape((rows, width), low),
+            shape(by["gains"].shape, f32),
+            shape((rows, (H + KVH) * HD), f32),
+            shape((rows, H * HD), low),
+            shape((rows, 128), f32),
+        ],
+        in_specs=[ANY] * n + [vmem] * 3,
+        out_specs=[ANY] * 7 + [vmem] * 5,
         scratch_shapes=[pltpu.VMEM(x.shape, x.dtype) for x in blocks]
         + [
+            pltpu.VMEM(places + (by["q"].shape[0], full), low),
+            pltpu.VMEM((rows, KVH * HD), low),
+            pltpu.VMEM((rows, KVH * HD), low),
+            pltpu.VMEM(places + by["gains"].shape, low),
             pltpu.SemaphoreType.DMA((sends,)),
             pltpu.SemaphoreType.DMA((takes,)),
             pltpu.SemaphoreType.DMA((n,)),
+            pltpu.SemaphoreType.DMA((2,)),
         ],
-        compiler_params=pltpu.CompilerParams(has_side_effects=True),
-        name=name,
-    )(*blocks)
-    return [x.reshape(total * x.shape[-2], x.shape[-1]) for x in outs]
-
-
-def scatter_kernel(grid, portions, layout, n, *refs):
+        compiler_params=pltpu.CompilerParams(
+            has_side_effects=True, vmem_limit_bytes=60 * 2**20, collective_id=0
+        ),
+        name="front",
+    )(*blocks, tokens, cosine, sine)
+    wqkv, wo, wgu, wd, _, keys, vals, normed, gains, raw, qlow, inverse = outs
+    flat = [x.reshape(-1, x.shape[-1]) for x in (wqkv, wo, wgu, wd, keys, vals)]
+    return flat + [normed, gains, raw, qlow, inverse]
+
+
+def scatter_kernel(grid, portions, layouts, n, *refs):
     srcs, outs, scratch = refs[:n], refs[n : 2 * n], list(refs[2 * n : -3])
     load, send, recv = [Pool(x) for x in refs[-3:]]
     grid.enter()
@@ -686,30 +872,32 @@
                 send.take(sends),
                 recv.take(takes),
                 outs[i].at[:, low:high],
-                layout,
+                layouts[i],
             )
         )
         parts[-1].open()
-    for level in range(len(layout) - 2, -1, -1):
+    for level in (2, 1, 0):
         for part in parts:
-            part.step(level)
+            if level < part.levels():
+                part.step(level)
     for part in parts:
         part.finish()
     for part in parts:
         part.close()
 
 
-def scatter(grid, layout, portions, name, dtypes, *sums):
+def scatter(grid, layouts, portions, name, dtypes, *sums):
     n = len(sums)
-    places = tuple(grid.sizes[x] for x in layout)
-    total = math.prod(places)
-    blocks = [x.reshape(places + (x.shape[0] // total, x.shape[1])) for x in sums]
+    blocks = []
+    for layout, x in zip(layouts, sums):
+        places = tuple(grid.sizes[axis] for axis in layout)
+        blocks.append(x.reshape(places + (x.shape[0] // math.prod(places), x.shape[1])))
     loads, sends, takes = [sum(x) for x in zip(*[Scatter.semaphores(grid, p[3]) for p in portions])]
     scratch = []
     for i, low, high, order in portions:
         scratch += Scatter.scratch(grid, order, blocks[i].shape[-2], high - low, blocks[i].dtype)
     return pl.pallas_call(
-        functools.partial(scatter_kernel, grid, portions, layout, n),
+        functools.partial(scatter_kernel, grid, portions, layouts, n),
         out_shape=[jax.ShapeDtypeStruct(x.shape[-2:], t) for x, t in zip(blocks, dtypes)],
         in_specs=[ANY] * n,
         out_specs=[pl.BlockSpec(memory_space=pltpu.VMEM)] * n,
@@ -724,15 +912,26 @@
     )(*blocks)
 
 
-def padded(x, rows):
-    return jnp.pad(x, ((0, rows - x.shape[0]), (0, 128 - x.shape[1])))
-
-
 def gain_rows(total, *gains):
     pieces = [x.reshape(total, 1, -1) for x in gains]
     pieces = [jnp.pad(x, ((0, 0), (0, 0), (0, 128 - x.shape[2]))) for x in pieces]
     block = jnp.concatenate(pieces, axis=1)
     return jnp.pad(block, ((0, 0), (0, 8 - len(gains)), (0, 0))).reshape(total * 8, 128)
+
+
+def swapped(x):
+    count = lax.axis_size("ctx")
+    return lax.ppermute(x, "ctx", [(i, i ^ 1) for i in range(count)])
+
+
+def chip_sums(left, right, right_other):
+    core = lax.axis_index("ctx") % 2
+    rows, width = left.shape
+    split = left.reshape(rows, lax.axis_size("ctx") // 2, 2, -1)
+    mine = lax.dynamic_index_in_dim(split, core, 2, False).reshape(rows, width // 2)
+    theirs = lax.dynamic_index_in_dim(split, 1 - core, 2, False).reshape(rows, width // 2)
+    both = jnp.concatenate([mine, swapped(theirs)], axis=0)
+    return left_dot(both, jnp.concatenate([right, right_other], axis=0)).astype(jnp.bfloat16)
 
 
 def on_device(
@@ -758,76 +957,78 @@
     ratio = H // KVH
     low = jnp.bfloat16
 
-    gains = jnp.concatenate(
-        [padded(x.reshape(1, -1), 1) for x in (attn_gain, mlp_gain, query_gain, key_gain)], axis=0
-    )
+    device = lax.axis_index("ctx") * lax.axis_size("fsdp") + lax.axis_index("fsdp")
+    gains = jnp.zeros((width // 128 * 2 + 16) * 128, low)
+    for at, x in ((0, attn_gain), (width, mlp_gain), (2 * width, query_gain), (2 * width + HD, key_gain)):
+        gains = lax.dynamic_update_slice_in_dim(gains, x, at + device * x.shape[0], 0)
+    gains = gains.reshape(-1, 128)
     hidden_width = gate_weight.shape[1]
-    wqkv = jnp.concatenate([query_weight, key_weight, value_weight], axis=1)
-    wgu = jnp.concatenate([gate_weight, up_weight], axis=1)
-    half = wqkv.shape[1] // 2
-    full_qkv, full_output, full_gu, full_down, all_gains = gather(
-        grid,
-        ALL_AXES,
-        [
-            (0, 0, half, BFA),
-            (0, half, 2 * half, AFB),
-            (1, 0, width // 2, FAB),
-            (1, width // 2, width, FBA),
-            (2, 0, hidden_width, BFA),
-            (2, hidden_width, 2 * hidden_width, AFB),
-            (3, 0, width // 2, FAB),
-            (3, width // 2, width, FBA),
-            (4, 0, 128, FAB),
-        ],
-        "gather_weights",
-        wqkv,
-        output_weight,
-        wgu,
-        down_weight,
-        padded(gains, 16),
-    )
-    all_gains = all_gains.reshape(total, 16, 128)
-    gain_one, gain_two, query_scale, key_scale = [
-        all_gains[:, i, : x.shape[0]].reshape(-1).astype(jnp.float32)
-        for i, x in enumerate((attn_gain, mlp_gain, query_gain, key_gain))
-    ]
 
     place = lax.axis_index("ctx")
     blocks = block_map.reshape(-1)
     own_blocks = lax.dynamic_slice_in_dim(blocks, 2 * place, 2, 0)
-    slots = jnp.argsort(blocks).astype(jnp.int32)
+    numbers = jnp.arange(2 * pairs, dtype=jnp.int32)
+    slots = jnp.sum(jnp.where(blocks[None, :] == numbers[:, None], numbers[None, :], 0), axis=1)
     high_slot = (own_blocks[1] > own_blocks[0]).astype(jnp.int32)
     table = jnp.concatenate([slots, high_slot[None], jnp.max(own_blocks)[None]]).astype(jnp.int32)
 
     spots = (own_blocks[:, None] * BLK + jnp.arange(BLK, dtype=jnp.int32)).reshape(rows)
     cosine, sine = rope_tables(spots)
+    turned = jnp.concatenate([-sine[:, : HD // 2], sine[:, HD // 2 :]], axis=1)
+    half_q, half_k = H * HD // 2, KVH * HD // 2
+    half = half_q + 2 * half_k
+    plan = (
+        (
+            ("gains", 0, 128, FAB + CORE),
+            ("q", 0, half_q, FAB + CORE),
+            ("q", half_q, 2 * half_q, FBA + CORE),
+            ("k", 0, 2 * half_k, BFA + CORE),
+            ("v", 0, 2 * half_k, AFB + CORE),
+        ),
+        (
+            ("o", 0, width // 2, BFA + CORE),
+            ("o", width // 2, width, AFB + CORE),
+            ("g", 0, hidden_width, BFA + CORE),
+            ("u", 0, hidden_width, AFB + CORE),
+            ("d", 0, width // 2, BFA + CORE),
+            ("d", width // 2, width, AFB + CORE),
+        ),
+    )
+    (
+        full_qkv,
+        full_output,
+        full_gu,
+        full_down,
+        key_all,
+        value_all,
+        normed,
+        gains,
+        raw,
+        query_low,
+        inverse_one,
+    ) = front(
+        grid,
+        plan,
+        (query_weight, key_weight, value_weight, output_weight, gate_weight, up_weight, down_weight, gains),
+        tokens.reshape(rows, width),
+        cosine,
+        turned,
+    )
+    attended, attended_low, totals = attention(table, pairs, query_low, key_all, value_all)
+    lanes = width // 128
+    gain_one, gain_two = gains[:lanes].reshape(-1), gains[lanes : 2 * lanes].reshape(-1)
+    query_scale, key_scale = gains[2 * lanes], gains[2 * lanes + 1]
+    inverse_one = inverse_one[:, :1]
+    inputs = tokens.reshape(rows, width).astype(jnp.float32)
+    normal_one = inputs * inverse_one
     cosine = cosine.reshape(rows, 1, HD)
     sine = sine.reshape(rows, 1, HD)
-    inputs = tokens.reshape(rows, width).astype(jnp.float32)
-    inverse_one = lax.rsqrt(jnp.mean(inputs * inputs, axis=-1, keepdims=True) + EPSILON)
-    normal_one = inputs * inverse_one
-    normed = (normal_one * gain_one).astype(low)
-    raw = plain_dot(normed, full_qkv)
     query_raw = raw[:, : H * HD].reshape(rows, H, HD)
-    key_raw = raw[:, H * HD : (H + KVH) * HD].reshape(rows, KVH, HD)
-    value_low = raw[:, (H + KVH) * HD :].astype(low)
+    key_raw = raw[:, H * HD :].reshape(rows, KVH, HD)
     query_inverse = lax.rsqrt(jnp.mean(query_raw * query_raw, axis=-1, keepdims=True) + EPSILON)
     query_unit = query_raw * query_inverse
-    query_normed = query_unit * query_scale
-    query_low = (query_normed * cosine + rotate(query_normed) * sine).astype(low).reshape(rows, H * HD)
     key_inverse = lax.rsqrt(jnp.mean(key_raw * key_raw, axis=-1, keepdims=True) + EPSILON)
     key_unit = key_raw * key_inverse
-    key_normed = key_unit * key_scale
-    key_low = (key_normed * cosine + rotate(key_normed) * sine).astype(low).reshape(rows, KVH * HD)
-    key_all, value_all = gather(
-        grid,
-        SLOT_AXES,
-        [(0, 0, KVH * HD, AB), (1, 0, KVH * HD, BA)],
-        "gather_keys",
-        key_low,
-        value_low,
-    )
-    attended, attended_low, totals = attention(table, pairs, query_low, key_all, value_all)
     row_totals = totals.reshape(KVH, 2, ratio, BLK).transpose(1, 3, 0, 2).reshape(rows, H, 1)
     middle = inputs + plain_dot(attended_low, full_output)
     inverse_two = lax.rsqrt(jnp.mean(middle * middle, axis=-1, keepdims=True) + EPSILON)
@@ -845,30 +1046,14 @@
     grad_gate = (grad_hidden * upper * sigmoid_gate * (1.0 + gate * (1.0 - sigmoid_gate))).astype(low)
     grad_upper = (grad_hidden * activated).astype(low)
     grad_both = jnp.concatenate([grad_gate, grad_upper], axis=1)
-    grad_down = left_dot(hidden, upstream).astype(low)
-    grad_gu = left_dot(normed_two, grad_both).astype(low)
+    grad_down = chip_sums(hidden, upstream, swapped(upstream))
+    grad_gu = chip_sums(normed_two, grad_both, swapped(grad_both))
     grad_normed_two = right_dot(grad_both, full_gu)
     grad_gain_two = jnp.sum(grad_normed_two * normal_two, axis=0)
     grad_middle = upstream.astype(jnp.float32) + norm_back(grad_normed_two, normal_two, inverse_two, gain_two)
     f32 = jnp.float32
-    out_gu, out_down, out_gain_two = scatter(
-        grid,
-        ALL_AXES,
-        [
-            (0, 0, hidden_width, BFA),
-            (0, hidden_width, 2 * hidden_width, AFB),
-            (1, 0, width // 2, FAB),
-            (1, width // 2, width, FBA),
-            (2, 0, 128, FAB),
-        ],
-        "scatter_mlp",
-        (f32, f32, f32),
-        grad_gu,
-        grad_down,
-        gain_rows(total, grad_gain_two),
-    )
     branch_grad = grad_middle.astype(low)
-    grad_woutput = left_dot(attended_low, branch_grad).astype(low)
+    grad_woutput = chip_sums(attended_low, branch_grad, swapped(branch_grad))
     grad_attended = right_dot(branch_grad, full_output).reshape(rows, H, HD)
     grad_summed = (grad_attended / row_totals).astype(low).reshape(rows, H * HD)
     drift = jnp.sum(grad_attended * attended.reshape(rows, H, HD), axis=-1) / row_totals[..., 0]
@@ -876,14 +1061,27 @@
     grad_query, grad_keys, grad_values = attention_back(
         table, pairs, query_low, key_all, value_all, grad_summed, drift
     )
-    own_keys, own_values = scatter(
+    f32 = jnp.float32
+    own_keys, own_values, out_gu, out_down, out_output = scatter(
         grid,
-        SLOT_AXES,
-        [(0, 0, KVH * HD, AB), (1, 0, KVH * HD, BA)],
-        "scatter_keys",
-        (f32, low),
+        [SLOT_AXES] * 2 + [CHIP_AXES] * 3,
+        [
+            (0, 0, KVH * HD, AB),
+            (1, 0, KVH * HD, BA),
+            (2, 0, hidden_width, BFA),
+            (2, hidden_width, 2 * hidden_width, AFB),
+            (3, 0, width // 2, BFA),
+            (3, width // 2, width, AFB),
+            (4, 0, width // 2, BFA),
+            (4, width // 2, width, AFB),
+        ],
+        "scatter_mlp",
+        (f32, low, f32, f32, f32),
         grad_keys,
         grad_values,
+        grad_gu,
+        grad_down,
+        grad_woutput,
     )
     grad_qrot = grad_query.reshape(rows, H, HD)
     grad_qnormed = grad_qrot * cosine + unrotate(grad_qrot) * sine
@@ -901,25 +1099,24 @@
         ],
         axis=1,
     )
-    grad_wqkv = left_dot(normed, grad_raw).astype(low)
+    grad_wqkv = chip_sums(normed, grad_raw, swapped(grad_raw))
     grad_normed = right_dot(grad_raw, full_qkv)
     grad_gain_one = jnp.sum(grad_normed * normal_one, axis=0)
     grad_inputs = grad_middle + norm_back(grad_normed, normal_one, inverse_one, gain_one)
-    out_qkv, out_output, out_gains = scatter(
+    out_qkv, out_gains = scatter(
         grid,
-        ALL_AXES,
+        [CHIP_AXES, ALL_AXES],
         [
-            (0, 0, half, BFA),
-            (0, half, 2 * half, AFB),
-            (1, 0, width // 2, FAB),
-            (1, width // 2, width, FBA),
-            (2, 0, 128, FAB),
+            (0, 0, half // 2, FAB),
+            (0, half // 2, half, FBA),
+            (0, half, 3 * half // 2, BFA),
+            (0, 3 * half // 2, 2 * half, AFB),
+            (1, 0, 128, FAB + CORE),
         ],
         "scatter_attention",
-        (f32, f32, f32),
+        (f32, f32),
         grad_wqkv,
-        grad_woutput,
-        gain_rows(total, grad_gain_one, grad_qscale, grad_kscale),
+        gain_rows(total, grad_gain_one, grad_qscale, grad_kscale, grad_gain_two),
     )
     return (
         output,
@@ -931,7 +1128,7 @@
         out_gains[1, : query_gain.shape[0]],
         out_gains[2, : key_gain.shape[0]],
         out_output,
-        out_gain_two[0, : mlp_gain.shape[0]],
+        out_gains[3, : mlp_gain.shape[0]],
         out_gu[:, :hidden_width],
         out_gu[:, hidden_width:],
         out_down,

time: 649 us -> 631 us (0.972)
  Pallas kernels: 498 us -> 445 us
  local copies, waits for them, and re-layouts: 34.3 us -> 78.7 us
  other arithmetic: 36.1 us -> 26.4 us
    pallas_call x5 -> x3, Pallas kernels: 456 us -> 404 us  [the longest x2 225 us: scatter(): pl.pallas_call(functools.partial(scatter_kernel, grid, portions, layouts,...]
    unnamed x94 -> x134, local copies, waits for them, and re-layouts: 9.64 us -> 32.2 us
    dynamic_slice x0 -> x4, local copies, waits for them, and re-layouts: none -> 12.9 us  [chip_sums(): lax.dynamic_index_in_dim(split, core, 2, False).reshape(rows, width // 2)]
    dot_general x4, matrix products: 21.4 us -> 31.1 us  [left_dot(): lax.dot_general(left, right, (((0,), (0,)), ((), ())), preferred_element_...]
    reshape x0 -> x4, local copies, waits for them, and re-layouts: none -> 9.62 us  [chip_sums(): split = left.reshape(rows, lax.axis_size('ctx') // 2, 2, -1)]
    dot_general x4 -> x3, matrix products: 20.8 us -> 13.2 us  [plain_dot(): return jnp.dot(left, right, preferred_element_type=jnp.float32)]
    dot_general x4, matrix products: 28.8 us -> 21.6 us  [right_dot(): lax.dot_general(left, right, (((1,), (1,)), ((), ())), preferred_element_...]
  transfers between devices with their start and end apart: 0 -> 8, of which waited for: 0 -> 0; matrix products, arithmetic and copies ran while one was open for 0% -> 19% of each run, Pallas kernels for 0% -> 28%
where the time goes in v2:
time: 631 us; the launch traced here: 621 us
  Pallas kernels  445 us (71%)
  local copies, waits for them, and re-layouts  78.7 us (12%)
  matrix products  65.8 us (10%)
  other arithmetic  26.4 us (4%)
    pallas_call x2, Pallas kernels, scatter(): pl.pallas_call(functools.partial(scatter_kernel, grid, portions, layouts,...  225 us
    pallas_call x1, Pallas kernels, front(): pl.pallas_call(functools.partial(front_kernel, grid, plan), out_shape=[sh...  179 us
    unnamed x134, local copies, waits for them, and re-layouts  32.2 us
    dot_general x4, matrix products, left_dot(): lax.dot_general(left, right, (((0,), (0,)), ((), ())), preferred_element_...  31.1 us
    pallas_call x1, Pallas kernels, attention_back(): pl.pallas_call(functools.partial(attention_back_kernel, pairs), grid_spec...  28.1 us
    dot_general x4, matrix products, right_dot(): lax.dot_general(left, right, (((1,), (1,)), ((), ())), preferred_element_...  21.6 us
    dot_general x3, matrix products, plain_dot(): return jnp.dot(left, right, preferred_element_type=jnp.float32)  13.2 us
    dynamic_slice x4, local copies, waits for them, and re-layouts, chip_sums(): lax.dynamic_index_in_dim(split, core, 2, False).reshape(rows, width // 2)  12.9 us
  transfers between devices with their start and end apart: 8, of which 0 were waited for; matrix products, arithmetic and copies ran while one was open for 19% of the time, Pallas kernels for 28%

profile of v2, /device:TPU:0, one launch (start us, length us, event | category | flops | bytes accessed | tf_op | source)
XLA Modules:
  0.0 621.4 jit_solution(102862739258217007)
XLA Ops:
  10.8 179.0 %front.1 = (bf16[2,2,2,4,32,4096]{5,4,3,2,1,0:T(8,128)(2,1)}, bf16[2,2,2,4,64,1024]{5,4,3,2,1,0:T(8,128)(2,1)}, bf16[2,2,2,4,32,6144]{5,4,3,2,1,0:T(8,128)(2,1)}...) custom-call(bf16[32,2048]{1,0:T(8,128)(2,1)} %refs_0_.1, ...), custom_call_target="tpu_custom_call" | custom-call | tf_op jit(solution)/shard_map/front/pallas_call | solution.py:815
  189.8 12.6 %attention.1 = (f32[256,2048]{1,0:T(8,128)}, bf16[256,2048]{1,0:T(8,128)(2,1)}, f32[8,2,256]{2,1,0:T(2,128)}) custom-call(s32[18]{0:T(128)} %pad_add_fusion.table, bf16[256,2048]{1,0:T(8,128)(2,1)} %get-tuple-element.37.q_ref, bf16[2048,1024]{1,0:T(8,128)(2,1)} %bitcast.192, bf16[2048,1024]{1,0:T(8,128)(2,1)} %bitcast.194), custom_call_target="tpu_custom_call" | custom-call | tf_op jit(solution)/shard_map/attention/pallas_call | solution.py:550
  202.5 3.9 multiply_reduce_fusion.9
  207.2 6.7 %fusion.68 = f32[256,6144]{1,0:T(8,128)S(1)} fusion(bf16[256,1024]{1,0:T(8,128)(2,1)S(1)} %multiply_convert_fusion.3, bf16[1024,6144]{1,0:T(8,128)(2,1)} %bitcast.198), kind=kOutput, calls=%fused_computation.160 | convolution fusion | flops 3221225472 | bytes 19398656 | tf_op jit(solution)/shard_map/dot_general | solution.py:57
  214.0 4.4 multiply_convert_fusion.1
  218.5 8.4 %multiply_reduce_fusion.4 = (f32[1024]{0:T(1024)}, f32[256]{0:T(256)S(1)}, f32[256,1024]{1,0:T(8,128)S(1)}) fusion(f32[256,1024]{1,0:T(8,128)S(1)} %get-tuple-element.112, f32[256]{0:T(256)S(1)} %add_rsqrt_fusion.2, f32[1024]{0:T(1024)S(1)} %get-tuple-element.99, bf16[1024,6144]{1,0:T(8,128)(2,1)} %bitcast.199, ...), kind=kOutput, calls=%fused_computation.74 | convolution fusion | flops 3229088512 | bytes 17836032 | tf_op jit(solution)/shard_map/dot_general | solution.py:51
  229.5 3.2 constant_dynamic-slice_fusion.3
  235.3 4.4 reshape.302
  239.7 4.4 constant_dynamic-slice_fusion.5
  244.1 3.2 copy.63
  247.8 4.1 pad_maximum_fusion
  259.6 5.3 multiply_reduce_fusion.2
  267.8 28.1 %attention_back.1 = (f32[256,2048]{1,0:T(8,128)}, bf16[2048,1024]{1,0:T(8,128)(2,1)}, bf16[2048,1024]{1,0:T(8,128)(2,1)}) custom-call(s32[18]{0:T(128)} %pad_add_fusion.table, bf16[256,2048]{1,0:T(8,128)(2,1)} %get-tuple-element.37.q_ref, bf16[2048,1024]{1,0:T(8,128)(2,1)} %bitcast.193, bf16[2048,1024]{1,0:T(8,128)(2,1)} %bitcast.195, ...), custom_call_target="tpu_custom_call" | custom-call | tf_op jit(solution)/shard_map/attention_back/pallas_call | solution.py:612
  305.7 5.1 multiply_reduce_fusion
  317.7 3.3 constant_dynamic-slice_fusion.1
  320.9 3.5 copy.64
  324.4 4.6 copy.62
  339.9 4.3 convolution_convert_fusion.3
  344.2 4.9 convolution_convert_fusion.2
  349.1 15.9 %convolution_convert_fusion = bf16[512,6144]{1,0:T(8,128)(2,1)} fusion(bf16[256,6144]{1,0:T(8,128)(2,1)} %collective-permute-done.1, bf16[256,3072]{1,0:T(8,128)(2,1)S(1)} %copy-done.28, bf16[256,3072]{1,0:T(8,128)(2,1)S(1)} %copy-done.26, bf16[256,512]{0,1:T(8,128)(2,1)S(1)} %collective-permute-done, bf16[256,512]{0,1:T(8,128)(2,1)S(1)} %bitcast.227), kind=kOutput, calls=%fused_computation | convolution fusion | flops 3244294144 | bytes 13107200 | tf_op jit(solution)/shard_map/dot_general | solution.py:45
  365.0 143.5 %scatter_mlp.1 = (f32[256,1024]{1,0:T(8,128)}, bf16[256,1024]{1,0:T(8,128)(2,1)}, f32[32,6144]{1,0:T(8,128)}, f32[96,1024]{1,0:T(8,128)}, f32[64,1024]{1,0:T(8,128)}) custom-call(bf16[2,2,2,256,1024]{4,3,2,1,0:T(8,128)(2,1)} %bitcast.208, bf16[2,2,2,256,1024]{4,3,2,1,0:T(8,128)(2,1)} %bitcast.209, bf16[2,2,4,32,6144]{4,3,2,1,0:T(8,128)(2,1)} %bitcast.207, ...), custom_call_target="tpu_custom_call" | custom-call | tf_op jit(solution)/shard_map/scatter_mlp/pallas_call | solution.py:899
  516.9 3.4 fusion.29
  526.1 6.0 convolution_convert_fusion.1
  532.2 81.4 %scatter_attention.1 = (f32[32,4096]{1,0:T(8,128)}, f32[8,128]{1,0:T(8,128)}) custom-call(bf16[2,2,4,32,4096]{4,3,2,1,0:T(8,128)(2,1)} %bitcast.210, f32[2,2,2,4,8,128]{5,4,3,2,1,0:T(8,128)} %bitcast.224), custom_call_target="tpu_custom_call" | custom-call | tf_op jit(solution)/shard_map/scatter_attention/pallas_call | solution.py:899
  (215 shorter events, 74.5 us)
Async XLA Ops:
  189.8 12.6 %copy-start.17 = (bf16[1,256,1024]{2,1,0:T(8,128)(2,1)S(1)}, bf16[1,256,1024]{2,1,0:T(8,128)(2,1)}, u32[]{:S(2)}) copy-start(bf16[1,256,1024]{2,1,0:T(8,128)(2,1)} %param.14) | copy-start | bytes 1572868
  206.3 20.6 %copy-start.1 = (f32[256,1024]{1,0:T(8,128)}, f32[256,1024]{1,0:T(8,128)S(1)}, u32[]{:S(2)}) copy-start(f32[256,1024]{1,0:T(8,128)S(1)} %get-tuple-element.112) | copy-start | bytes 3145732
  206.4 20.6 %copy-start.44 = (f32[256]{0:T(256)}, f32[256]{0:T(256)S(1)}, u32[]{:S(2)}) copy-start(f32[256]{0:T(256)S(1)} %add_rsqrt_fusion.2) | copy-start | bytes 3076
  207.0 19.9 %copy-start.39 = (f32[1024]{0:T(1024)}, f32[1024]{0:T(1024)S(1)}, u32[]{:S(2)}) copy-start(f32[1024]{0:T(1024)S(1)} %get-tuple-element.99) | copy-start | bytes 12292
  207.0 6.9 %slice-start.2 = ((s8[6291456]{0:T(1024)(128)(4,1)}), s8[4194304]{0:T(1024)(128)(4,1)S(1)}, s32[]{:S(2)}) async-start(s8[6291456]{0:T(1024)(128)(4,1)} %bitcast.236), calls=%async_computation.2 | async-start | bytes 8388608
  207.2 6.8 %copy-start.8 = (bf16[256,1024]{1,0:T(8,128)(2,1)}, bf16[256,1024]{1,0:T(8,128)(2,1)S(1)}, u32[]{:S(2)}) copy-start(bf16[256,1024]{1,0:T(8,128)(2,1)S(1)} %multiply_convert_fusion.3) | copy-start | bytes 1572868
  207.2 6.8 %copy-start.19 = (bf16[1,256,1024]{2,1,0:T(8,128)(2,1)S(1)}, bf16[1,256,1024]{2,1,0:T(8,128)(2,1)}, u32[]{:S(2)}) copy-start(bf16[1,256,1024]{2,1,0:T(8,128)(2,1)} %param.15) | copy-start | bytes 1572868
  207.2 6.8 %slice-start.3 = ((s8[6291456]{0:T(1024)(128)(4,1)}), s8[2097152]{0:T(1024)(128)(4,1)S(1)}, s32[]{:S(2)}) async-start(s8[6291456]{0:T(1024)(128)(4,1)} %bitcast.236), calls=%async_computation.3 | async-start | bytes 4194304
  218.5 8.4 %copy-start.25 = (bf16[256,3072]{1,0:T(8,128)(2,1)}, bf16[256,3072]{1,0:T(8,128)(2,1)S(1)}, u32[]{:S(2)}) copy-start(bf16[256,3072]{1,0:T(8,128)(2,1)S(1)} %get-tuple-element.73) | copy-start | bytes 4718596
  218.5 8.4 %copy-start.27 = (bf16[256,3072]{1,0:T(8,128)(2,1)}, bf16[256,3072]{1,0:T(8,128)(2,1)S(1)}, u32[]{:S(2)}) copy-start(bf16[256,3072]{1,0:T(8,128)(2,1)S(1)} %get-tuple-element.74) | copy-start | bytes 4718596
  228.0 111.2 %collective-permute-start.5 = (bf16[256,1024]{1,0:T(8,128)(2,1)}, bf16[256,1024]{1,0:T(8,128)(2,1)}, u32[]{:S(2)}, u32[]{:S(2)}) collective-permute-start(bf16[256,1024]{1,0:T(8,128)(2,1)} %fusion.60), channel_id=1, source_target_pairs={{0,4},{4,0},{8,12},{12,8},{16,20},{20,16},{24,28},{28,24},{1,5},{5... | collective-permute-start | bytes 1572872 | tf_op jit(solution)/shard_map/ppermute | solution.py:924
  234.6 105.2 %collective-permute-start.4 = (bf16[256,1024]{0,1:T(8,128)(2,1)}, bf16[256,1024]{0,1:T(8,128)(2,1)}, u32[]{:S(2)}, u32[]{:S(2)}) collective-permute-start(bf16[256,1024]{0,1:T(8,128)(2,1)} %bitcast.36), channel_id=1, source_target_pairs={{0,4},{4,0},{8,12},{12,8},{16,20},{20,16},{24,28},{28,24},{1,5},{5... | collective-permute-start | bytes 1572872 | tf_op jit(solution)/shard_map/ppermute | solution.py:924
  247.3 96.9 %collective-permute-start.2 = (bf16[256,1536]{0,1:T(8,128)(2,1)}, bf16[256,1536]{0,1:T(8,128)(2,1)}, u32[]{:S(2)}, u32[]{:S(2)}) collective-permute-start(bf16[256,1536]{0,1:T(8,128)(2,1)} %bitcast.33), channel_id=1, source_target_pairs={{0,4},{4,0},{8,12},{12,8},{16,20},{20,16},{24,28},{28,24},{1,5},{5... | collective-permute-start | bytes 2359304 | tf_op jit(solution)/shard_map/ppermute | solution.py:924
  247.3 6.8 %copy-start = (f32[256,3072]{1,0:T(8,128)S(1)}, f32[256,3072]{1,0:T(8,128)}, u32[]{:S(2)}) copy-start(f32[256,3072]{1,0:T(8,128)} %get-tuple-element.46) | copy-start | bytes 9437188
  247.3 96.9 %collective-permute-start.3 = (bf16[256,1024]{1,0:T(8,128)(2,1)}, bf16[256,1024]{1,0:T(8,128)(2,1)}, u32[]{:S(2)}, u32[]{:S(2)}) collective-permute-start(bf16[256,1024]{1,0:T(8,128)(2,1)} %bitcast.219), channel_id=1, source_target_pairs={{0,4},{4,0},{8,12},{12,8},{16,20},{20,16},{24,28},{28,24},{1,5},{5... | collective-permute-start | bytes 1572872 | tf_op jit(solution)/shard_map/ppermute | solution.py:924
  251.8 97.3 %collective-permute-start.1 = (bf16[256,6144]{1,0:T(8,128)(2,1)}, bf16[256,6144]{1,0:T(8,128)(2,1)}, u32[]{:S(2)}, u32[]{:S(2)}) collective-permute-start(bf16[256,6144]{1,0:T(8,128)(2,1)} %pad_maximum_fusion), channel_id=1, source_target_pairs={{0,4},{4,0},{8,12},{12,8},{16,20},{20,16},{24,28},{28,24},{1,5},{5... | collective-permute-start | bytes 9437192 | tf_op jit(solution)/shard_map/ppermute | solution.py:924
  251.8 49.1 %copy-start.49 = (f32[128]{0:T(128)}, f32[128]{0:T(128)S(1)}, u32[]{:S(2)}) copy-start(f32[128]{0:T(128)S(1)} %get-tuple-element.101) | copy-start | bytes 1540
  339.2 176.6 %copy-start.51 = (f32[256]{0:T(256)}, f32[256]{0:T(256)S(1)}, u32[]{:S(2)}) copy-start(f32[256]{0:T(256)S(1)} %slice_reduce_fusion) | copy-start | bytes 3076
  339.2 9.9 %collective-permute-start = (bf16[256,512]{0,1:T(8,128)(2,1)}, bf16[256,512]{0,1:T(8,128)(2,1)S(1)}, u32[]{:S(2)}, u32[]{:S(2)}) collective-permute-start(bf16[256,512]{0,1:T(8,128)(2,1)} %bitcast.228), channel_id=1, source_target_pairs={{0,4},{4,0},{8,12},{12,8},{16,20},{20,16},{24,28},{28,24},{1,5},{5... | collective-permute-start | bytes 786440 | tf_op jit(solution)/shard_map/ppermute | solution.py:924
  339.8 186.3 %collective-permute-start.6 = (bf16[256,512]{0,1:T(8,128)(2,1)}, bf16[256,512]{0,1:T(8,128)(2,1)}, u32[]{:S(2)}, u32[]{:S(2)}) collective-permute-start(bf16[256,512]{0,1:T(8,128)(2,1)} %bitcast.226), channel_id=1, source_target_pairs={{0,4},{4,0},{8,12},{12,8},{16,20},{20,16},{24,28},{28,24},{1,5},{5... | collective-permute-start | bytes 786440 | tf_op jit(solution)/shard_map/ppermute | solution.py:924
  515.8 10.3 %collective-permute-start.7 = (bf16[256,4096]{1,0:T(8,128)(2,1)}, bf16[256,4096]{1,0:T(8,128)(2,1)}, u32[]{:S(2)}, u32[]{:S(2)}) collective-permute-start(bf16[256,4096]{1,0:T(8,128)(2,1)} %pad_maximum_fusion.1), channel_id=1, source_target_pairs={{0,4},{4,0},{8,12},{12,8},{16,20},{20,16},{24,28},{28,24},{1,5},{5... | collective-permute-start | bytes 6291464 | tf_op jit(solution)/shard_map/ppermute | solution.py:924
  516.8 6.7 %copy-start.13 = (f32[256,1024]{1,0:T(8,128)S(1)}, f32[256,1024]{1,0:T(8,128)}, u32[]{:S(2)}) copy-start(f32[256,1024]{1,0:T(8,128)} %copy-done.12) | copy-start | bytes 3145732
  532.2 87.3 %copy-start.36 = (f32[64,1024]{1,0:T(8,128)S(1)}, f32[64,1024]{1,0:T(8,128)}, u32[]{:S(2)}) copy-start(f32[64,1024]{1,0:T(8,128)} %get-tuple-element.137) | copy-start | bytes 786436
  532.2 88.0 %copy-start.33 = (f32[96,1024]{1,0:T(8,128)S(1)}, f32[96,1024]{1,0:T(8,128)}, u32[]{:S(2)}) copy-start(f32[96,1024]{1,0:T(8,128)} %get-tuple-element.141) | copy-start | bytes 1179652
  (42 other events, 156.8 us)

commit v3 on v2

--- a/solution.py
+++ b/solution.py
@@ -637,6 +637,7 @@
 SLOT_AXES = ("a", "b", "core")
 CHIP_AXES = ("a", "b", "f")
 BFA, AFB, FAB, FBA = ("b", "f", "a"), ("a", "f", "b"), ("f", "a", "b"), ("f", "b", "a")
+ABF, BAF = ("a", "b", "f"), ("b", "a", "f")
 AB, BA = ("a", "b", "core"), ("b", "a", "core")
 CORE = ("core",)
 
@@ -851,6 +852,332 @@
     return flat + [normed, gains, raw, qlow, inverse]
 
 
+def sums_kernel(core, left, left_other, right, right_other, out):
+    lhs = jnp.concatenate([left[...], left_other[...]], axis=0)
+    rhs = jnp.concatenate([right[...], right_other[...]], axis=0)
+    out[...] = left_dot(lhs, rhs).astype(out.dtype)
+
+
+def chip_sums(left, left_other, right, right_other):
+    rows, width = left.shape
+    count = lax.axis_size("ctx")
+    block = width // count
+    tile = min(1024, right.shape[1])
+    if block % 128:
+        place = lax.axis_index("ctx") % 2
+        halves = [
+            lax.dynamic_index_in_dim(x.reshape(rows, count // 2, 2, block), place, 2, False)
+            for x in (left, left_other)
+        ]
+        lhs = jnp.concatenate(halves, axis=0).reshape(2 * rows, width // 2)
+        return left_dot(lhs, jnp.concatenate([right, right_other], axis=0)).astype(jnp.bfloat16)
+    core = (lax.axis_index("ctx") % 2).astype(jnp.int32)[None]
+    lhs = pl.BlockSpec((rows, block), lambda n, j, c: (0, 2 * j + c[0]))
+    rhs = pl.BlockSpec((rows, tile), lambda n, j, c: (0, n))
+    return pl.pallas_call(
+        sums_kernel,
+        grid_spec=pltpu.PrefetchScalarGridSpec(
+            num_scalar_prefetch=1,
+            grid=(right.shape[1] // tile, count // 2),
+            in_specs=[lhs, lhs, rhs, rhs],
+            out_specs=pl.BlockSpec((block, tile), lambda n, j, c: (j, n)),
+        ),
+        out_shape=jax.ShapeDtypeStruct((width // 2, right.shape[1]), jnp.bfloat16),
+        name="chip_sums",
+    )(core, left, left_other, right, right_other)
+
+
+BACK_SUMS = ("g", "u", "d", "o")
+
+
+def back_kernel(grid, plan, *refs):
+    refs = list(refs)
+
+    def take(n):
+        found = refs[:n]
+        del refs[:n]
+        return found
+
+    src = dict(zip(BACK_SUMS, take(len(BACK_SUMS))))
+    gk_ref, gv_ref, wqkv_ref = take(3)
+    dq_ref, raw_ref, cos_ref, turn_ref, gains_ref, normed_ref, tokens_ref, inv_ref, mid_ref, gain2_ref = take(10)
+    outs = dict(zip(BACK_SUMS + ("q", "k", "v"), take(len(BACK_SUMS) + 3)))
+    din_ref, gsum_ref, sums_ref, gall_ref = take(4)
+    weights, both_normed, both_raw, own_k, own_v, stage, acc, gbuf, gblock = take(9)
+    load, send, recv, misc = [Pool(x) for x in refs[-4:]]
+    del refs[-4:]
+    scratch = refs
+    grid.enter()
+    grid.barrier()
+    rows, width = tokens_ref.shape
+    lanes = width // 128
+    core = grid.at["core"]
+    chunk = 2 * HD
+    misc_sem = [misc.take(1).at[0] for _ in range(12)]
+
+    def make(source, columns, order, out, layout):
+        loads, sends, takes = Scatter.semaphores(grid, order)
+        own, *recvs = scratch[: 1 + len(order)]
+        del scratch[: 1 + len(order)]
+        return Scatter(
+            grid, order, source, columns, own, recvs,
+            load.take(loads), send.take(sends), recv.take(takes), out, layout,
+        )
+
+    def portions(group):
+        found = []
+        for name, low, high, order in group:
+            found.append(
+                make(src[name], pl.ds(low, high - low), order, outs[name].at[:, low:high], CHIP_AXES)
+            )
+        return found
+
+    slabs = [
+        make(gk_ref, pl.ds(0, KVH * HD), AB, own_k, SLOT_AXES),
+        make(gv_ref, pl.ds(0, KVH * HD), BA, own_v, SLOT_AXES),
+    ]
+    early, late = portions(plan[0]), portions(plan[1])
+    last = []
+    for name, at, low, high, order in plan[2]:
+        last.append(
+            make(sums_ref, pl.ds(at + low, high - low), order, outs[name].at[:, low:high], CHIP_AXES)
+        )
+
+    def sibling(source, dst, k):
+        return pltpu.make_async_remote_copy(
+            src_ref=source, dst_ref=dst, send_sem=misc_sem[2 * k], recv_sem=misc_sem[2 * k + 1],
+            device_id=grid.peer("core", 1 - core), device_id_type=MESH,
+        )
+
+    for p in slabs + early:
+        p.open()
+    swap_normed = sibling(normed_ref, both_normed.at[1], 0)
+    swap_normed.start()
+    both_normed[0] = normed_ref[...]
+    gblock[...] = jnp.zeros_like(gblock)
+    gblock[lanes : 2 * lanes, :] = gain2_ref[...]
+
+    def loop(count, body):
+        def once(c, carry):
+            body(c)
+            return carry
+
+        lax.fori_loop(0, count, once, 0)
+
+    def heads(source, in_at, raw_at, gain_row, c):
+        at = pl.ds(pl.multiple_of(raw_at + c * chunk, chunk), chunk)
+        grads = source[:, pl.ds(pl.multiple_of(in_at + c * chunk, chunk), chunk)]
+        raw = raw_ref[:, at]
+        gain = gains_ref[gain_row : gain_row + 1, :]
+        done = []
+        for i in range(2):
+            g = grads[:, i * HD : (i + 1) * HD]
+            g = g * cos_ref[...] - pltpu.roll(g, HD // 2, 1) * turn_ref[...]
+            one = raw[:, i * HD : (i + 1) * HD]
+            inverse = lax.rsqrt(jnp.mean(one * one, axis=-1, keepdims=True) + EPSILON)
+            unit = one * inverse
+            gblock[gain_row : gain_row + 1, :] += jnp.sum(g * unit, axis=0, keepdims=True)
+            done.append(norm_back(g, unit, inverse, gain))
+        both_raw[0, :, at] = jnp.concatenate(done, axis=1).astype(jnp.bfloat16)
+
+    loop(H // 4, functools.partial(heads, dq_ref, 0, 0, 2 * lanes))
+    for p in slabs:
+        p.step(1)
+    for p in late[: len(late) // 2]:
+        p.open()
+    half_q = H * HD // 2
+    loop(H // 4, functools.partial(heads, dq_ref, half_q, half_q, 2 * lanes))
+    q_cols, kv_cols = pl.ds(0, H * HD), pl.ds(H * HD, 2 * KVH * HD)
+    swap_q = sibling(both_raw.at[0, :, q_cols], both_raw.at[1, :, q_cols], 1)
+    swap_q.start()
+    for p in slabs:
+        p.step(0)
+    for p in late[len(late) // 2 :]:
+        p.open()
+    for p in early:
+        for level in range(p.levels() - 1, 0, -1):
+            p.step(level)
+    for p in slabs:
+        p.finish()
+    loop(KVH // 2, functools.partial(heads, own_k, 0, H * HD, 2 * lanes + 1))
+    at = (H + KVH) * HD
+    both_raw[0, :, at : at + KVH * HD] = own_v[...].astype(jnp.bfloat16)
+    swap_kv = sibling(both_raw.at[0, :, kv_cols], both_raw.at[1, :, kv_cols], 2)
+    swap_kv.start()
+    for p in late[: len(late) // 2]:
+        p.step(1)
+    swap_normed.wait()
+    swap_q.wait()
+    swap_kv.wait()
+    flat_normed = both_normed.reshape(2 * rows, width)
+    flat_raw = both_raw.reshape(2 * rows, both_raw.shape[-1])
+    count = grid.sizes["a"] * grid.sizes["b"]
+    block = width // (2 * count)
+    piece = block // grid.sizes["f"]
+    full = both_raw.shape[-1]
+    tile = 512
+
+    for j in range(count):
+        if j >= 2:
+            pltpu.make_async_copy(
+                stage.at[j % 2], sums_ref.at[(j - 2) // 2, (j - 2) % 2], misc_sem[9 + j % 2]
+            ).wait()
+        lhs = flat_normed[:, pl.ds(pl.multiple_of((2 * j + core) * block, block), block)]
+
+        def sums(c):
+            cols = pl.ds(pl.multiple_of(c * tile, tile), tile)
+            value = left_dot(lhs, flat_raw[:, cols]).astype(jnp.bfloat16)
+            stage[j % 2, :, :, cols] = value.reshape(grid.sizes["f"], piece, tile)
+
+        loop(full // tile, sums)
+        pltpu.make_async_copy(stage.at[j % 2], sums_ref.at[j // 2, j % 2], misc_sem[9 + j % 2]).start()
+    for j in range(count - 2, count):
+        pltpu.make_async_copy(stage.at[j % 2], sums_ref.at[j // 2, j % 2], misc_sem[9 + j % 2]).wait()
+    for p in last:
+        p.open()
+    for p in late[len(late) // 2 :]:
+        p.step(1)
+    tiles = [
+        pltpu.make_async_copy(
+            wqkv_ref.at[:, c * tile : (c + 1) * tile], weights.at[c % 2], misc_sem[6 + c % 2]
+        )
+        for c in range(full // tile)
+    ]
+    tiles[0].start()
+    for c in range(full // tile):
+        if c + 1 < full // tile:
+            tiles[c + 1].start()
+        tiles[c].wait()
+        value = right_dot(both_raw[0, :, c * tile : (c + 1) * tile], weights[c % 2])
+        acc[...] = value if c == 0 else acc[...] + value
+    inverse = inv_ref[...]
+    for j in range(lanes):
+        cols = slice(j * 128, (j + 1) * 128)
+        normal = tokens_ref[:, cols].astype(jnp.float32) * inverse
+        gblock[j : j + 1, :] = jnp.sum(acc[:, cols] * normal, axis=0, keepdims=True)
+    copy = pltpu.make_async_copy(gblock, gbuf, misc_sem[11])
+    copy.start()
+    copy.wait()
+    order = FAB + CORE
+    sends, takes = Gather.semaphores(grid, order)
+    spread = Gather(
+        grid, order, gbuf, gall_ref, slice(None), send.take(sends), recv.take(takes), ALL_AXES
+    )
+    spread.open()
+    mine = tuple(grid.at[x] for x in ALL_AXES)
+    gall_ref[mine] = gblock[...]
+    for p in early + late:
+        p.step(0)
+    for p in last:
+        p.step(1)
+    spread.first()
+    dots = jnp.zeros((rows, 1), jnp.float32)
+    for j in range(lanes):
+        cols = slice(j * 128, (j + 1) * 128)
+        normal = tokens_ref[:, cols].astype(jnp.float32) * inverse
+        dots += jnp.sum(acc[:, cols] * gains_ref[j : j + 1, :] * normal, axis=1, keepdims=True)
+    dots = dots / width
+    for j in range(lanes):
+        cols = slice(j * 128, (j + 1) * 128)
+        normal = tokens_ref[:, cols].astype(jnp.float32) * inverse
+        grad = inverse * (acc[:, cols] * gains_ref[j : j + 1, :] - normal * dots)
+        din_ref[:, cols] = (mid_ref[:, cols] + grad).astype(jnp.bfloat16)
+    spread.arrivals(1)
+    for p in early + late:
+        p.finish()
+    for p in last:
+        p.step(0)
+    spread.arrivals(2)
+    spread.arrivals(3)
+    places = math.prod(grid.sizes[x] for x in ALL_AXES)
+    gsum_ref[...] = jnp.sum(gall_ref.reshape((places,) + gblock.shape)[...], axis=0)
+    for p in last:
+        p.finish()
+    for p in slabs + early + late + last:
+        p.close()
+    spread.close()
+
+
+def back_scratch(grid, plan, pieces, rows, width):
+    low = jnp.bfloat16
+    scratch, counts = [], []
+    for order in (AB, BA):
+        scratch += Scatter.scratch(grid, order, rows, KVH * HD, low)
+        counts.append(Scatter.semaphores(grid, order))
+    for name, begin, end, order in plan[0] + plan[1] + tuple((p[0],) + p[2:] for p in plan[2]):
+        scratch += Scatter.scratch(grid, order, pieces[name], end - begin, low)
+        counts.append(Scatter.semaphores(grid, order))
+    return scratch, [sum(x) for x in zip(*counts)]
+
+
+def back_fits(grid, plan, rows, width, hidden, total):
+    pieces = {name: width // total for name in ("g", "u", "q", "k", "v")}
+    pieces.update({"d": hidden // total, "o": H * HD // total})
+    scratch = back_scratch(grid, plan, pieces, rows, width)[0]
+    taken = sum(2 * math.prod(x.shape) for x in scratch)
+    held = 2 * rows * (11 * width + 3 * (H + 2 * KVH) * HD + 4 * (H + KVH) * HD) + 6 * 2**20
+    return taken + held < 62 * 2**20
+
+
+def back(grid, plan, sums, gk, gv, wqkv, dq, raw, cosine, turned, gains, normed, tokens, inverse, middle, gain2):
+    low, f32 = jnp.bfloat16, jnp.float32
+    rows, width = tokens.shape
+    chips = tuple(grid.sizes[x] for x in CHIP_AXES)
+    places = tuple(grid.sizes[x] for x in ALL_AXES)
+    slots = tuple(grid.sizes[x] for x in SLOT_AXES)
+    blocks = [x.reshape(chips + (x.shape[0] // math.prod(chips), x.shape[1])) for x in sums]
+    shape = jax.ShapeDtypeStruct
+    vmem = pl.BlockSpec(memory_space=pltpu.VMEM)
+    piece = width // math.prod(places)
+    pieces = dict(zip(BACK_SUMS, [x.shape[-2] for x in blocks]))
+    pieces.update({"q": piece, "k": piece, "v": piece})
+    scratch, (loads, sends, takes) = back_scratch(grid, plan, pieces, rows, width)
+    more = Gather.semaphores(grid, FAB + CORE)
+    full = wqkv.shape[1]
+    count = grid.sizes["a"] * grid.sizes["b"]
+    outs = pl.pallas_call(
+        functools.partial(back_kernel, grid, plan),
+        out_shape=[shape(x.shape[-2:], f32) for x in blocks]
+        + [shape((piece, n), f32) for n in (H * HD, KVH * HD, KVH * HD)]
+        + [
+            shape((rows, width), low),
+            shape(gains.shape, f32),
+            shape(chips + (piece, full), low),
+        ],
+        in_specs=[ANY] * (len(blocks) + 3) + [vmem] * 10,
+        out_specs=[vmem] * (len(blocks) + 5) + [ANY],
+        scratch_shapes=[
+            pltpu.VMEM(places + gains.shape, f32),
+            pltpu.VMEM((2, width, 512), low),
+            pltpu.VMEM((2, rows, width), low),
+            pltpu.VMEM((2, rows, full), low),
+            pltpu.VMEM((rows, KVH * HD), f32),
+            pltpu.VMEM((rows, KVH * HD), f32),
+            pltpu.VMEM((2, grid.sizes["f"], piece, full), low),
+            pltpu.VMEM((rows, width), f32),
+            pltpu.VMEM(gains.shape, f32),
+            pltpu.VMEM(gains.shape, f32),
+        ]
+        + scratch
+        + [
+            pltpu.SemaphoreType.DMA((loads,)),
+            pltpu.SemaphoreType.DMA((sends + more[0],)),
+            pltpu.SemaphoreType.DMA((takes + more[1],)),
+            pltpu.SemaphoreType.DMA((12,)),
+        ],
+        compiler_params=pltpu.CompilerParams(
+            has_side_effects=True, vmem_limit_bytes=63 * 2**20, collective_id=1
+        ),
+        name="back",
+    )(
+        *blocks,
+        gk.reshape(slots + (rows, KVH * HD)),
+        gv.reshape(slots + (rows, KVH * HD)),
+        wqkv, dq, raw, cosine, turned, gains, normed, tokens, inverse, middle, gain2,
+    )
+    return outs
+
+
 def scatter_kernel(grid, portions, layouts, n, *refs):
     srcs, outs, scratch = refs[:n], refs[n : 2 * n], list(refs[2 * n : -3])
     load, send, recv = [Pool(x) for x in refs[-3:]]
@@ -922,16 +1249,6 @@
 def swapped(x):
     count = lax.axis_size("ctx")
     return lax.ppermute(x, "ctx", [(i, i ^ 1) for i in range(count)])
-
-
-def chip_sums(left, right, right_other):
-    core = lax.axis_index("ctx") % 2
-    rows, width = left.shape
-    split = left.reshape(rows, lax.axis_size("ctx") // 2, 2, -1)
-    mine = lax.dynamic_index_in_dim(split, core, 2, False).reshape(rows, width // 2)
-    theirs = lax.dynamic_index_in_dim(split, 1 - core, 2, False).reshape(rows, width // 2)
-    both = jnp.concatenate([mine, swapped(theirs)], axis=0)
-    return left_dot(both, jnp.concatenate([right, right_other], axis=0)).astype(jnp.bfloat16)
 
 
 def on_device(
@@ -1018,6 +1335,7 @@
     lanes = width // 128
     gain_one, gain_two = gains[:lanes].reshape(-1), gains[lanes : 2 * lanes].reshape(-1)
     query_scale, key_scale = gains[2 * lanes], gains[2 * lanes + 1]
+    inverse_rows = inverse_one
     inverse_one = inverse_one[:, :1]
     inputs = tokens.reshape(rows, width).astype(jnp.float32)
     normal_one = inputs * inverse_one
@@ -1046,14 +1364,16 @@
     grad_gate = (grad_hidden * upper * sigmoid_gate * (1.0 + gate * (1.0 - sigmoid_gate))).astype(low)
     grad_upper = (grad_hidden * activated).astype(low)
     grad_both = jnp.concatenate([grad_gate, grad_upper], axis=1)
-    grad_down = chip_sums(hidden, upstream, swapped(upstream))
-    grad_gu = chip_sums(normed_two, grad_both, swapped(grad_both))
+    normed_other, upstream_other = swapped(normed_two), swapped(upstream)
+    grad_down = chip_sums(hidden, swapped(hidden), upstream, upstream_other)
+    grad_g = chip_sums(normed_two, normed_other, grad_gate, swapped(grad_gate))
+    grad_u = chip_sums(normed_two, normed_other, grad_upper, swapped(grad_upper))
     grad_normed_two = right_dot(grad_both, full_gu)
     grad_gain_two = jnp.sum(grad_normed_two * normal_two, axis=0)
     grad_middle = upstream.astype(jnp.float32) + norm_back(grad_normed_two, normal_two, inverse_two, gain_two)
     f32 = jnp.float32
     branch_grad = grad_middle.astype(low)
-    grad_woutput = chip_sums(attended_low, branch_grad, swapped(branch_grad))
+    grad_woutput = chip_sums(attended_low, swapped(attended_low), branch_grad, swapped(branch_grad))
     grad_attended = right_dot(branch_grad, full_output).reshape(rows, H, HD)
     grad_summed = (grad_attended / row_totals).astype(low).reshape(rows, H * HD)
     drift = jnp.sum(grad_attended * attended.reshape(rows, H, HD), axis=-1) / row_totals[..., 0]
@@ -1061,25 +1381,80 @@
     grad_query, grad_keys, grad_values = attention_back(
         table, pairs, query_low, key_all, value_all, grad_summed, drift
     )
+    back_plan = (
+        (("d", 0, width // 2, ABF), ("d", width // 2, width, BAF)),
+        (
+            ("g", 0, hidden_width, FAB),
+            ("u", 0, hidden_width, FBA),
+            ("o", 0, width // 2, FAB),
+            ("o", width // 2, width, FBA),
+        ),
+        (
+            ("q", 0, 0, half_q, FAB),
+            ("q", 0, half_q, 2 * half_q, FBA),
+            ("k", H * HD, 0, 2 * half_k, BFA),
+            ("v", (H + KVH) * HD, 0, 2 * half_k, AFB),
+        ),
+    )
+    if back_fits(grid, back_plan, rows, width, hidden_width, total):
+        out_g, out_u, out_down, out_output, out_q, out_k, out_v, grad_tokens, gain_sums, _ = back(
+            grid,
+            back_plan,
+            (grad_g, grad_u, grad_down, grad_woutput),
+            grad_keys,
+            grad_values,
+            full_qkv,
+            grad_query,
+            raw,
+            cosine.reshape(rows, HD),
+            turned,
+            gains,
+            normed,
+            tokens.reshape(rows, width),
+            inverse_rows,
+            grad_middle,
+            grad_gain_two.reshape(lanes, 128),
+        )
+        flat_sums = gain_sums.reshape(-1)
+
+        def own_piece(at, x):
+            return lax.dynamic_slice_in_dim(flat_sums, at + device * x.shape[0], x.shape[0], 0)
+
+        return (
+            output,
+            grad_tokens.reshape(groups, rows, width),
+            own_piece(0, attn_gain),
+            out_q,
+            out_k,
+            out_v,
+            own_piece(2 * width, query_gain),
+            own_piece(2 * width + HD, key_gain),
+            out_output,
+            own_piece(width, mlp_gain),
+            out_g,
+            out_u,
+            out_down,
+        )
     f32 = jnp.float32
-    own_keys, own_values, out_gu, out_down, out_output = scatter(
+    own_keys, own_values, out_g, out_u, out_down, out_output = scatter(
         grid,
-        [SLOT_AXES] * 2 + [CHIP_AXES] * 3,
+        [SLOT_AXES] * 2 + [CHIP_AXES] * 4,
         [
             (0, 0, KVH * HD, AB),
             (1, 0, KVH * HD, BA),
             (2, 0, hidden_width, BFA),
-            (2, hidden_width, 2 * hidden_width, AFB),
-            (3, 0, width // 2, BFA),
-            (3, width // 2, width, AFB),
+            (3, 0, hidden_width, AFB),
             (4, 0, width // 2, BFA),
             (4, width // 2, width, AFB),
+            (5, 0, width // 2, BFA),
+            (5, width // 2, width, AFB),
         ],
         "scatter_mlp",
-        (f32, low, f32, f32, f32),
+        (f32, low, f32, f32, f32, f32),
         grad_keys,
         grad_values,
-        grad_gu,
+        grad_g,
+        grad_u,
         grad_down,
         grad_woutput,
     )
@@ -1099,7 +1474,7 @@
         ],
         axis=1,
     )
-    grad_wqkv = chip_sums(normed, grad_raw, swapped(grad_raw))
+    grad_wqkv = chip_sums(normed, swapped(normed), grad_raw, swapped(grad_raw))
     grad_normed = right_dot(grad_raw, full_qkv)
     grad_gain_one = jnp.sum(grad_normed * normal_one, axis=0)
     grad_inputs = grad_middle + norm_back(grad_normed, normal_one, inverse_one, gain_one)
@@ -1129,8 +1504,8 @@
         out_gains[2, : key_gain.shape[0]],
         out_output,
         out_gains[3, : mlp_gain.shape[0]],
-        out_gu[:, :hidden_width],
-        out_gu[:, hidden_width:],
+        out_g,
+        out_u,
         out_down,
     )
 

time: 631 us -> 559 us (0.89); the launches traced: 621 us -> 557 us
  local copies, waits for them, and re-layouts: 78.7 us -> 25 us
  Pallas kernels: 445 us -> 486 us
  matrix products: 65.8 us -> 34.7 us
  other arithmetic: 26.4 us -> 6.95 us
    pallas_call x2 -> x5, Pallas kernels: 225 us -> 266 us  [the longest x1 235 us: back(): pl.pallas_call(functools.partial(back_kernel, grid, plan), out_shape=[sha...]
    dot_general x4 -> x0, matrix products: 31.1 us -> none  [left_dot(): lax.dot_general(left, right, (((0,), (0,)), ((), ())), preferred_element_...]
    unnamed x134 -> x33, local copies, waits for them, and re-layouts: 32.2 us -> 12.5 us
    reshape x8 -> x0, local copies, waits for them, and re-layouts: 11.2 us -> none  [the longest x4 9.62 us: chip_sums(): split = left.reshape(rows, lax.axis_size('ctx') // 2, 2, -1)]
    reduce_sum x8 -> x0, other arithmetic: 10.4 us -> none  [the longest x2 5.1 us: on_device(): grad_qscale = jnp.sum(grad_qnormed * query_unit, axis=(0, 1))]
    dynamic_slice x4 -> x2, local copies, waits for them, and re-layouts: 12.9 us -> 2.62 us  [own_piece(): lax.dynamic_slice_in_dim(flat_sums, at + device * x.shape[0], x.shape[0], 0)]
    slice x4 -> x0, local copies, waits for them, and re-layouts: 6.56 us -> none  [the longest x1 2.2 us: on_device(): out_gu[:, hidden_width:]]
    dot_general x4 -> x3, matrix products: 21.6 us -> 18.3 us  [right_dot(): lax.dot_general(left, right, (((1,), (1,)), ((), ())), preferred_element_...]
  transfers between devices with their start and end apart: 8 -> 7, of which waited for: 0 -> 0; matrix products, arithmetic and copies ran while one was open for 19% -> 8% of each run, Pallas kernels for 28% -> 10%
where the time goes in v3:
time: 559 us; the launch traced here: 557 us
  Pallas kernels  486 us (87%)
  matrix products  34.7 us (6%)
  local copies, waits for them, and re-layouts  25 us (4%)
  other arithmetic  6.95 us (1%)
    pallas_call x1, Pallas kernels, back(): pl.pallas_call(functools.partial(back_kernel, grid, plan), out_shape=[sha...  235 us
    pallas_call x1, Pallas kernels, front(): pl.pallas_call(functools.partial(front_kernel, grid, plan), out_shape=[sh...  179 us
    pallas_call x4, Pallas kernels, chip_sums(): pl.pallas_call(sums_kernel, grid_spec=pltpu.PrefetchScalarGridSpec(num_sc...  31.2 us
    pallas_call x1, Pallas kernels, attention_back(): pl.pallas_call(functools.partial(attention_back_kernel, pairs), grid_spec...  28 us
    dot_general x3, matrix products, right_dot(): lax.dot_general(left, right, (((1,), (1,)), ((), ())), preferred_element_...  18.3 us
    dot_general x3, matrix products, plain_dot(): return jnp.dot(left, right, preferred_element_type=jnp.float32)  16.4 us
    pallas_call x1, Pallas kernels, attention(): pl.pallas_call(functools.partial(attention_kernel, pairs), grid_spec=pltp...  12.6 us
    unnamed x33, local copies, waits for them, and re-layouts  12.5 us
  transfers between devices with their start and end apart: 7, of which 0 were waited for; matrix products, arithmetic and copies ran while one was open for 8% of the time, Pallas kernels for 10%

profile of v3, /device:TPU:0, one launch (start us, length us, event | category | flops | bytes accessed | tf_op | source)
XLA Modules:
  0.0 556.7 jit_solution(17159095445691769201)
XLA Ops:
  10.8 179.1 %front.1 = (bf16[2,2,2,4,32,4096]{5,4,3,2,1,0:T(8,128)(2,1)}, bf16[2,2,2,4,64,1024]{5,4,3,2,1,0:T(8,128)(2,1)}, bf16[2,2,2,4,32,6144]{5,4,3,2,1,0:T(8,128)(2,1)}...) custom-call(bf16[32,2048]{1,0:T(8,128)(2,1)} %refs_0_.1, ...), custom_call_target="tpu_custom_call" | custom-call | tf_op jit(solution)/shard_map/front/pallas_call | solution.py:816
  189.8 12.6 %attention.1 = (f32[256,2048]{1,0:T(8,128)}, bf16[256,2048]{1,0:T(8,128)(2,1)}, f32[8,2,256]{2,1,0:T(2,128)}) custom-call(s32[18]{0:T(128)} %pad_add_fusion.table, bf16[256,2048]{1,0:T(8,128)(2,1)} %get-tuple-element.39.q_ref, bf16[2048,1024]{1,0:T(8,128)(2,1)} %bitcast.76, bf16[2048,1024]{1,0:T(8,128)(2,1)} %bitcast.78), custom_call_target="tpu_custom_call" | custom-call | tf_op jit(solution)/shard_map/attention/pallas_call | solution.py:550
  203.1 3.9 multiply_reduce_fusion.3
  207.9 6.7 %fusion.17 = f32[256,6144]{1,0:T(8,128)S(1)} fusion(bf16[256,1024]{1,0:T(8,128)(2,1)S(1)} %multiply_convert_fusion.3.left, bf16[1024,6144]{1,0:T(8,128)(2,1)} %bitcast.80), kind=kOutput, calls=%fused_computation.47 | convolution fusion | flops 3221225472 | bytes 19398656 | tf_op jit(solution)/shard_map/dot_general | solution.py:57
  214.7 4.9 multiply_convert_fusion
  220.1 8.1 %multiply_reduce_fusion.1 = (f32[1024]{0:T(1024)}, f32[256]{0:T(256)S(1)}, f32[256,1024]{1,0:T(8,128)S(1)}) fusion(f32[256,1024]{1,0:T(8,128)S(1)} %get-tuple-element.86, f32[256]{0:T(256)S(1)} %add_rsqrt_fusion, f32[1024]{0:T(1024)S(1)} %slice_bitcast_fusion, bf16[1024,6144]{1,0:T(8,128)(2,1)} %bitcast.81, bf16[256,3072]{1,0:T(8,128)(2,1)} %get-tuple-element.71.right, ...), kind=kOutput, calls=%fused_computation.16 | convolution fusion | flops 3229088512 | bytes 17836032 | tf_op jit(solution)/shard_map/dot_general | solution.py:51
  228.2 1.3 fusion.13
  230.1 2.9 copy.40
  233.0 5.2 multiply_reduce_fusion
  238.2 2.3 copy.39.g_ref
  241.2 28.0 %attention_back.1 = (f32[256,2048]{1,0:T(8,128)}, bf16[2048,1024]{1,0:T(8,128)(2,1)}, bf16[2048,1024]{1,0:T(8,128)(2,1)}) custom-call(s32[18]{0:T(128)} %pad_add_fusion.table, bf16[256,2048]{1,0:T(8,128)(2,1)} %get-tuple-element.39.q_ref, bf16[2048,1024]{1,0:T(8,128)(2,1)} %bitcast.77, bf16[2048,1024]{1,0:T(8,128)(2,1)} %bitcast.79, ...), custom_call_target="tpu_custom_call" | custom-call | tf_op jit(solution)/shard_map/attention_back/pallas_call | solution.py:612
  269.8 5.9 %fusion.6 = bf16[1,256,1024]{2,1,0:T(8,128)(2,1)} fusion(f32[256,1024]{1,0:T(8,128)S(1)} %get-tuple-element.86, bf16[256,3072]{1,0:T(8,128)(2,1)} %get-tuple-element.73.left, bf16[3072,1024]{1,0:T(8,128)(2,1)} %bitcast.102), kind=kOutput, calls=%fused_computation.15 | convolution fusion | flops 1611137024 | bytes 9437184 | tf_op jit(solution)/shard_map/dot_general | solution.py:57
  275.7 4.9 chip_sums.7
  281.4 10.4 %chip_sums.5 = bf16[512,3072]{1,0:T(8,128)(2,1)} custom-call(s32[1]{0:T(128)} %bitcast.14.core, bf16[256,1024]{1,0:T(8,128)(2,1)} %copy-done, bf16[256,1024]{1,0:T(8,128)(2,1)} %copy-done.4, bf16[256,3072]{1,0:T(8,128)(2,1)} %get-tuple-element.71.right, bf16[256,3072]{1,0:T(8,128)(2,1)} %collective-permute-done.2.right_other), custom_call_target="tpu_custom_call" | custom-call | tf_op jit(solution)/shard_map/chip_sums/pallas_call | solution.py:877
  291.8 10.4 %chip_sums.4 = bf16[512,3072]{1,0:T(8,128)(2,1)} custom-call(s32[1]{0:T(128)} %bitcast.14.core, bf16[256,1024]{1,0:T(8,128)(2,1)} %copy-done, bf16[256,1024]{1,0:T(8,128)(2,1)} %copy-done.4, bf16[256,3072]{1,0:T(8,128)(2,1)} %get-tuple-element.72.right, bf16[256,3072]{1,0:T(8,128)(2,1)} %collective-permute-done.1.right_other), custom_call_target="tpu_custom_call" | custom-call | tf_op jit(solution)/shard_map/chip_sums/pallas_call | solution.py:877
  302.2 5.6 chip_sums.6
  307.8 234.7 %back.1 = (f32[32,3072]{1,0:T(8,128)}, f32[32,3072]{1,0:T(8,128)}, f32[96,1024]{1,0:T(8,128)}, f32[64,1024]{1,0:T(8,128)}, f32[32,2048]{1,0:T(8,128)}, /*index=5...) custom-call(bf16[2,2,4,32,3072]{4,3,2,1,0:T(8,128)(2,1)} %bitcast.83, ...), custom_call_target="tpu_custom_call" | custom-call | tf_op jit(solution)/shard_map/back/pallas_call | solution.py:1138
  542.4 1.3 fusion.15
  545.1 1.9 copy.56
  546.9 1.7 copy.57
  548.6 1.6 copy.58
  550.2 1.6 copy.59
  551.7 1.7 copy.60
  553.4 1.8 copy.61
  (63 shorter events, 16.2 us)
Async XLA Ops:
  8.7 2.1 copy-start.9
  189.8 13.3 %copy-start.1 = (bf16[1,256,1024]{2,1,0:T(8,128)(2,1)S(1)}, bf16[1,256,1024]{2,1,0:T(8,128)(2,1)}, u32[]{:S(2)}) copy-start(bf16[1,256,1024]{2,1,0:T(8,128)(2,1)} %param.14) | copy-start | bytes 1572868
  202.5 67.0 %collective-permute-start.5 = (bf16[256,2048]{1,0:T(8,128)(2,1)}, bf16[256,2048]{1,0:T(8,128)(2,1)}, u32[]{:S(2)}, u32[]{:S(2)}) collective-permute-start(bf16[256,2048]{1,0:T(8,128)(2,1)} %get-tuple-element.42.left), channel_id=1, source_target_pairs={{0,4},{4,0},{8,12},{12,8},{16,20},{20,16},{24,28},{28,24},{1,5},{5... | collective-permute-start | bytes 3145736 | tf_op jit(solution)/shard_map/ppermute | solution.py:1251
  207.7 6.9 %slice-start = ((s8[6291456]{0:T(1024)(128)(4,1)}), s8[4194304]{0:T(1024)(128)(4,1)S(1)}, s32[]{:S(2)}) async-start(s8[6291456]{0:T(1024)(128)(4,1)} %bitcast.103), calls=%async_computation | async-start | bytes 8388608
  207.9 61.3 %copy-start = (bf16[256,1024]{1,0:T(8,128)(2,1)}, bf16[256,1024]{1,0:T(8,128)(2,1)S(1)}, u32[]{:S(2)}) copy-start(bf16[256,1024]{1,0:T(8,128)(2,1)S(1)} %multiply_convert_fusion.3.left) | copy-start | bytes 1572868
  207.9 6.8 %copy-start.2 = (bf16[1,256,1024]{2,1,0:T(8,128)(2,1)S(1)}, bf16[1,256,1024]{2,1,0:T(8,128)(2,1)}, u32[]{:S(2)}) copy-start(bf16[1,256,1024]{2,1,0:T(8,128)(2,1)} %param.15) | copy-start | bytes 1572868
  207.9 6.8 %slice-start.1 = ((s8[6291456]{0:T(1024)(128)(4,1)}), s8[2097152]{0:T(1024)(128)(4,1)S(1)}, s32[]{:S(2)}) async-start(s8[6291456]{0:T(1024)(128)(4,1)} %bitcast.103), calls=%async_computation.1 | async-start | bytes 4194304
  219.6 82.6 %collective-permute-start.3 = (bf16[256,3072]{1,0:T(8,128)(2,1)}, bf16[256,3072]{1,0:T(8,128)(2,1)}, u32[]{:S(2)}, u32[]{:S(2)}) collective-permute-start(bf16[256,3072]{1,0:T(8,128)(2,1)} %get-tuple-element.73.left), channel_id=1, source_target_pairs={{0,4},{4,0},{8,12},{12,8},{16,20},{20,16},{24,28},{28,24},{1,5},{5... | collective-permute-start | bytes 4718600 | tf_op jit(solution)/shard_map/ppermute | solution.py:1251
  219.6 61.0 %collective-permute-start.2 = (bf16[256,3072]{1,0:T(8,128)(2,1)}, bf16[256,3072]{1,0:T(8,128)(2,1)}, u32[]{:S(2)}, u32[]{:S(2)}) collective-permute-start(bf16[256,3072]{1,0:T(8,128)(2,1)} %get-tuple-element.71.right), channel_id=1, source_target_pairs={{0,4},{4,0},{8,12},{12,8},{16,20},{20,16},{24,28},{28,24},{1,5},{5... | collective-permute-start | bytes 4718600 | tf_op jit(solution)/shard_map/ppermute | solution.py:1251
  220.1 71.7 %collective-permute-start.1 = (bf16[256,3072]{1,0:T(8,128)(2,1)}, bf16[256,3072]{1,0:T(8,128)(2,1)}, u32[]{:S(2)}, u32[]{:S(2)}) collective-permute-start(bf16[256,3072]{1,0:T(8,128)(2,1)} %get-tuple-element.72.right), channel_id=1, source_target_pairs={{0,4},{4,0},{8,12},{12,8},{16,20},{20,16},{24,28},{28,24},{1,5},{5... | collective-permute-start | bytes 4718600 | tf_op jit(solution)/shard_map/ppermute | solution.py:1251
  229.6 8.6 %copy-start.3 = (bf16[256,1024]{1,0:T(8,128)(2,1)}, bf16[256,1024]{1,0:T(8,128)(2,1)S(1)}, u32[]{:S(2)}) copy-start(bf16[256,1024]{1,0:T(8,128)(2,1)S(1)} %get-tuple-element.67.right) | copy-start | bytes 1572868
  229.6 3.4 copy-start.8
  229.6 39.6 %collective-permute-start.6 = (bf16[256,1024]{1,0:T(8,128)(2,1)S(1)}, bf16[256,1024]{1,0:T(8,128)(2,1)S(1)}, u32[]{:S(2)}, u32[]{:S(2)}) collective-permute-start(bf16[256,1024]{1,0:T(8,128)(2,1)S(1)} %get-tuple-element.67.right), channel_id=1, source_target_pairs={{0,4},{4,0},{8,12},{12,8},{16,20},{20,16},{24,28},{28,24},{1,5},{5... | collective-permute-start | bytes 1572872 | tf_op jit(solution)/shard_map/ppermute | solution.py:1251
  269.2 6.4 %copy-start.5 = (bf16[256,1024]{1,0:T(8,128)(2,1)}, bf16[256,1024]{1,0:T(8,128)(2,1)S(1)}, u32[]{:S(2)}) copy-start(bf16[256,1024]{1,0:T(8,128)(2,1)S(1)} %collective-permute-done.6.right_other) | copy-start | bytes 1572868
  269.2 11.3 %collective-permute-start = (bf16[256,1024]{1,0:T(8,128)(2,1)S(1)}, bf16[256,1024]{1,0:T(8,128)(2,1)S(1)}, u32[]{:S(2)}, u32[]{:S(2)}) collective-permute-start(bf16[256,1024]{1,0:T(8,128)(2,1)S(1)} %multiply_convert_fusion.3.left), channel_id=1, source_target_pairs={{0,4},{4,0},{8,12},{12,8},{16,20},{20,16},{24,28},{28,24},{1,5},{5... | collective-permute-start | bytes 1572872 | tf_op jit(solution)/shard_map/ppermute | solution.py:1251
  269.5 32.7 %collective-permute-start.4 = (bf16[256,1024]{1,0:T(8,128)(2,1)S(1)}, bf16[256,1024]{1,0:T(8,128)(2,1)}, u32[]{:S(2)}, u32[]{:S(2)}) collective-permute-start(bf16[256,1024]{1,0:T(8,128)(2,1)S(1)} %bitcast.92), channel_id=1, source_target_pairs={{0,4},{4,0},{8,12},{12,8},{16,20},{20,16},{24,28},{28,24},{1,5},{5... | collective-permute-start | bytes 1572872 | tf_op jit(solution)/shard_map/ppermute | solution.py:1251
  280.5 0.8 copy-start.4
  542.4 12.8 %copy-start.7 = (f32[32,3072]{1,0:T(8,128)S(1)}, f32[32,3072]{1,0:T(8,128)}, u32[]{:S(2)}) copy-start(f32[32,3072]{1,0:T(8,128)} %get-tuple-element.114) | copy-start | bytes 1179652
  542.4 13.5 %copy-start.6 = (f32[96,1024]{1,0:T(8,128)S(1)}, f32[96,1024]{1,0:T(8,128)}, u32[]{:S(2)}) copy-start(f32[96,1024]{1,0:T(8,128)} %get-tuple-element.115) | copy-start | bytes 1179652

commit v4 on v3

--- a/solution.py
+++ b/solution.py
@@ -1,4 +1,5 @@
 import functools
+import itertools
 import math
 
 import jax
@@ -81,7 +82,7 @@
         count = 0
         for axis in ("core", "b", "a", "f"):
             n, p = self.sizes[axis], self.at[axis]
-            for step in (1,) if n == 2 else (1, n - 1):
+            for step in range(1, n):
                 pl.semaphore_signal(
                     sem, inc=1, device_id=self.peer(axis, lax.rem(p + step, n)), device_id_type=MESH
                 )
@@ -121,7 +122,7 @@
             return [(None, 1 - p)]
         return [(p + 1 < n, p + 1), (p >= 1, p - 1)]
 
-    def nearest(self, axis):
+    def spread(self, axis):
         n, p = self.sizes[axis], self.at[axis]
         if n == 2:
             return [p, 1 - p]
@@ -131,6 +132,13 @@
                 if way not in order:
                     order.append(way)
         return [lax.rem(p + s, n) for s in order]
+
+    def others(self, axis):
+        n, p = self.sizes[axis], self.at[axis]
+        return [1 - p] if n == 2 else [lax.rem(p + step, n) for step in range(1, n)]
+
+    def nearest(self, axis):
+        return [self.at[axis]] + self.others(axis)
 
 
 class Pool:
@@ -240,7 +248,7 @@
         axis = self.order[level]
         inner = [{}]
         for x in self.order[1:level]:
-            inner = [{**places, x: j} for places in inner for j in self.grid.nearest(x)]
+            inner = [{**places, x: j} for places in inner for j in self.grid.spread(x)]
         fixed = {x: self.grid.at[x] for x in self.order[level + 1 :]}
         for places in inner:
             for cond, origin, onward, more in self.grid.sources(axis):
@@ -257,7 +265,7 @@
             guarded(cond, lambda: make().wait_send())
 
 
-def add_into(total, term, out=None):
+def add_into(total, terms, out=None):
     shape = total.shape
     rows = min(16, shape[-2])
     steps = shape[-2] // rows
@@ -271,7 +279,7 @@
             rest = rest // n
         at = index + (pl.ds(pl.multiple_of(lax.rem(i, steps) * rows, rows), rows), slice(None))
         value = total[at].astype(jnp.float32)
-        if term is not None:
+        for term in terms:
             value = value + term[at].astype(jnp.float32)
         if out is None:
             total[at] = value.astype(total.dtype)
@@ -288,17 +296,13 @@
         self.own, self.recvs, self.out = own, recvs, out
         self.load_sem, self.send_sem, self.recv_sem = load_sem, send_sem, recv_sem
         self.layout_axes = layout_axes
-        self.sends = 0
         self.pending = []
         self.base = {}
+        self.top = len(order) - 1
         number = 0
-        for level in range(len(order) - 1, -1, -1):
+        for level in range(self.top, -1, -1):
             self.base[level] = number
             number += self.slots(grid, order, level)
-
-    @staticmethod
-    def kept(grid, order):
-        return order[1:-1] if grid.sizes[order[-1]] == 2 else order[1:]
 
     @staticmethod
     def inner(grid, order, level):
@@ -306,46 +310,35 @@
 
     @staticmethod
     def slots(grid, order, level):
-        n = grid.sizes[order[level]]
-        lines = 1 if n == 2 else n + 1
-        return lines * math.prod(Scatter.inner(grid, order, level))
+        return (grid.sizes[order[level]] - 1) * math.prod(Scatter.inner(grid, order, level))
 
     @staticmethod
     def scratch(grid, order, rows, columns, dtype):
         n1 = grid.sizes[order[0]]
-        own = tuple(grid.sizes[x] for x in Scatter.kept(grid, order)) + (n1, rows, columns)
-        recvs = []
-        for level in range(len(order)):
-            n = grid.sizes[order[level]]
-            lead = () if n == 2 else (n + 1,)
+        shapes = [tuple(grid.sizes[x] for x in order[1:-1]) + (n1, rows, columns)]
+        for level, axis in enumerate(order):
             block = (rows, columns) if level == 0 else (n1, rows, columns)
-            recvs.append(lead + tuple(Scatter.inner(grid, order, level)) + block)
-        return [pltpu.VMEM(s, dtype) for s in [own] + recvs]
+            shapes.append((grid.sizes[axis] - 1,) + tuple(Scatter.inner(grid, order, level)) + block)
+        return [pltpu.VMEM(x, dtype) for x in shapes]
 
     @staticmethod
     def semaphores(grid, order):
-        loads = math.prod(grid.sizes[x] for x in Scatter.kept(grid, order))
-        slots = [Scatter.slots(grid, order, level) for level in range(len(order))]
-        sends = [
-            (1 if grid.sizes[x] == 2 else 2 * (grid.sizes[x] - 1))
-            * math.prod(Scatter.inner(grid, order, level))
-            for level, x in enumerate(order)
-        ]
-        return loads, sum(sends), sum(slots)
+        loads = math.prod(grid.sizes[x] for x in order[1:-1])
+        slots = sum(Scatter.slots(grid, order, level) for level in range(len(order)))
+        return loads, slots, slots
 
     def hbm(self, places):
         idx = tuple(places.get(x, slice(None)) for x in self.layout_axes)
         return self.src.at[idx + (slice(None), self.columns)]
 
-    def units(self, level, first=None):
+    def units(self, level):
         found = [{}]
         for x in self.order[1:level]:
             found = [{**places, x: j} for places in found for j in reversed(self.grid.nearest(x))]
         return found
 
     def mine(self, places):
-        idx = tuple(places.get(x, self.grid.at[x]) for x in self.kept(self.grid, self.order))
-        return self.own.at[idx]
+        return self.own.at[tuple(places.get(x, self.grid.at[x]) for x in self.order[1:-1])]
 
     def number(self, places, axes):
         value = 0
@@ -353,40 +346,31 @@
             value = value * self.grid.sizes[x] + places[x]
         return value
 
-    def slot(self, level, places, way=None, target=None):
+    def slot(self, level, places, line):
         axes = self.order[1:level]
-        idx = tuple(places[x] for x in axes)
-        inner = math.prod(self.grid.sizes[x] for x in axes)
-        number = self.number(places, axes)
-        if way is not None:
-            line = target + 1 - way
-            idx = (line,) + idx
-            number = line * inner + number
-        ref = self.recvs[level]
-        return (ref.at[idx] if idx else ref), self.recv_sem.at[self.base[level] + number]
-
-    def send(self, cond, view, landing, axis, place):
-        slot = self.sends
-        self.sends += 1
-        ref, sem = landing
-
-        def make():
-            return pltpu.make_async_remote_copy(
-                src_ref=view,
-                dst_ref=ref,
-                send_sem=self.send_sem.at[slot],
-                recv_sem=sem,
-                device_id=self.grid.peer(axis, place),
-                device_id_type=MESH,
-            )
-
-        guarded(cond, lambda: make().start())
-        self.pending.append((cond, make))
-
-    def take(self, cond, landing, total, out=None):
-        ref, sem = landing
-
-        def body():
+        number = line * math.prod(self.grid.sizes[x] for x in axes) + self.number(places, axes)
+        ref = self.recvs[level].at[(line,) + tuple(places[x] for x in axes)]
+        return ref, self.recv_sem.at[self.base[level] + number]
+
+    def send(self, level, places, step, place, view):
+        axis = self.order[level]
+        ref, sem = self.slot(level, places, self.grid.sizes[axis] - 1 - step)
+        copy = pltpu.make_async_remote_copy(
+            src_ref=view,
+            dst_ref=ref,
+            send_sem=self.send_sem.at[len(self.pending)],
+            recv_sem=sem,
+            device_id=self.grid.peer(axis, place),
+            device_id_type=MESH,
+        )
+        copy.start()
+        self.pending.append(copy)
+
+    def take(self, level, places, total, out=None):
+        lines = self.grid.sizes[self.order[level]] - 1
+        terms = []
+        for line in range(lines):
+            ref, sem = self.slot(level, places, line)
             pltpu.make_async_remote_copy(
                 src_ref=ref,
                 dst_ref=ref,
@@ -395,95 +379,46 @@
                 device_id={},
                 device_id_type=MESH,
             ).wait_recv()
-            add_into(total, ref, out)
-
-        guarded(cond, body)
+            terms.append(ref)
+        add_into(total, terms, out)
 
     def load(self, places):
-        axes = self.kept(self.grid, self.order)
-        here = {self.order[-1]: self.grid.at[self.order[-1]], **places}
-        return pltpu.make_async_copy(
-            self.hbm(here), self.mine(places), self.load_sem.at[self.number(places, axes)]
-        )
+        here = {**places, self.order[-1]: self.grid.at[self.order[-1]]}
+        number = self.number(places, self.order[1:-1])
+        return pltpu.make_async_copy(self.hbm(here), self.mine(places), self.load_sem.at[number])
 
     def open(self):
-        top = len(self.order) - 1
-        axis = self.order[top]
-        if self.grid.sizes[axis] > 2:
-            for places in self.units(top + 1):
-                self.load(places).start()
-            return
-        there = 1 - self.grid.at[axis]
-        for places in self.units(top):
-            self.send(None, self.hbm({**places, axis: there}), self.slot(top, places), axis, there)
+        axis = self.order[self.top]
+        for places in self.units(self.top):
+            for step, place in enumerate(self.grid.others(axis), 1):
+                self.send(self.top, places, step, place, self.hbm({**places, axis: place}))
             self.load(places).start()
 
     def settle(self, level, places):
-        above = level + 1
-        top = len(self.order) - 1
-        total = self.mine(places)
-        if above > top:
+        if level + 1 == self.top:
             self.load(places).wait()
-            return
-        if above == top and self.grid.sizes[self.order[top]] == 2:
-            self.load(places).wait()
-            self.take(None, self.slot(above, places), total)
-            return
-        axis = self.order[above]
-        n, p = self.grid.sizes[axis], self.grid.at[axis]
-        if n == 2:
-            self.take(None, self.slot(above, places), total)
-        else:
-            self.take(p >= 1, self.slot(above, places, 0, p), total)
-            self.take(p + 1 < n, self.slot(above, places, 1, p), total)
-
-    def levels(self):
-        top = len(self.order) - 1
-        return top if self.grid.sizes[self.order[top]] == 2 else top + 1
+        self.take(level + 1, places, self.mine(places))
 
     def step(self, level):
         axis = self.order[level]
-        n, p = self.grid.sizes[axis], self.grid.at[axis]
         if level == 0:
             self.settle(0, {})
-            whole = self.mine({})
-            self.along(level, {}, lambda t: whole.at[t])
+            for step, place in enumerate(self.grid.others(axis), 1):
+                self.send(0, {}, step, place, self.mine({}).at[place])
             return
         for places in self.units(level):
-            self.along(level, places, lambda t: self.mine({**places, axis: t}))
-            self.settle(level, {**places, axis: p})
-
-    def along(self, level, places, view):
-        axis = self.order[level]
-        n, p = self.grid.sizes[axis], self.grid.at[axis]
-        if n == 2:
-            if level:
-                self.settle(level, {**places, axis: 1 - p})
-            self.send(None, view(1 - p), self.slot(level, places), axis, 1 - p)
-            return
-        for s in range(n - 1):
-            for way, t in ((0, n - 1 - s), (1, s)):
-                wanted = (t > p) if way == 0 else (t < p)
-                behind = (p >= 1) if way == 0 else (p + 1 < n)
-                if level:
-                    pl.when(wanted)(lambda: self.settle(level, {**places, axis: t}))
-                self.take(jnp.logical_and(wanted, behind), self.slot(level, places, way, t), view(t))
-                self.send(wanted, view(t), self.slot(level, places, way, t), axis, p + (1 if way == 0 else -1))
+            for step, place in enumerate(self.grid.others(axis), 1):
+                unit = {**places, axis: place}
+                self.settle(level, unit)
+                self.send(level, places, step, place, self.mine(unit))
+            self.settle(level, {**places, axis: self.grid.at[axis]})
 
     def finish(self):
-        axis = self.order[0]
-        n, p = self.grid.sizes[axis], self.grid.at[axis]
-        total = self.mine({}).at[p]
-        if n == 2:
-            self.take(None, self.slot(0, {}), total, self.out)
-            return
-        self.take(p >= 1, self.slot(0, {}, 0, p), total)
-        self.take(p + 1 < n, self.slot(0, {}, 1, p), total)
-        add_into(total, None, self.out)
+        self.take(0, {}, self.mine({}).at[self.grid.at[self.order[0]]], self.out)
 
     def close(self):
-        for cond, make in self.pending:
-            guarded(cond, lambda: make().wait_send())
+        for copy in self.pending:
+            copy.wait_send()
 
 
 def half_pairs(ref, s):
@@ -887,6 +822,22 @@
     )(core, left, left_other, right, right_other)
 
 
+def handed_kernel(*refs):
+    for source, out in zip(refs[: len(refs) // 2], refs[len(refs) // 2 :]):
+        out[...] = source[...]
+
+
+def handed(*results):
+    vmem = pl.BlockSpec(memory_space=pltpu.VMEM)
+    return pl.pallas_call(
+        handed_kernel,
+        out_shape=[jax.ShapeDtypeStruct(x.shape, x.dtype) for x in results],
+        in_specs=[vmem] * len(results),
+        out_specs=[vmem] * len(results),
+        name="handed",
+    )(*results)
+
+
 BACK_SUMS = ("g", "u", "d", "o")
 
 
@@ -936,7 +887,8 @@
         make(gk_ref, pl.ds(0, KVH * HD), AB, own_k, SLOT_AXES),
         make(gv_ref, pl.ds(0, KVH * HD), BA, own_v, SLOT_AXES),
     ]
-    early, late = portions(plan[0]), portions(plan[1])
+    early, waves = portions(plan[0]), [portions(group) for group in plan[1]]
+    late = [p for wave in waves for p in wave]
     last = []
     for name, at, low, high, order in plan[2]:
         last.append(
@@ -980,23 +932,21 @@
             done.append(norm_back(g, unit, inverse, gain))
         both_raw[0, :, at] = jnp.concatenate(done, axis=1).astype(jnp.bfloat16)
 
+    half_q = H * HD // 2
+    q_cols, kv_cols = pl.ds(0, H * HD), pl.ds(H * HD, 2 * KVH * HD)
     loop(H // 4, functools.partial(heads, dq_ref, 0, 0, 2 * lanes))
     for p in slabs:
         p.step(1)
-    for p in late[: len(late) // 2]:
-        p.open()
-    half_q = H * HD // 2
     loop(H // 4, functools.partial(heads, dq_ref, half_q, half_q, 2 * lanes))
-    q_cols, kv_cols = pl.ds(0, H * HD), pl.ds(H * HD, 2 * KVH * HD)
     swap_q = sibling(both_raw.at[0, :, q_cols], both_raw.at[1, :, q_cols], 1)
     swap_q.start()
     for p in slabs:
         p.step(0)
-    for p in late[len(late) // 2 :]:
-        p.open()
-    for p in early:
-        for level in range(p.levels() - 1, 0, -1):
-            p.step(level)
+    def every(group, what, *args):
+        for p in group:
+            getattr(p, what)(*args)
+
+    every(waves[0], "open")
     for p in slabs:
         p.finish()
     loop(KVH // 2, functools.partial(heads, own_k, 0, H * HD, 2 * lanes + 1))
@@ -1004,8 +954,7 @@
     both_raw[0, :, at : at + KVH * HD] = own_v[...].astype(jnp.bfloat16)
     swap_kv = sibling(both_raw.at[0, :, kv_cols], both_raw.at[1, :, kv_cols], 2)
     swap_kv.start()
-    for p in late[: len(late) // 2]:
-        p.step(1)
+    every(waves[1], "open")
     swap_normed.wait()
     swap_q.wait()
     swap_kv.wait()
@@ -1017,11 +966,12 @@
     full = both_raw.shape[-1]
     tile = 512
 
+    def stored(j):
+        return pltpu.make_async_copy(stage.at[j % 2], sums_ref.at[j // 2, j % 2], misc_sem[9 + j % 2])
+
     for j in range(count):
         if j >= 2:
-            pltpu.make_async_copy(
-                stage.at[j % 2], sums_ref.at[(j - 2) // 2, (j - 2) % 2], misc_sem[9 + j % 2]
-            ).wait()
+            stored(j - 2).wait()
         lhs = flat_normed[:, pl.ds(pl.multiple_of((2 * j + core) * block, block), block)]
 
         def sums(c):
@@ -1030,13 +980,15 @@
             stage[j % 2, :, :, cols] = value.reshape(grid.sizes["f"], piece, tile)
 
         loop(full // tile, sums)
-        pltpu.make_async_copy(stage.at[j % 2], sums_ref.at[j // 2, j % 2], misc_sem[9 + j % 2]).start()
+        stored(j).start()
     for j in range(count - 2, count):
-        pltpu.make_async_copy(stage.at[j % 2], sums_ref.at[j // 2, j % 2], misc_sem[9 + j % 2]).wait()
-    for p in last:
-        p.open()
-    for p in late[len(late) // 2 :]:
-        p.step(1)
+        stored(j).wait()
+    every(waves[0], "step", 1)
+    every(last, "open")
+    every(waves[2], "open")
+    every(early, "step", 1)
+    every(waves[1], "step", 1)
+    every(waves[0], "step", 0)
     tiles = [
         pltpu.make_async_copy(
             wqkv_ref.at[:, c * tile : (c + 1) * tile], weights.at[c % 2], misc_sem[6 + c % 2]
@@ -1066,10 +1018,10 @@
     spread.open()
     mine = tuple(grid.at[x] for x in ALL_AXES)
     gall_ref[mine] = gblock[...]
-    for p in early + late:
-        p.step(0)
-    for p in last:
-        p.step(1)
+    every(early, "step", 0)
+    every(last, "step", 1)
+    every(waves[2], "step", 1)
+    every(waves[1], "step", 0)
     spread.first()
     dots = jnp.zeros((rows, 1), jnp.float32)
     for j in range(lanes):
@@ -1083,16 +1035,14 @@
         grad = inverse * (acc[:, cols] * gains_ref[j : j + 1, :] - normal * dots)
         din_ref[:, cols] = (mid_ref[:, cols] + grad).astype(jnp.bfloat16)
     spread.arrivals(1)
-    for p in early + late:
-        p.finish()
-    for p in last:
-        p.step(0)
+    every(last, "step", 0)
+    every(waves[2], "step", 0)
     spread.arrivals(2)
+    every(waves[0] + early + waves[1], "finish")
     spread.arrivals(3)
+    every(last + waves[2], "finish")
     places = math.prod(grid.sizes[x] for x in ALL_AXES)
     gsum_ref[...] = jnp.sum(gall_ref.reshape((places,) + gblock.shape)[...], axis=0)
-    for p in last:
-        p.finish()
     for p in slabs + early + late + last:
         p.close()
     spread.close()
@@ -1104,7 +1054,7 @@
     for order in (AB, BA):
         scratch += Scatter.scratch(grid, order, rows, KVH * HD, low)
         counts.append(Scatter.semaphores(grid, order))
-    for name, begin, end, order in plan[0] + plan[1] + tuple((p[0],) + p[2:] for p in plan[2]):
+    for name, begin, end, order in plan[0] + sum(plan[1], ()) + tuple((p[0],) + p[2:] for p in plan[2]):
         scratch += Scatter.scratch(grid, order, pieces[name], end - begin, low)
         counts.append(Scatter.semaphores(grid, order))
     return scratch, [sum(x) for x in zip(*counts)]
@@ -1205,7 +1155,7 @@
         parts[-1].open()
     for level in (2, 1, 0):
         for part in parts:
-            if level < part.levels():
+            if level < part.top:
                 part.step(level)
     for part in parts:
         part.finish()
@@ -1303,8 +1253,8 @@
             ("v", 0, 2 * half_k, AFB + CORE),
         ),
         (
-            ("o", 0, width // 2, BFA + CORE),
-            ("o", width // 2, width, AFB + CORE),
+            ("o", 0, width // 2, ABF + CORE),
+            ("o", width // 2, width, BAF + CORE),
             ("g", 0, hidden_width, BFA + CORE),
             ("u", 0, hidden_width, AFB + CORE),
             ("d", 0, width // 2, BFA + CORE),
@@ -1384,16 +1334,15 @@
     back_plan = (
         (("d", 0, width // 2, ABF), ("d", width // 2, width, BAF)),
         (
-            ("g", 0, hidden_width, FAB),
-            ("u", 0, hidden_width, FBA),
-            ("o", 0, width // 2, FAB),
-            ("o", width // 2, width, FBA),
+            (("g", 0, hidden_width // 2, FAB), ("g", hidden_width // 2, hidden_width, FBA)),
+            (("u", 0, hidden_width // 2, FAB), ("u", hidden_width // 2, hidden_width, FBA)),
+            (("o", 0, width // 2, FAB), ("o", width // 2, width, FBA)),
         ),
         (
-            ("q", 0, 0, half_q, FAB),
-            ("q", 0, half_q, 2 * half_q, FBA),
-            ("k", H * HD, 0, 2 * half_k, BFA),
-            ("v", (H + KVH) * HD, 0, 2 * half_k, AFB),
+            ("q", 0, 0, half_q, ABF),
+            ("q", 0, half_q, 2 * half_q, BAF),
+            ("k", H * HD, 0, 2 * half_k, FAB),
+            ("v", (H + KVH) * HD, 0, 2 * half_k, FBA),
         ),
     )
     if back_fits(grid, back_plan, rows, width, hidden_width, total):
@@ -1414,6 +1363,9 @@
             inverse_rows,
             grad_middle,
             grad_gain_two.reshape(lanes, 128),
+        )
+        out_g, out_u, out_down, out_output, out_q, out_k, out_v, grad_tokens = handed(
+            out_g, out_u, out_down, out_output, out_q, out_k, out_v, grad_tokens
         )
         flat_sums = gain_sums.reshape(-1)
 

time: 559 us -> 491 us (0.88)
  Pallas kernels: 486 us -> 430 us
  local copies, waits for them, and re-layouts: 25 us -> 13.3 us
    pallas_call x1, Pallas kernels: 235 us -> 184 us  [back(): pl.pallas_call(functools.partial(back_kernel, grid, plan), out_shape=[sha...]
    unnamed x33 -> x21, local copies, waits for them, and re-layouts: 12.5 us -> 0.86 us
    pallas_call x1, Pallas kernels: 179 us -> 171 us  [front(): pl.pallas_call(functools.partial(front_kernel, grid, plan), out_shape=[sh...]
  transfers between devices with their start and end apart: 7 -> 7, of which waited for: 0 -> 0; matrix products, arithmetic and copies ran while one was open for 8% -> 9% of each run, Pallas kernels for 10% -> 11%
where the time goes in v4:
time: 491 us; the launch traced here: 489 us
  Pallas kernels  430 us (88%)
  matrix products  34.7 us (7%)
  local copies, waits for them, and re-layouts  13.3 us (3%)
  other arithmetic  6.94 us (1%)
    pallas_call x1, Pallas kernels, back(): pl.pallas_call(functools.partial(back_kernel, grid, plan), out_shape=[sha...  184 us
    pallas_call x1, Pallas kernels, front(): pl.pallas_call(functools.partial(front_kernel, grid, plan), out_shape=[sh...  171 us
    pallas_call x4, Pallas kernels, chip_sums(): pl.pallas_call(sums_kernel, grid_spec=pltpu.PrefetchScalarGridSpec(num_sc...  31.2 us
    pallas_call x1, Pallas kernels, attention_back(): pl.pallas_call(functools.partial(attention_back_kernel, pairs), grid_spec...  28 us
    dot_general x3, matrix products, right_dot(): lax.dot_general(left, right, (((1,), (1,)), ((), ())), preferred_element_...  18.3 us
    dot_general x3, matrix products, plain_dot(): return jnp.dot(left, right, preferred_element_type=jnp.float32)  16.4 us
    pallas_call x1, Pallas kernels, attention(): pl.pallas_call(functools.partial(attention_kernel, pairs), grid_spec=pltp...  12.6 us
  transfers between devices with their start and end apart: 7, of which 0 were waited for; matrix products, arithmetic and copies ran while one was open for 9% of the time, Pallas kernels for 11%

profile of v4, /device:TPU:0, one launch (start us, length us, event | category | flops | bytes accessed | tf_op | source)
XLA Modules:
  0.0 489.4 jit_solution(15665729066349300125)
XLA Ops:
  5.3 0.9 dynamic_update_slice.12
  6.2 0.8 dynamic_update_slice.13
  8.7 0.8 pad_maximum_fusion
  9.5 1.2 pad_add_fusion.table
  10.8 171.5 %front.1 = (bf16[2,2,2,4,32,4096]{5,4,3,2,1,0:T(8,128)(2,1)}, bf16[2,2,2,4,64,1024]{5,4,3,2,1,0:T(8,128)(2,1)}, bf16[2,2,2,4,32,6144]{5,4,3,2,1,0:T(8,128)(2,1)}...) custom-call(bf16[32,2048]{1,0:T(8,128)(2,1)} %refs_0_.1, ...), custom_call_target="tpu_custom_call" | custom-call | tf_op jit(solution)/shard_map/front/pallas_call | solution.py:751
  182.3 12.6 %attention.1 = (f32[256,2048]{1,0:T(8,128)}, bf16[256,2048]{1,0:T(8,128)(2,1)}, f32[8,2,256]{2,1,0:T(2,128)}) custom-call(s32[18]{0:T(128)} %pad_add_fusion.table, bf16[256,2048]{1,0:T(8,128)(2,1)} %get-tuple-element.47.q_ref, bf16[2048,1024]{1,0:T(8,128)(2,1)} %bitcast.76, bf16[2048,1024]{1,0:T(8,128)(2,1)} %bitcast.78), custom_call_target="tpu_custom_call" | custom-call | tf_op jit(solution)/shard_map/attention/pallas_call | solution.py:485
  195.6 3.9 multiply_reduce_fusion.3
  200.3 6.7 %fusion.17 = f32[256,6144]{1,0:T(8,128)S(1)} fusion(bf16[256,1024]{1,0:T(8,128)(2,1)S(1)} %multiply_convert_fusion.3.left, bf16[1024,6144]{1,0:T(8,128)(2,1)} %bitcast.80), kind=kOutput, calls=%fused_computation.47 | convolution fusion | flops 3221225472 | bytes 19398656 | tf_op jit(solution)/shard_map/dot_general | solution.py:58
  207.1 4.9 multiply_convert_fusion
  212.5 8.2 %multiply_reduce_fusion.1 = (f32[1024]{0:T(1024)}, f32[256]{0:T(256)S(1)}, f32[256,1024]{1,0:T(8,128)S(1)}) fusion(f32[256,1024]{1,0:T(8,128)S(1)} %get-tuple-element.102, f32[256]{0:T(256)S(1)} %add_rsqrt_fusion, f32[1024]{0:T(1024)S(1)} %slice_bitcast_fusion, bf16[1024,6144]{1,0:T(8,128)(2,1)} %bitcast.81, bf16[256,3072]{1,0:T(8,128)(2,1)} %get-tuple-element.87.right, ...), kind=kOutput, calls=%fused_computation.16 | convolution fusion | flops 3229088512 | bytes 17836032 | tf_op jit(solution)/shard_map/dot_general | solution.py:52
  220.6 1.3 fusion.13
  222.5 2.9 copy.40
  225.4 5.2 %multiply_reduce_fusion = (f32[256,16]{0,1:T(8,128)S(1)}, bf16[256,16,128]{0,2,1:T(8,128)(2,1)}) fusion(f32[256,2048]{0,1:T(8,128)} %copy.40, f32[256,16]{0,1:T(8,128)S(1)} %bitcast.96, bf16[16,128,1024]{2,1,0:T(8,128)(2,1)} %bitcast.106, bf16[256,1024]{1,0:T(8,128)(2,1)S(1)} %get-tuple-element.83.right), kind=kOutput, calls=%fused_computation.10 | convolution fusion | flops 1075834880 | bytes 7897088 | tf_op jit(solution)/shard_map/dot_general | solution.py:52
  230.6 2.3 copy.39.g_ref
  233.6 28.0 %attention_back.1 = (f32[256,2048]{1,0:T(8,128)}, bf16[2048,1024]{1,0:T(8,128)(2,1)}, bf16[2048,1024]{1,0:T(8,128)(2,1)}) custom-call(s32[18]{0:T(128)} %pad_add_fusion.table, bf16[256,2048]{1,0:T(8,128)(2,1)} %get-tuple-element.47.q_ref, bf16[2048,1024]{1,0:T(8,128)(2,1)} %bitcast.77, bf16[2048,1024]{1,0:T(8,128)(2,1)} %bitcast.79, ...), custom_call_target="tpu_custom_call" | custom-call | tf_op jit(solution)/shard_map/attention_back/pallas_call | solution.py:547
  262.2 5.9 %fusion.6 = bf16[1,256,1024]{2,1,0:T(8,128)(2,1)} fusion(f32[256,1024]{1,0:T(8,128)S(1)} %get-tuple-element.102, bf16[256,3072]{1,0:T(8,128)(2,1)} %get-tuple-element.89.left, bf16[3072,1024]{1,0:T(8,128)(2,1)} %bitcast.101), kind=kOutput, calls=%fused_computation.15 | convolution fusion | flops 1611137024 | bytes 9437184 | tf_op jit(solution)/shard_map/dot_general | solution.py:58
  268.1 4.9 chip_sums.7
  273.8 10.4 %chip_sums.5 = bf16[512,3072]{1,0:T(8,128)(2,1)} custom-call(s32[1]{0:T(128)} %bitcast.14.core, bf16[256,1024]{1,0:T(8,128)(2,1)} %copy-done, bf16[256,1024]{1,0:T(8,128)(2,1)} %copy-done.4, bf16[256,3072]{1,0:T(8,128)(2,1)} %get-tuple-element.87.right, bf16[256,3072]{1,0:T(8,128)(2,1)} %collective-permute-done.2.right_other), custom_call_target="tpu_custom_call" | custom-call | tf_op jit(solution)/shard_map/chip_sums/pallas_call | solution.py:812
  284.2 10.4 %chip_sums.4 = bf16[512,3072]{1,0:T(8,128)(2,1)} custom-call(s32[1]{0:T(128)} %bitcast.14.core, bf16[256,1024]{1,0:T(8,128)(2,1)} %copy-done, bf16[256,1024]{1,0:T(8,128)(2,1)} %copy-done.4, bf16[256,3072]{1,0:T(8,128)(2,1)} %get-tuple-element.88.right, bf16[256,3072]{1,0:T(8,128)(2,1)} %collective-permute-done.1.right_other), custom_call_target="tpu_custom_call" | custom-call | tf_op jit(solution)/shard_map/chip_sums/pallas_call | solution.py:812
  294.6 5.6 %chip_sums.6 = bf16[1536,1024]{1,0:T(8,128)(2,1)} custom-call(s32[1]{0:T(128)} %bitcast.14.core, bf16[256,3072]{1,0:T(8,128)(2,1)} %get-tuple-element.89.left, bf16[256,3072]{1,0:T(8,128)(2,1)} %collective-permute-done.3.left_other, bf16[256,1024]{1,0:T(8,128)(2,1)} %bitcast.91, bf16[256,1024]{1,0:T(8,128)(2,1)} %collective-permute-done.4.right_other), custom_call_target="tpu_custom_call" | custom-call | tf_op jit(solution)/shard_map/chip_sums/pallas_call | solution.py:812
  300.1 183.5 %back.1 = (f32[32,3072]{1,0:T(8,128)}, f32[32,3072]{1,0:T(8,128)}, f32[96,1024]{1,0:T(8,128)}, f32[64,1024]{1,0:T(8,128)}, f32[32,2048]{1,0:T(8,128)}, /*index=5...) custom-call(bf16[2,2,4,32,3072]{4,3,2,1,0:T(8,128)(2,1)} %bitcast.83, ...), custom_call_target="tpu_custom_call" | custom-call | tf_op jit(solution)/shard_map/back/pallas_call | solution.py:1088
  483.7 1.4 fusion.15
  485.0 1.3 fusion.14
  486.3 3.1 handed.1
  (52 shorter events, 9.7 us)
Async XLA Ops:
  8.7 2.1 copy-start.7
  182.3 13.3 %copy-start.1 = (bf16[1,256,1024]{2,1,0:T(8,128)(2,1)S(1)}, bf16[1,256,1024]{2,1,0:T(8,128)(2,1)}, u32[]{:S(2)}) copy-start(bf16[1,256,1024]{2,1,0:T(8,128)(2,1)} %param.14) | copy-start | bytes 1572868
  194.9 67.0 %collective-permute-start.5 = (bf16[256,2048]{1,0:T(8,128)(2,1)}, bf16[256,2048]{1,0:T(8,128)(2,1)}, u32[]{:S(2)}, u32[]{:S(2)}) collective-permute-start(bf16[256,2048]{1,0:T(8,128)(2,1)} %get-tuple-element.50.left), channel_id=1, source_target_pairs={{0,4},{4,0},{8,12},{12,8},{16,20},{20,16},{24,28},{28,24},{1,5},{5... | collective-permute-start | bytes 3145736 | tf_op jit(solution)/shard_map/ppermute | solution.py:1201
  200.1 6.9 %slice-start = ((s8[6291456]{0:T(1024)(128)(4,1)}), s8[4194304]{0:T(1024)(128)(4,1)S(1)}, s32[]{:S(2)}) async-start(s8[6291456]{0:T(1024)(128)(4,1)} %bitcast.102), calls=%async_computation | async-start | bytes 8388608
  200.3 61.3 %copy-start = (bf16[256,1024]{1,0:T(8,128)(2,1)}, bf16[256,1024]{1,0:T(8,128)(2,1)S(1)}, u32[]{:S(2)}) copy-start(bf16[256,1024]{1,0:T(8,128)(2,1)S(1)} %multiply_convert_fusion.3.left) | copy-start | bytes 1572868
  200.3 6.8 %copy-start.2 = (bf16[1,256,1024]{2,1,0:T(8,128)(2,1)S(1)}, bf16[1,256,1024]{2,1,0:T(8,128)(2,1)}, u32[]{:S(2)}) copy-start(bf16[1,256,1024]{2,1,0:T(8,128)(2,1)} %param.15) | copy-start | bytes 1572868
  200.3 6.8 %slice-start.1 = ((s8[6291456]{0:T(1024)(128)(4,1)}), s8[2097152]{0:T(1024)(128)(4,1)S(1)}, s32[]{:S(2)}) async-start(s8[6291456]{0:T(1024)(128)(4,1)} %bitcast.102), calls=%async_computation.1 | async-start | bytes 4194304
  211.9 82.6 %collective-permute-start.3 = (bf16[256,3072]{1,0:T(8,128)(2,1)}, bf16[256,3072]{1,0:T(8,128)(2,1)}, u32[]{:S(2)}, u32[]{:S(2)}) collective-permute-start(bf16[256,3072]{1,0:T(8,128)(2,1)} %get-tuple-element.89.left), channel_id=1, source_target_pairs={{0,4},{4,0},{8,12},{12,8},{16,20},{20,16},{24,28},{28,24},{1,5},{5... | collective-permute-start | bytes 4718600 | tf_op jit(solution)/shard_map/ppermute | solution.py:1201
  212.0 61.0 %collective-permute-start.2 = (bf16[256,3072]{1,0:T(8,128)(2,1)}, bf16[256,3072]{1,0:T(8,128)(2,1)}, u32[]{:S(2)}, u32[]{:S(2)}) collective-permute-start(bf16[256,3072]{1,0:T(8,128)(2,1)} %get-tuple-element.87.right), channel_id=1, source_target_pairs={{0,4},{4,0},{8,12},{12,8},{16,20},{20,16},{24,28},{28,24},{1,5},{5... | collective-permute-start | bytes 4718600 | tf_op jit(solution)/shard_map/ppermute | solution.py:1201
  212.5 71.7 %collective-permute-start.1 = (bf16[256,3072]{1,0:T(8,128)(2,1)}, bf16[256,3072]{1,0:T(8,128)(2,1)}, u32[]{:S(2)}, u32[]{:S(2)}) collective-permute-start(bf16[256,3072]{1,0:T(8,128)(2,1)} %get-tuple-element.88.right), channel_id=1, source_target_pairs={{0,4},{4,0},{8,12},{12,8},{16,20},{20,16},{24,28},{28,24},{1,5},{5... | collective-permute-start | bytes 4718600 | tf_op jit(solution)/shard_map/ppermute | solution.py:1201
  222.0 8.7 %copy-start.3 = (bf16[256,1024]{1,0:T(8,128)(2,1)}, bf16[256,1024]{1,0:T(8,128)(2,1)S(1)}, u32[]{:S(2)}) copy-start(bf16[256,1024]{1,0:T(8,128)(2,1)S(1)} %get-tuple-element.83.right) | copy-start | bytes 1572868
  222.0 3.4 copy-start.6
  222.0 39.6 %collective-permute-start.6 = (bf16[256,1024]{1,0:T(8,128)(2,1)S(1)}, bf16[256,1024]{1,0:T(8,128)(2,1)S(1)}, u32[]{:S(2)}, u32[]{:S(2)}) collective-permute-start(bf16[256,1024]{1,0:T(8,128)(2,1)S(1)} %get-tuple-element.83.right), channel_id=1, source_target_pairs={{0,4},{4,0},{8,12},{12,8},{16,20},{20,16},{24,28},{28,24},{1,5},{5... | collective-permute-start | bytes 1572872 | tf_op jit(solution)/shard_map/ppermute | solution.py:1201
  261.6 6.4 %copy-start.5 = (bf16[256,1024]{1,0:T(8,128)(2,1)}, bf16[256,1024]{1,0:T(8,128)(2,1)S(1)}, u32[]{:S(2)}) copy-start(bf16[256,1024]{1,0:T(8,128)(2,1)S(1)} %collective-permute-done.6.right_other) | copy-start | bytes 1572868
  261.6 11.3 %collective-permute-start = (bf16[256,1024]{1,0:T(8,128)(2,1)S(1)}, bf16[256,1024]{1,0:T(8,128)(2,1)S(1)}, u32[]{:S(2)}, u32[]{:S(2)}) collective-permute-start(bf16[256,1024]{1,0:T(8,128)(2,1)S(1)} %multiply_convert_fusion.3.left), channel_id=1, source_target_pairs={{0,4},{4,0},{8,12},{12,8},{16,20},{20,16},{24,28},{28,24},{1,5},{5... | collective-permute-start | bytes 1572872 | tf_op jit(solution)/shard_map/ppermute | solution.py:1201
  261.9 32.7 %collective-permute-start.4 = (bf16[256,1024]{1,0:T(8,128)(2,1)S(1)}, bf16[256,1024]{1,0:T(8,128)(2,1)}, u32[]{:S(2)}, u32[]{:S(2)}) collective-permute-start(bf16[256,1024]{1,0:T(8,128)(2,1)S(1)} %bitcast.92), channel_id=1, source_target_pairs={{0,4},{4,0},{8,12},{12,8},{16,20},{20,16},{24,28},{28,24},{1,5},{5... | collective-permute-start | bytes 1572872 | tf_op jit(solution)/shard_map/ppermute | solution.py:1201
  272.9 0.8 copy-start.4

commit v5 on v4

--- a/solution.py
+++ b/solution.py
@@ -426,6 +426,17 @@
     return jnp.concatenate([ref[rows, :HD], ref[rows, HD:]], axis=0)
 
 
+def read_map(blocks, table, pairs):
+    @pl.when(pl.program_id(0) == 0)
+    def _():
+        for t in range(2 * pairs):
+            table[blocks[t]] = t
+        place = lax.axis_index("ctx")
+        first, second = blocks[2 * place], blocks[2 * place + 1]
+        table[2 * pairs] = jnp.where(second > first, 1, 0)
+        table[2 * pairs + 1] = jnp.maximum(first, second)
+
+
 def items(table, pairs):
     high_slot, high = table[pairs * 2], table[pairs * 2 + 1]
     low_block = 2 * pairs - 1 - high
@@ -449,7 +460,8 @@
     return lax.dot_general(left, right, (((1,), (1,)), ((), ())), preferred_element_type=jnp.float32)
 
 
-def attention_kernel(pairs, table, q_ref, k_ref, v_ref, o_ref, low_ref, t_ref, qs, acc, tot):
+def attention_kernel(pairs, blocks, q_ref, k_ref, v_ref, o_ref, low_ref, over_ref, table, qs, acc, tot):
+    read_map(blocks, table, pairs)
     for s in range(2):
         qs[s] = half_pairs(q_ref, s)
     acc[...] = jnp.zeros_like(acc)
@@ -467,29 +479,30 @@
         tot[s] += weights[:, :HD] + weights[:, HD:]
         acc[s] += jnp.dot(weights.astype(jnp.bfloat16), vals, preferred_element_type=jnp.float32)
     for s in range(2):
-        total = tot[s]
-        value = acc[s] / jnp.sum(total, axis=1, keepdims=True)
+        over = 1.0 / jnp.sum(tot[s], axis=1, keepdims=True)
+        value = acc[s] * over
+        over = jnp.broadcast_to(over, value.shape)
         rows = pl.ds(s * BLK, BLK)
         for i in range(2):
             part = value[i * BLK : (i + 1) * BLK]
             o_ref[rows, i * HD : (i + 1) * HD] = part
             low_ref[rows, i * HD : (i + 1) * HD] = part.astype(jnp.bfloat16)
-        t_ref[0, s : s + 1, :] = jnp.sum(total.T, axis=0, keepdims=True)
-
-
-def attention(table, pairs, queries, keys, values):
+            over_ref[rows, i * HD : (i + 1) * HD] = over[i * BLK : (i + 1) * BLK]
+
+
+def attention(blocks, pairs, queries, keys, values):
     rows, length = queries.shape[0], keys.shape[0]
     head = pl.BlockSpec((rows, 2 * HD), lambda h, t: (0, h))
     side = pl.BlockSpec((length, HD), lambda h, t: (0, h))
-    stats = pl.BlockSpec((1, 2, 2 * BLK), lambda h, t: (h, 0, 0))
     return pl.pallas_call(
         functools.partial(attention_kernel, pairs),
         grid_spec=pltpu.PrefetchScalarGridSpec(
             num_scalar_prefetch=1,
             grid=(KVH,),
             in_specs=[head, side, side],
-            out_specs=[head, head, stats],
+            out_specs=[head, head, head],
             scratch_shapes=[
+                pltpu.SMEM((2 * pairs + 2,), jnp.int32),
                 pltpu.VMEM((2, 2 * BLK, HD), jnp.bfloat16),
                 pltpu.VMEM((2, 2 * BLK, HD), jnp.float32),
                 pltpu.VMEM((2, 2 * BLK, HD), jnp.float32),
@@ -498,19 +511,22 @@
         out_shape=[
             jax.ShapeDtypeStruct((rows, H * HD), jnp.float32),
             jax.ShapeDtypeStruct((rows, H * HD), jnp.bfloat16),
-            jax.ShapeDtypeStruct((KVH, 2, 2 * BLK), jnp.float32),
+            jax.ShapeDtypeStruct((rows, H * HD), jnp.float32),
         ],
         name="attention",
-    )(table, queries, keys, values)
+    )(blocks, queries, keys, values)
 
 
 def attention_back_kernel(
-    pairs, table, q_ref, k_ref, v_ref, g_ref, d_ref, dq_ref, dk_ref, dv_ref, qs, gs, dq, dk, dv
+    pairs, blocks, q_ref, k_ref, v_ref, g_ref, o_ref, dq_ref, dk_ref, dv_ref, table, qs, gs, drift, dq, dk, dv
 ):
+    read_map(blocks, table, pairs)
     scale = HD ** (-0.5)
     for s in range(2):
         qs[s] = half_pairs(q_ref, s)
         gs[s] = half_pairs(g_ref, s)
+        products = gs[s].astype(jnp.float32) * half_pairs(o_ref, s)
+        drift[s : s + 1, :] = jnp.sum(products.T, axis=0, keepdims=True)
     for total in (dq, dk, dv):
         total[...] = jnp.zeros_like(total)
     for s, c, block in items(table, pairs):
@@ -524,7 +540,7 @@
             allowed = rows <= lax.rem(cols, BLK) + (block - 2 * c) * BLK
             weights = jnp.where(allowed, weights, 0.0)
         through = row_contract(vals, grads)
-        scores = (weights * (through - d_ref[0, pl.ds(s, 1), :])).astype(jnp.bfloat16)
+        scores = (weights * (through - drift[pl.ds(s, 1), :])).astype(jnp.bfloat16)
         to_values = jnp.dot(weights.astype(jnp.bfloat16), grads, preferred_element_type=jnp.float32)
         to_keys = jnp.dot(scores, queries, preferred_element_type=jnp.float32)
         for i in range(2):
@@ -539,21 +555,22 @@
             dq_ref[pl.ds(s * BLK, BLK), i * HD : (i + 1) * HD] = dq[s, i * BLK : (i + 1) * BLK] * scale
 
 
-def attention_back(table, pairs, queries, keys, values, grads, drift):
+def attention_back(blocks, pairs, queries, keys, values, grads, attended):
     rows, length = queries.shape[0], keys.shape[0]
     head = pl.BlockSpec((rows, 2 * HD), lambda h, t: (0, h))
     side = pl.BlockSpec((length, HD), lambda h, t: (0, h))
-    stats = pl.BlockSpec((1, 2, 2 * BLK), lambda h, t: (h, 0, 0))
     return pl.pallas_call(
         functools.partial(attention_back_kernel, pairs),
         grid_spec=pltpu.PrefetchScalarGridSpec(
             num_scalar_prefetch=1,
             grid=(KVH,),
-            in_specs=[head, side, side, head, stats],
+            in_specs=[head, side, side, head, head],
             out_specs=[head, side, side],
             scratch_shapes=[
+                pltpu.SMEM((2 * pairs + 2,), jnp.int32),
                 pltpu.VMEM((2, 2 * BLK, HD), jnp.bfloat16),
                 pltpu.VMEM((2, 2 * BLK, HD), jnp.bfloat16),
+                pltpu.VMEM((2, 2 * BLK), jnp.float32),
                 pltpu.VMEM((2, 2 * BLK, HD), jnp.float32),
                 pltpu.VMEM((length, HD), jnp.float32),
                 pltpu.VMEM((length, HD), jnp.float32),
@@ -564,8 +581,13 @@
             jax.ShapeDtypeStruct((length, KVH * HD), jnp.bfloat16),
             jax.ShapeDtypeStruct((length, KVH * HD), jnp.bfloat16),
         ],
+        cost_estimate=pl.CostEstimate(
+            flops=20 * (pairs + 1) * KVH * (2 * BLK) ** 2 * HD,
+            bytes_accessed=14 * rows * H * HD + 8 * length * KVH * HD,
+            transcendentals=(pairs + 1) * KVH * (2 * BLK) ** 2,
+        ),
         name="attention_back",
-    )(table, queries, keys, values, grads, drift)
+    )(blocks, queries, keys, values, grads, attended)
 
 
 ALL_AXES = ("a", "b", "core", "f")
@@ -580,20 +602,34 @@
 FRONT_SRC = ("q", "k", "v", "o", "g", "u", "d", "gains")
 
 
-def front_kernel(grid, plan, *refs):
+def front_kernel(grid, plan, pieces, *refs):
     n = len(FRONT_SRC)
     src = dict(zip(FRONT_SRC, refs[:n]))
     tokens_ref, cosine_ref, sine_ref = refs[n : n + 3]
+    rows_of = refs[n - 1]
     outs = refs[n + 3 : n + 15]
     wqkv_ref, wo_ref, wgu_ref, wd_ref, allgains_ref, k_out, v_out = outs[:7]
     normed_ref, gains_ref, raw_ref, qlow_ref, inv_ref = outs[7:]
     scratch = refs[n + 15 :]
     held = dict(zip(FRONT_SRC, scratch[:n]))
-    weights, klow, vlow, gbuf = scratch[n : n + 4]
-    send, recv, local, load = scratch[n + 4 :]
+    weights, klow, vlow, gbuf, gmine = scratch[n : n + 5]
+    send, recv, local, load = scratch[n + 5 :]
     grid.enter()
     grid.barrier()
     send, recv = Pool(send), Pool(recv)
+    device = grid.c * grid.sizes["f"] + grid.at["f"]
+    block_rows = lax.broadcasted_iota(jnp.int32, gmine.shape, 0)
+    block = jnp.zeros(gmine.shape, jnp.float32)
+    for i, (at, size) in enumerate(pieces):
+        spot = at + device * size
+        line = jnp.broadcast_to(rows_of[i : i + 1, :], (8, 128))
+        line = pltpu.roll(line, lax.rem(spot, 128), 1)[:1]
+        block = jnp.where(block_rows == spot // 128, line, block)
+    gmine[...] = block.astype(gmine.dtype)
+    copy = pltpu.make_async_copy(gmine, held["gains"], local.at[n - 1])
+    copy.start()
+    copy.wait()
+    src["gains"] = held["gains"]
     width = tokens_ref.shape[1]
     rows = tokens_ref.shape[0]
     spans = {"q": (wqkv_ref, 0), "k": (wqkv_ref, H * HD), "v": (wqkv_ref, (H + KVH) * HD)}
@@ -608,7 +644,7 @@
             held[name], dst.at[mine + (slice(None), pl.ds(at, src[name].shape[1]))], local.at[i]
         )
 
-    for i, name in enumerate(FRONT_SRC):
+    for i, name in enumerate(FRONT_SRC[:-1]):
         pltpu.make_async_copy(src[name], held[name], local.at[i]).start()
 
     def part(name, low, high, order):
@@ -626,7 +662,8 @@
     for p in late:
         p.open()
     for i, name in enumerate(FRONT_SRC):
-        pltpu.make_async_copy(src[name], held[name], local.at[i]).wait()
+        if name != "gains":
+            pltpu.make_async_copy(src[name], held[name], local.at[i]).wait()
         own_copy(i, name).start()
     inputs = tokens_ref[...].astype(jnp.float32)
     inverse = lax.rsqrt(jnp.mean(inputs * inputs, axis=-1, keepdims=True) + EPSILON)
@@ -735,11 +772,13 @@
         p.close()
 
 
-def front(grid, plan, blocks, tokens, cosine, sine):
+def front(grid, plan, pieces, blocks, gain_rows, tokens, cosine, sine):
     n = len(FRONT_SRC)
     rows, width = tokens.shape
     places = tuple(grid.sizes[x] for x in ALL_AXES)
     slots = tuple(grid.sizes[x] for x in SLOT_AXES)
+    gains = jax.ShapeDtypeStruct((width // 128 * 2 + 16, 128), jnp.bfloat16)
+    blocks = tuple(blocks) + (gains,)
     by = dict(zip(FRONT_SRC, blocks))
     low, f32 = jnp.bfloat16, jnp.float32
     full = (H + 2 * KVH) * HD
@@ -749,7 +788,7 @@
     shape = jax.ShapeDtypeStruct
     vmem = pl.BlockSpec(memory_space=pltpu.VMEM)
     outs = pl.pallas_call(
-        functools.partial(front_kernel, grid, plan),
+        functools.partial(front_kernel, grid, plan, pieces),
         out_shape=[
             shape(places + (by["q"].shape[0], full), low),
             shape(places + by["o"].shape, low),
@@ -764,7 +803,7 @@
             shape((rows, H * HD), low),
             shape((rows, 128), f32),
         ],
-        in_specs=[ANY] * n + [vmem] * 3,
+        in_specs=[ANY] * (n - 1) + [vmem] * 4,
         out_specs=[ANY] * 7 + [vmem] * 5,
         scratch_shapes=[pltpu.VMEM(x.shape, x.dtype) for x in blocks]
         + [
@@ -772,6 +811,7 @@
             pltpu.VMEM((rows, KVH * HD), low),
             pltpu.VMEM((rows, KVH * HD), low),
             pltpu.VMEM(places + by["gains"].shape, low),
+            pltpu.VMEM(by["gains"].shape, low),
             pltpu.SemaphoreType.DMA((sends,)),
             pltpu.SemaphoreType.DMA((takes,)),
             pltpu.SemaphoreType.DMA((n,)),
@@ -781,23 +821,32 @@
             has_side_effects=True, vmem_limit_bytes=60 * 2**20, collective_id=0
         ),
         name="front",
-    )(*blocks, tokens, cosine, sine)
+    )(*blocks[:-1], gain_rows, tokens, cosine, sine)
     wqkv, wo, wgu, wd, _, keys, vals, normed, gains, raw, qlow, inverse = outs
     flat = [x.reshape(-1, x.shape[-1]) for x in (wqkv, wo, wgu, wd, keys, vals)]
     return flat + [normed, gains, raw, qlow, inverse]
 
 
-def sums_kernel(core, left, left_other, right, right_other, out):
-    lhs = jnp.concatenate([left[...], left_other[...]], axis=0)
+def sums_kernel(count, core, left, left_other, right, right_other, out, turned):
+    rows, width = left.shape
+    block = width // count
+
+    @pl.when(pl.program_id(0) == 0)
+    def _():
+        for j in range(count // 2):
+            at = pl.ds(pl.multiple_of((2 * j + core[0]) * block, block), block)
+            for k, ref in enumerate((left, left_other)):
+                turned[j * block : (j + 1) * block, k * rows : (k + 1) * rows] = ref[:, at].T
+
     rhs = jnp.concatenate([right[...], right_other[...]], axis=0)
-    out[...] = left_dot(lhs, rhs).astype(out.dtype)
+    out[...] = jnp.dot(turned[...], rhs, preferred_element_type=jnp.float32).astype(out.dtype)
 
 
 def chip_sums(left, left_other, right, right_other):
     rows, width = left.shape
     count = lax.axis_size("ctx")
     block = width // count
-    tile = min(1024, right.shape[1])
+    tile = 512
     if block % 128:
         place = lax.axis_index("ctx") % 2
         halves = [
@@ -807,15 +856,16 @@
         lhs = jnp.concatenate(halves, axis=0).reshape(2 * rows, width // 2)
         return left_dot(lhs, jnp.concatenate([right, right_other], axis=0)).astype(jnp.bfloat16)
     core = (lax.axis_index("ctx") % 2).astype(jnp.int32)[None]
-    lhs = pl.BlockSpec((rows, block), lambda n, j, c: (0, 2 * j + c[0]))
-    rhs = pl.BlockSpec((rows, tile), lambda n, j, c: (0, n))
+    lhs = pl.BlockSpec((rows, width), lambda n, c: (0, 0))
+    rhs = pl.BlockSpec((rows, tile), lambda n, c: (0, n))
     return pl.pallas_call(
-        sums_kernel,
+        functools.partial(sums_kernel, count),
         grid_spec=pltpu.PrefetchScalarGridSpec(
             num_scalar_prefetch=1,
-            grid=(right.shape[1] // tile, count // 2),
+            grid=(right.shape[1] // tile,),
             in_specs=[lhs, lhs, rhs, rhs],
-            out_specs=pl.BlockSpec((block, tile), lambda n, j, c: (j, n)),
+            out_specs=pl.BlockSpec((width // 2, tile), lambda n, c: (0, n)),
+            scratch_shapes=[pltpu.VMEM((width // 2, 2 * rows), jnp.bfloat16)],
         ),
         out_shape=jax.ShapeDtypeStruct((width // 2, right.shape[1]), jnp.bfloat16),
         name="chip_sums",
@@ -1128,6 +1178,118 @@
     return outs
 
 
+def middle_kernel(
+    steps, alow_ref, over_ref, wo_ref, wg_ref, wu_ref, wd_ref, tokens_ref, cot_ref, gains_ref,
+    out_ref, hidden_ref, gg_ref, gu_ref, normed_ref, mid_ref, branch_ref, gain_ref, gs_ref,
+    middle, total, back, inv,
+):
+    c = pl.program_id(0)
+    rows, width = tokens_ref.shape
+    lanes = width // 128
+    low = jnp.bfloat16
+
+    @pl.when(c == 0)
+    def _():
+        value = tokens_ref[...].astype(jnp.float32) + plain_dot(alow_ref[...], wo_ref[...])
+        inverse = lax.rsqrt(jnp.mean(value * value, axis=-1, keepdims=True) + EPSILON)
+        inv[...] = jnp.broadcast_to(inverse, inv.shape)
+        middle[...] = value
+        total[...] = value
+        for j in range(lanes):
+            cols = slice(j * 128, (j + 1) * 128)
+            gain = gains_ref[lanes + j : lanes + j + 1, :]
+            normed_ref[:, cols] = (middle[:, cols] * inv[...] * gain).astype(low)
+        back[...] = jnp.zeros_like(back)
+
+    normed = normed_ref[...]
+    gate = plain_dot(normed, wg_ref[...])
+    upper = plain_dot(normed, wu_ref[...])
+    grads = right_dot(cot_ref[...], wd_ref[...])
+    sig = jax.nn.sigmoid(gate)
+    activated = gate * sig
+    hidden = (activated * upper).astype(low)
+    grad_gate = (grads * upper * sig * (1.0 + gate * (1.0 - sig))).astype(low)
+    grad_upper = (grads * activated).astype(low)
+    hidden_ref[...] = hidden
+    gg_ref[...] = grad_gate
+    gu_ref[...] = grad_upper
+    total[...] += plain_dot(hidden, wd_ref[...])
+    back[...] += right_dot(grad_gate, wg_ref[...]) + right_dot(grad_upper, wu_ref[...])
+
+    @pl.when(c == steps - 1)
+    def _():
+        out_ref[...] = total[...].astype(low)
+        inverse = inv[...]
+        dots = jnp.zeros((rows, 1), jnp.float32)
+        for j in range(lanes):
+            cols = slice(j * 128, (j + 1) * 128)
+            normal = middle[:, cols] * inverse
+            gain_ref[j : j + 1, :] = jnp.sum(back[:, cols] * normal, axis=0, keepdims=True)
+            gain = gains_ref[lanes + j : lanes + j + 1, :]
+            dots += jnp.sum(back[:, cols] * gain * normal, axis=1, keepdims=True)
+        dots = dots / width
+        for j in range(lanes):
+            cols = slice(j * 128, (j + 1) * 128)
+            gain = gains_ref[lanes + j : lanes + j + 1, :]
+            normal = middle[:, cols] * inverse
+            grad = cot_ref[:, cols].astype(jnp.float32) + inverse * (back[:, cols] * gain - normal * dots)
+            mid_ref[:, cols] = grad
+            branch_ref[:, cols] = grad.astype(low)
+        tile = 512
+        for j in range(gs_ref.shape[1] // tile):
+            cols = slice(j * tile, (j + 1) * tile)
+            attended = right_dot(branch_ref[...], wo_ref[cols, :])
+            gs_ref[:, cols] = (attended * over_ref[:, cols]).astype(low)
+
+
+def middle_part(alow, over, wo, wgu, wd, tokens, cotangent, gains):
+    low, f32 = jnp.bfloat16, jnp.float32
+    rows, width = tokens.shape
+    hidden = wd.shape[0]
+    tile = 512
+    steps = hidden // tile
+    shape = jax.ShapeDtypeStruct
+
+    def whole(x):
+        return pl.BlockSpec(x.shape, lambda c: (0,) * len(x.shape))
+
+    def columns(at):
+        return pl.BlockSpec((width, tile), lambda c: (0, at + c))
+
+    chunk = pl.BlockSpec((rows, tile), lambda c: (0, c))
+    outs = [
+        shape((rows, width), low),
+        shape((rows, hidden), low),
+        shape((rows, hidden), low),
+        shape((rows, hidden), low),
+        shape((rows, width), low),
+        shape((rows, width), f32),
+        shape((rows, width), low),
+        shape((width // 128, 128), f32),
+        shape(alow.shape, low),
+    ]
+    return pl.pallas_call(
+        functools.partial(middle_kernel, steps),
+        grid=(steps,),
+        in_specs=[
+            whole(alow),
+            whole(over),
+            whole(wo),
+            columns(0),
+            columns(steps),
+            pl.BlockSpec((tile, width), lambda c: (c, 0)),
+            whole(tokens),
+            whole(cotangent),
+            whole(gains),
+        ],
+        out_specs=[whole(outs[0])] + [chunk] * 3 + [whole(x) for x in outs[4:]],
+        out_shape=outs,
+        scratch_shapes=[pltpu.VMEM((rows, width), f32)] * 3 + [pltpu.VMEM((rows, 128), f32)],
+        compiler_params=pltpu.CompilerParams(vmem_limit_bytes=60 * 2**20),
+        name="middle",
+    )(alow, over, wo, wgu, wgu, wd, tokens, cotangent, gains)
+
+
 def scatter_kernel(grid, portions, layouts, n, *refs):
     srcs, outs, scratch = refs[:n], refs[n : 2 * n], list(refs[2 * n : -3])
     load, send, recv = [Pool(x) for x in refs[-3:]]
@@ -1225,20 +1387,21 @@
     low = jnp.bfloat16
 
     device = lax.axis_index("ctx") * lax.axis_size("fsdp") + lax.axis_index("fsdp")
-    gains = jnp.zeros((width // 128 * 2 + 16) * 128, low)
-    for at, x in ((0, attn_gain), (width, mlp_gain), (2 * width, query_gain), (2 * width + HD, key_gain)):
-        gains = lax.dynamic_update_slice_in_dim(gains, x, at + device * x.shape[0], 0)
-    gains = gains.reshape(-1, 128)
+    gain_pieces = [
+        (at, x.shape[0])
+        for at, x in ((0, attn_gain), (width, mlp_gain), (2 * width, query_gain), (2 * width + HD, key_gain))
+    ]
+    gain_lines = jnp.concatenate(
+        [
+            jnp.pad(x.astype(jnp.float32).reshape(1, -1), ((0, 0), (0, 128 - x.shape[0])))
+            for x in (attn_gain, mlp_gain, query_gain, key_gain)
+        ]
+    )
     hidden_width = gate_weight.shape[1]
 
     place = lax.axis_index("ctx")
     blocks = block_map.reshape(-1)
     own_blocks = lax.dynamic_slice_in_dim(blocks, 2 * place, 2, 0)
-    numbers = jnp.arange(2 * pairs, dtype=jnp.int32)
-    slots = jnp.sum(jnp.where(blocks[None, :] == numbers[:, None], numbers[None, :], 0), axis=1)
-    high_slot = (own_blocks[1] > own_blocks[0]).astype(jnp.int32)
-    table = jnp.concatenate([slots, high_slot[None], jnp.max(own_blocks)[None]]).astype(jnp.int32)
-
     spots = (own_blocks[:, None] * BLK + jnp.arange(BLK, dtype=jnp.int32)).reshape(rows)
     cosine, sine = rope_tables(spots)
     turned = jnp.concatenate([-sine[:, : HD // 2], sine[:, HD // 2 :]], axis=1)
@@ -1276,14 +1439,16 @@
     ) = front(
         grid,
         plan,
-        (query_weight, key_weight, value_weight, output_weight, gate_weight, up_weight, down_weight, gains),
+        gain_pieces,
+        (query_weight, key_weight, value_weight, output_weight, gate_weight, up_weight, down_weight),
+        gain_lines,
         tokens.reshape(rows, width),
         cosine,
         turned,
     )
-    attended, attended_low, totals = attention(table, pairs, query_low, key_all, value_all)
+    attended, attended_low, over_totals = attention(blocks, pairs, query_low, key_all, value_all)
     lanes = width // 128
-    gain_one, gain_two = gains[:lanes].reshape(-1), gains[lanes : 2 * lanes].reshape(-1)
+    gain_one = gains[:lanes].reshape(-1)
     query_scale, key_scale = gains[2 * lanes], gains[2 * lanes + 1]
     inverse_rows = inverse_one
     inverse_one = inverse_one[:, :1]
@@ -1297,39 +1462,29 @@
     query_unit = query_raw * query_inverse
     key_inverse = lax.rsqrt(jnp.mean(key_raw * key_raw, axis=-1, keepdims=True) + EPSILON)
     key_unit = key_raw * key_inverse
-    row_totals = totals.reshape(KVH, 2, ratio, BLK).transpose(1, 3, 0, 2).reshape(rows, H, 1)
-    middle = inputs + plain_dot(attended_low, full_output)
-    inverse_two = lax.rsqrt(jnp.mean(middle * middle, axis=-1, keepdims=True) + EPSILON)
-    normal_two = middle * inverse_two
-    normed_two = (normal_two * gain_two).astype(low)
-    both = plain_dot(normed_two, full_gu)
-    gate, upper = both[:, :hidden_width], both[:, hidden_width:]
-    sigmoid_gate = jax.nn.sigmoid(gate)
-    activated = gate * sigmoid_gate
-    hidden = (activated * upper).astype(low)
-    output = (middle + plain_dot(hidden, full_down)).astype(low).reshape(groups, rows, width)
-
     upstream = cotangent.reshape(rows, width)
-    grad_hidden = right_dot(upstream, full_down)
-    grad_gate = (grad_hidden * upper * sigmoid_gate * (1.0 + gate * (1.0 - sigmoid_gate))).astype(low)
-    grad_upper = (grad_hidden * activated).astype(low)
-    grad_both = jnp.concatenate([grad_gate, grad_upper], axis=1)
+    (
+        output,
+        hidden,
+        grad_gate,
+        grad_upper,
+        normed_two,
+        grad_middle,
+        branch_grad,
+        grad_gain_two,
+        grad_summed,
+    ) = middle_part(
+        attended_low, over_totals, full_output, full_gu, full_down, tokens.reshape(rows, width), upstream, gains
+    )
+    output = output.reshape(groups, rows, width)
+    grad_gain_two = grad_gain_two.reshape(width)
     normed_other, upstream_other = swapped(normed_two), swapped(upstream)
     grad_down = chip_sums(hidden, swapped(hidden), upstream, upstream_other)
     grad_g = chip_sums(normed_two, normed_other, grad_gate, swapped(grad_gate))
     grad_u = chip_sums(normed_two, normed_other, grad_upper, swapped(grad_upper))
-    grad_normed_two = right_dot(grad_both, full_gu)
-    grad_gain_two = jnp.sum(grad_normed_two * normal_two, axis=0)
-    grad_middle = upstream.astype(jnp.float32) + norm_back(grad_normed_two, normal_two, inverse_two, gain_two)
-    f32 = jnp.float32
-    branch_grad = grad_middle.astype(low)
     grad_woutput = chip_sums(attended_low, swapped(attended_low), branch_grad, swapped(branch_grad))
-    grad_attended = right_dot(branch_grad, full_output).reshape(rows, H, HD)
-    grad_summed = (grad_attended / row_totals).astype(low).reshape(rows, H * HD)
-    drift = jnp.sum(grad_attended * attended.reshape(rows, H, HD), axis=-1) / row_totals[..., 0]
-    drift = drift.reshape(2, BLK, KVH, ratio).transpose(2, 0, 3, 1).reshape(KVH, 2, ratio * BLK)
     grad_query, grad_keys, grad_values = attention_back(
-        table, pairs, query_low, key_all, value_all, grad_summed, drift
+        blocks, pairs, query_low, key_all, value_all, grad_summed, attended
     )
     back_plan = (
         (("d", 0, width // 2, ABF), ("d", width // 2, width, BAF)),

time: 491 us -> 462 us (0.941)
  matrix products: 34.7 us -> 0 us
  Pallas kernels: 430 us -> 448 us
  local copies, waits for them, and re-layouts: 13.3 us -> 6.03 us
    dot_general x6 -> x0, matrix products: 34.7 us -> none  [the longest x3 18.3 us: right_dot(): lax.dot_general(left, right, (((1,), (1,)), ((), ())), preferred_element_...]
    pallas_call x5 -> x6, Pallas kernels: 203 us -> 219 us  [the longest x1 172 us: front(): pl.pallas_call(functools.partial(front_kernel, grid, plan, pieces), out_s...]
    reshape x2 -> x0, local copies, waits for them, and re-layouts: 5.21 us -> none  [the longest x1 2.91 us: on_device(): attended.reshape(rows, H, HD)]
  transfers between devices with their start and end apart: 7 -> 7, of which waited for: 0 -> 1; matrix products, arithmetic and copies ran while one was open for 9% -> 0% of each run, Pallas kernels for 11% -> 15%
where the time goes in v5:
time: 462 us; the launch traced here: 461 us
  Pallas kernels  448 us (97%)
  local copies, waits for them, and re-layouts  6.03 us (1%)
    pallas_call x1, Pallas kernels, back(): pl.pallas_call(functools.partial(back_kernel, grid, plan), out_shape=[sha...  184 us
    pallas_call x1, Pallas kernels, front(): pl.pallas_call(functools.partial(front_kernel, grid, plan, pieces), out_s...  172 us
    pallas_call x1, Pallas kernels, attention_back(): pl.pallas_call(functools.partial(attention_back_kernel, pairs), grid_spec...  28.5 us
    pallas_call x4, Pallas kernels, chip_sums(): pl.pallas_call(functools.partial(sums_kernel, count), grid_spec=pltpu.Pre...  24.1 us
    pallas_call x1, Pallas kernels, middle_part(): pl.pallas_call(functools.partial(middle_kernel, steps), grid=(steps,), in...  23.1 us
    pallas_call x1, Pallas kernels, attention(): pl.pallas_call(functools.partial(attention_kernel, pairs), grid_spec=pltp...  13.2 us
  transfers between devices with their start and end apart: 7, of which 1 were waited for; matrix products, arithmetic and copies ran while one was open for 0% of the time, Pallas kernels for 15%

profile of v5, /device:TPU:0, one launch (start us, length us, event | category | flops | bytes accessed | tf_op | source)
XLA Modules:
  0.0 461.2 jit_solution(6843220128302575610)
XLA Ops:
  0.7 0.7 multiply_bitcast_fusion
  1.5 0.5 fusion
  2.0 0.8 pad_maximum_fusion
  2.9 1.3 fusion.9.refs_7_
  4.1 172.1 %front.1 = (bf16[2,2,2,4,32,4096]{5,4,3,2,1,0:T(8,128)(2,1)}, bf16[2,2,2,4,64,1024]{5,4,3,2,1,0:T(8,128)(2,1)}, bf16[2,2,2,4,32,6144]{5,4,3,2,1,0:T(8,128)(2,1)}...) custom-call(bf16[32,2048]{1,0:T(8,128)(2,1)} %refs_0_.1, ...), custom_call_target="tpu_custom_call" | custom-call | tf_op jit(solution)/shard_map/front/pallas_call | solution.py:790
  176.3 13.2 %attention.1 = (f32[256,2048]{1,0:T(8,128)}, bf16[256,2048]{1,0:T(8,128)(2,1)}, f32[256,2048]{1,0:T(8,128)}) custom-call(s32[16]{0:T(128)} %bitcast.48, bf16[256,2048]{1,0:T(8,128)(2,1)} %get-tuple-element.56.q_ref, bf16[2048,1024]{1,0:T(8,128)(2,1)} %bitcast.41, bf16[2048,1024]{1,0:T(8,128)(2,1)} %bitcast.43), custom_call_target="tpu_custom_call" | custom-call | tf_op jit(solution)/shard_map/attention/pallas_call | solution.py:497
  189.4 0.7 collective-permute-start.5
  190.1 23.1 %middle.1 = (bf16[256,1024]{1,0:T(8,128)(2,1)}, bf16[256,3072]{1,0:T(8,128)(2,1)}, bf16[256,3072]{1,0:T(8,128)(2,1)}, bf16[256,3072]{1,0:T(8,128)(2,1)}, bf16[25...) custom-call(bf16[256,2048]{1,0:T(8,128)(2,1)} %get-tuple-element.59., ...), custom_call_target="tpu_custom_call" | custom-call | tf_op jit(solution)/shard_map/middle/pallas_call | solution.py:1271
  213.3 0.5 collective-permute-start.2
  213.9 0.4 collective-permute-start.3
  214.3 1.1 collective-permute-done.6.right_other
  215.6 0.7 copy-done.4
  216.4 28.5 %attention_back.1 = (f32[256,2048]{1,0:T(8,128)}, bf16[2048,1024]{1,0:T(8,128)(2,1)}, bf16[2048,1024]{1,0:T(8,128)(2,1)}) custom-call(s32[16]{0:T(128)} %bitcast.49, bf16[256,2048]{1,0:T(8,128)(2,1)} %get-tuple-element.56.q_ref, bf16[2048,1024]{1,0:T(8,128)(2,1)} %bitcast.42, bf16[2048,1024]{1,0:T(8,128)(2,1)} %bitcast.44, ...), custom_call_target="tpu_custom_call" | custom-call | flops 12079595520 | bytes 24117248 | tf_op jit(solution)/shard_map/attention_back/pallas_call | solution.py:562
  244.9 4.5 chip_sums.7
  249.4 0.8 copy-done.1
  250.2 6.9 %chip_sums.5 = bf16[512,3072]{1,0:T(8,128)(2,1)} custom-call(s32[1]{0:T(128)} %bitcast.15.core, bf16[256,1024]{1,0:T(8,128)(2,1)} %get-tuple-element.66.left, bf16[256,1024]{1,0:T(8,128)(2,1)} %copy-done.1, bf16[256,3072]{1,0:T(8,128)(2,1)} %get-tuple-element.68.right, bf16[256,3072]{1,0:T(8,128)(2,1)} %collective-permute-done.2.right_other), custom_call_target="tpu_custom_call" | custom-call | tf_op jit(solution)/shard_map/chip_sums/pallas_call | solution.py:861
  257.1 7.0 %chip_sums.4 = bf16[512,3072]{1,0:T(8,128)(2,1)} custom-call(s32[1]{0:T(128)} %bitcast.15.core, bf16[256,1024]{1,0:T(8,128)(2,1)} %get-tuple-element.66.left, bf16[256,1024]{1,0:T(8,128)(2,1)} %copy-done.1, bf16[256,3072]{1,0:T(8,128)(2,1)} %get-tuple-element.67.right, bf16[256,3072]{1,0:T(8,128)(2,1)} %collective-permute-done.1.right_other), custom_call_target="tpu_custom_call" | custom-call | tf_op jit(solution)/shard_map/chip_sums/pallas_call | solution.py:861
  264.0 0.8 copy-done.3
  264.8 1.2 copy-done.2
  266.0 5.7 %chip_sums.6 = bf16[1536,1024]{1,0:T(8,128)(2,1)} custom-call(s32[1]{0:T(128)} %bitcast.15.core, bf16[256,3072]{1,0:T(8,128)(2,1)} %get-tuple-element.69.left, bf16[256,3072]{1,0:T(8,128)(2,1)} %copy-done.2, bf16[256,1024]{1,0:T(8,128)(2,1)} %bitcast.46, bf16[256,1024]{1,0:T(8,128)(2,1)} %copy-done.3), custom_call_target="tpu_custom_call" | custom-call | tf_op jit(solution)/shard_map/chip_sums/pallas_call | solution.py:861
  271.8 183.7 %back.1 = (f32[32,3072]{1,0:T(8,128)}, f32[32,3072]{1,0:T(8,128)}, f32[96,1024]{1,0:T(8,128)}, f32[64,1024]{1,0:T(8,128)}, f32[32,2048]{1,0:T(8,128)}, /*index=5...) custom-call(bf16[2,2,4,32,3072]{4,3,2,1,0:T(8,128)(2,1)} %bitcast.30, ...), custom_call_target="tpu_custom_call" | custom-call | tf_op jit(solution)/shard_map/back/pallas_call | solution.py:1138
  455.5 1.3 fusion.12
  456.8 1.3 fusion.11
  458.1 3.1 handed.1
  (18 shorter events, 0.5 us)
Async XLA Ops:
  189.4 26.1 %collective-permute-start.5 = (bf16[256,2048]{1,0:T(8,128)(2,1)}, bf16[256,2048]{1,0:T(8,128)(2,1)}, u32[]{:S(2)}, u32[]{:S(2)}) collective-permute-start(bf16[256,2048]{1,0:T(8,128)(2,1)} %get-tuple-element.59.alow_ref.left), channel_id=1, source_target_pairs={{0,4},{4,0},{8,12},{12,8},{16,20},{20,16},{24,28},{28,24},{1,5},{5... | collective-permute-start | bytes 3145736 | tf_op jit(solution)/shard_map/ppermute | solution.py:1363
  190.1 25.3 %copy-start = (bf16[1,256,1024]{2,1,0:T(8,128)(2,1)S(1)}, bf16[1,256,1024]{2,1,0:T(8,128)(2,1)}, u32[]{:S(2)}) copy-start(bf16[1,256,1024]{2,1,0:T(8,128)(2,1)} %param.15) | copy-start | bytes 1572868
  213.2 2.2 collective-permute-start.6
  213.3 36.1 %collective-permute-start.2 = (bf16[256,3072]{1,0:T(8,128)(2,1)}, bf16[256,3072]{1,0:T(8,128)(2,1)}, u32[]{:S(2)}, u32[]{:S(2)}) collective-permute-start(bf16[256,3072]{1,0:T(8,128)(2,1)} %get-tuple-element.68.right), channel_id=1, source_target_pairs={{0,4},{4,0},{8,12},{12,8},{16,20},{20,16},{24,28},{28,24},{1,5},{5... | collective-permute-start | bytes 4718600 | tf_op jit(solution)/shard_map/ppermute | solution.py:1363
  213.8 43.3 %collective-permute-start.1 = (bf16[256,3072]{1,0:T(8,128)(2,1)}, bf16[256,3072]{1,0:T(8,128)(2,1)}, u32[]{:S(2)}, u32[]{:S(2)}) collective-permute-start(bf16[256,3072]{1,0:T(8,128)(2,1)} %get-tuple-element.67.right), channel_id=1, source_target_pairs={{0,4},{4,0},{8,12},{12,8},{16,20},{20,16},{24,28},{28,24},{1,5},{5... | collective-permute-start | bytes 4718600 | tf_op jit(solution)/shard_map/ppermute | solution.py:1363
  213.9 50.1 %collective-permute-start.3 = (bf16[256,3072]{1,0:T(8,128)(2,1)}, bf16[256,3072]{1,0:T(8,128)(2,1)S(1)}, u32[]{:S(2)}, u32[]{:S(2)}) collective-permute-start(bf16[256,3072]{1,0:T(8,128)(2,1)} %get-tuple-element.69.left), channel_id=1, source_target_pairs={{0,4},{4,0},{8,12},{12,8},{16,20},{20,16},{24,28},{28,24},{1,5},{5... | collective-permute-start | bytes 4718600 | tf_op jit(solution)/shard_map/ppermute | solution.py:1363
  215.4 0.8 copy-start.4
  215.4 48.6 %collective-permute-start.4 = (bf16[256,1024]{1,0:T(8,128)(2,1)S(1)}, bf16[256,1024]{1,0:T(8,128)(2,1)S(1)}, u32[]{:S(2)}, u32[]{:S(2)}) collective-permute-start(bf16[256,1024]{1,0:T(8,128)(2,1)S(1)} %bitcast.47), channel_id=1, source_target_pairs={{0,4},{4,0},{8,12},{12,8},{16,20},{20,16},{24,28},{28,24},{1,5},{5... | collective-permute-start | bytes 1572872 | tf_op jit(solution)/shard_map/ppermute | solution.py:1363
  216.2 33.2 %collective-permute-start = (bf16[256,1024]{1,0:T(8,128)(2,1)}, bf16[256,1024]{1,0:T(8,128)(2,1)S(1)}, u32[]{:S(2)}, u32[]{:S(2)}) collective-permute-start(bf16[256,1024]{1,0:T(8,128)(2,1)} %get-tuple-element.66.left), channel_id=1, source_target_pairs={{0,4},{4,0},{8,12},{12,8},{16,20},{20,16},{24,28},{28,24},{1,5},{5... | collective-permute-start | bytes 1572872 | tf_op jit(solution)/shard_map/ppermute | solution.py:1363
  249.4 0.8 copy-start.1
  264.0 0.8 copy-start.3
  264.8 1.2 copy-start.2

commit v6 on v5

--- a/solution.py
+++ b/solution.py
@@ -94,51 +94,55 @@
             return {"fsdp": place}
         return {"ctx": self.c + (place - self.at[axis]) * self.stride[axis]}
 
-    def sources(self, axis):
-        n, p = self.sizes[axis], self.at[axis]
-        if n == 2:
-            return [(None, 1 - p, None, None)]
-        found = []
-        for step in range(1, n):
-            for way in (1, -1):
-                origin = p - way * step
-                onward = p + way
-                found.append(
-                    (
-                        jnp.logical_and(origin >= 0, origin < n),
-                        origin,
-                        onward,
-                        jnp.logical_and(
-                            jnp.logical_and(origin >= 0, origin < n),
-                            jnp.logical_and(onward >= 0, onward < n),
-                        ),
-                    )
-                )
-        return found
-
-    def around(self, axis):
-        n, p = self.sizes[axis], self.at[axis]
-        if n == 2:
-            return [(None, 1 - p)]
-        return [(p + 1 < n, p + 1), (p >= 1, p - 1)]
-
-    def spread(self, axis):
-        n, p = self.sizes[axis], self.at[axis]
-        if n == 2:
-            return [p, 1 - p]
-        order = [0]
-        for step in range(1, n):
-            for way in (step, n - step):
-                if way not in order:
-                    order.append(way)
-        return [lax.rem(p + s, n) for s in order]
-
     def others(self, axis):
         n, p = self.sizes[axis], self.at[axis]
         return [1 - p] if n == 2 else [lax.rem(p + step, n) for step in range(1, n)]
 
     def nearest(self, axis):
         return [self.at[axis]] + self.others(axis)
+
+
+class Pairs:
+    def __init__(self, ctx, fsdp):
+        self.bits = {"b": ("b",), "core": ("core",)}
+        self.stride = {"b": ("ctx", 2), "core": ("ctx", 1)}
+        for axis, name, count, unit in (("a", "ctx", ctx // 4, 4), ("f", "fsdp", fsdp, 1)):
+            bits = []
+            for k in reversed(range(count.bit_length() - 1)):
+                bits.append(f"{axis}{k}")
+                self.stride[bits[-1]] = (name, unit << k)
+            self.bits[axis] = tuple(bits)
+        self.sizes = dict.fromkeys(self.stride, 2)
+
+    def axes(self, order):
+        return tuple(bit for axis in order for bit in self.bits[axis])
+
+    def shape(self, order):
+        return (2,) * len(self.axes(order))
+
+    def enter(self):
+        self.index = {"ctx": lax.axis_index("ctx"), "fsdp": lax.axis_index("fsdp")}
+        self.at = {}
+        for bit, (name, unit) in self.stride.items():
+            self.at[bit] = lax.rem(self.index[name] // unit, 2)
+
+    def barrier(self):
+        sem = pltpu.get_barrier_semaphore()
+        for bit in self.stride:
+            pl.semaphore_signal(
+                sem, inc=1, device_id=self.peer(bit, 1 - self.at[bit]), device_id_type=MESH
+            )
+        pl.semaphore_wait(sem, len(self.stride))
+
+    def peer(self, axis, place):
+        name, unit = self.stride[axis]
+        return {name: self.index[name] + (place - self.at[axis]) * unit}
+
+    def others(self, axis):
+        return [1 - self.at[axis]]
+
+    def nearest(self, axis):
+        return [self.at[axis], 1 - self.at[axis]]
 
 
 class Pool:
@@ -149,13 +153,6 @@
         first = self.used
         self.used += count
         return self.ref.at[pl.ds(first, count)]
-
-
-def guarded(cond, body):
-    if cond is None:
-        body()
-    else:
-        pl.when(cond)(body)
 
 
 class Gather:
@@ -163,19 +160,15 @@
         self.grid, self.order, self.src, self.dst = grid, order, src, dst
         self.columns, self.send_sem, self.recv_sem = columns, send_sem, recv_sem
         self.layout_axes = layout_axes
-        self.sends = 0
         self.pending = []
 
     @staticmethod
     def semaphores(grid, order):
-        near = {x: 1 if grid.sizes[x] == 2 else 2 for x in order}
-        far = {x: 0 if grid.sizes[x] == 2 else 2 * (grid.sizes[x] - 1) for x in order}
-        sends = near[order[0]] + far[order[0]] + sum(near[x] for x in order[1:])
-        inner = 1
+        near = {x: grid.sizes[x] - 1 for x in order}
+        sends, inner = sum(near.values()), 1
         for level in range(1, len(order)):
             axis = order[level]
-            onward = sum(near[x] for x in order[level + 1 :])
-            sends += inner * (far[axis] + max(far[axis], 1) * onward)
+            sends += inner * near[axis] * sum(near[x] for x in order[level + 1 :])
             inner *= grid.sizes[axis]
         return sends, grid.sizes[order[0]] + inner
 
@@ -189,22 +182,17 @@
             number = number * self.grid.sizes[x] + places[x]
         return number
 
-    def start(self, cond, view, axis, place, sem):
-        slot = self.sends
-        self.sends += 1
-
-        def make():
-            return pltpu.make_async_remote_copy(
-                src_ref=view[0],
-                dst_ref=view[1],
-                send_sem=self.send_sem.at[slot],
-                recv_sem=self.recv_sem.at[sem],
-                device_id=self.grid.peer(axis, place),
-                device_id_type=MESH,
-            )
-
-        guarded(cond, lambda: make().start())
-        self.pending.append((cond, make))
+    def start(self, source, view, axis, place, sem):
+        copy = pltpu.make_async_remote_copy(
+            src_ref=source,
+            dst_ref=view,
+            send_sem=self.send_sem.at[len(self.pending)],
+            recv_sem=self.recv_sem.at[sem],
+            device_id=self.grid.peer(axis, place),
+            device_id_type=MESH,
+        )
+        copy.start()
+        self.pending.append(copy)
 
     def wait_recv(self, view, sem):
         pltpu.make_async_remote_copy(
@@ -221,48 +209,38 @@
 
     def open(self):
         axis = self.order[0]
-        own = self.view(self.own_places())
-        for cond, place in self.grid.around(axis):
-            self.start(cond, (self.src, own), axis, place, self.grid.at[axis])
+        for place in self.grid.others(axis):
+            self.start(self.src, self.view(self.own_places()), axis, place, self.grid.at[axis])
 
     def first(self):
         axis = self.order[0]
-        for cond, origin, onward, more in self.grid.sources(axis):
-            view = self.view({**self.own_places(), axis: origin})
-            guarded(cond, lambda: self.wait_recv(view, origin))
-            if onward is not None:
-                self.start(more, (view, view), axis, onward, origin)
-        self.pass_on(None, 1, {x: self.grid.at[x] for x in self.order[1:]})
-
-    def pass_on(self, cond, level, places):
-        n1 = self.grid.sizes[self.order[0]]
-        sem = n1 + self.unit_number(places)
+        for origin in self.grid.others(axis):
+            self.wait_recv(self.view({**self.own_places(), axis: origin}), origin)
+        self.pass_on(1, {x: self.grid.at[x] for x in self.order[1:]})
+
+    def pass_on(self, level, places):
+        sem = self.grid.sizes[self.order[0]] + self.unit_number(places)
         view = self.view(places)
         for axis in self.order[level:]:
-            for near, place in self.grid.around(axis):
-                both = near if cond is None else cond if near is None else jnp.logical_and(cond, near)
-                self.start(both, (view, view), axis, place, sem)
+            for place in self.grid.others(axis):
+                self.start(view, view, axis, place, sem)
 
     def arrivals(self, level):
         n1 = self.grid.sizes[self.order[0]]
         axis = self.order[level]
         inner = [{}]
         for x in self.order[1:level]:
-            inner = [{**places, x: j} for places in inner for j in self.grid.spread(x)]
+            inner = [{**places, x: j} for places in inner for j in self.grid.nearest(x)]
         fixed = {x: self.grid.at[x] for x in self.order[level + 1 :]}
         for places in inner:
-            for cond, origin, onward, more in self.grid.sources(axis):
+            for origin in self.grid.others(axis):
                 unit = {**places, **fixed, axis: origin}
-                view = self.view(unit)
-                sem = n1 + self.unit_number(unit)
-                guarded(cond, lambda: self.wait_recv(view, sem))
-                if onward is not None:
-                    self.start(more, (view, view), axis, onward, sem)
-                self.pass_on(cond, level + 1, unit)
+                self.wait_recv(self.view(unit), n1 + self.unit_number(unit))
+                self.pass_on(level + 1, unit)
 
     def close(self):
-        for cond, make in self.pending:
-            guarded(cond, lambda: make().wait_send())
+        for copy in self.pending:
+            copy.wait_send()
 
 
 def add_into(total, terms, out=None):
@@ -599,6 +577,7 @@
 CORE = ("core",)
 
 
+PUMP = (6, 1, 2, 2)
 FRONT_SRC = ("q", "k", "v", "o", "g", "u", "d", "gains")
 
 
@@ -617,7 +596,7 @@
     grid.enter()
     grid.barrier()
     send, recv = Pool(send), Pool(recv)
-    device = grid.c * grid.sizes["f"] + grid.at["f"]
+    device = grid.index["ctx"] * 2 ** len(grid.bits["f"]) + grid.index["fsdp"]
     block_rows = lax.broadcasted_iota(jnp.int32, gmine.shape, 0)
     block = jnp.zeros(gmine.shape, jnp.float32)
     for i, (at, size) in enumerate(pieces):
@@ -636,7 +615,7 @@
     hidden = src["g"].shape[1]
     spans.update({"o": (wo_ref, 0), "g": (wgu_ref, 0), "u": (wgu_ref, hidden), "d": (wd_ref, 0)})
     spans["gains"] = (allgains_ref, 0)
-    mine = tuple(grid.at[x] for x in ALL_AXES)
+    mine = tuple(grid.at[x] for x in grid.axes(ALL_AXES))
 
     def own_copy(i, name):
         dst, at = spans[name]
@@ -649,10 +628,12 @@
 
     def part(name, low, high, order):
         dst, at = spans[name]
+        order = grid.axes(order)
         sends, takes = Gather.semaphores(grid, order)
         columns = pl.ds(at + low, high - low)
         return Gather(
-            grid, order, src[name].at[:, low:high], dst, columns, send.take(sends), recv.take(takes), ALL_AXES
+            grid, order, src[name].at[:, low:high], dst, columns, send.take(sends), recv.take(takes),
+            grid.axes(ALL_AXES),
         )
 
     early = [part(*p) for p in plan[0]]
@@ -673,13 +654,14 @@
 
     for p in early:
         p.first()
-    for level in (1, 2):
+    levels = len(early[0].order)
+    for level in range(1, levels - 1):
         for p in early:
             p.arrivals(level)
     pump = []
     for p in late:
         pump.append(p.first)
-    for level in (1, 2, 3):
+    for level in range(1, levels):
         for p in late:
             pump.append(functools.partial(p.arrivals, level))
 
@@ -688,11 +670,11 @@
             if pump:
                 pump.pop(0)()
 
-    step(len(late))
+    step(PUMP[0])
     for p in early:
-        p.arrivals(3)
-
-    places = math.prod(grid.sizes[x] for x in ALL_AXES)
+        p.arrivals(levels - 1)
+
+    places = math.prod(grid.shape(ALL_AXES))
     copy = pltpu.make_async_copy(allgains_ref, gbuf, load.at[0])
     copy.start()
     big = pltpu.make_async_copy(wqkv_ref, weights, load.at[1])
@@ -707,7 +689,7 @@
         part_of = tokens_ref[:, cols].astype(jnp.float32) * inv_ref[...] * gains_ref[j : j + 1, :]
         normed_ref[:, cols] = part_of.astype(jnp.bfloat16)
     big.wait()
-    step(1)
+    step(PUMP[1])
     flat = weights.reshape(width, weights.shape[-1])
     normed = normed_ref[...]
     chunk = 2 * HD
@@ -742,12 +724,14 @@
     loop(KVH // 2, to_values)
 
     def pair(source, dst, order):
+        order = grid.axes(order)
         sends, takes = Gather.semaphores(grid, order)
         return Gather(
-            grid, order, source, dst, pl.ds(0, KVH * HD), send.take(sends), recv.take(takes), SLOT_AXES
+            grid, order, source, dst, pl.ds(0, KVH * HD), send.take(sends), recv.take(takes),
+            grid.axes(SLOT_AXES),
         )
 
-    slot = tuple(grid.at[x] for x in SLOT_AXES)
+    slot = tuple(grid.at[x] for x in grid.axes(SLOT_AXES))
     slabs = [pair(klow, k_out, AB), pair(vlow, v_out, BA)]
     saves = [
         pltpu.make_async_copy(klow, k_out.at[slot], load.at[0]),
@@ -756,18 +740,20 @@
     for p, save in zip(slabs, saves):
         p.open()
         save.start()
-    step(2)
+    step(PUMP[2])
     loop(KVH // 2, functools.partial(heads, qlow_ref, 2 * lanes, 0, 0))
     for p, save in zip(slabs, saves):
         save.wait()
         p.first()
-    step(2)
+    step(PUMP[3])
     loop(KVH // 2, functools.partial(heads, qlow_ref, 2 * lanes, H * HD // 2, H * HD // 2))
-    for p in slabs:
-        p.arrivals(1)
+    depth = len(slabs[0].order)
+    for level in range(1, depth - 1):
+        for p in slabs:
+            p.arrivals(level)
     step(len(pump))
     for p in slabs:
-        p.arrivals(2)
+        p.arrivals(depth - 1)
     for p in early + late + slabs:
         p.close()
 
@@ -775,15 +761,15 @@
 def front(grid, plan, pieces, blocks, gain_rows, tokens, cosine, sine):
     n = len(FRONT_SRC)
     rows, width = tokens.shape
-    places = tuple(grid.sizes[x] for x in ALL_AXES)
-    slots = tuple(grid.sizes[x] for x in SLOT_AXES)
+    places = grid.shape(ALL_AXES)
+    slots = grid.shape(SLOT_AXES)
     gains = jax.ShapeDtypeStruct((width // 128 * 2 + 16, 128), jnp.bfloat16)
     blocks = tuple(blocks) + (gains,)
     by = dict(zip(FRONT_SRC, blocks))
     low, f32 = jnp.bfloat16, jnp.float32
     full = (H + 2 * KVH) * HD
-    counts = [Gather.semaphores(grid, p[3]) for p in plan[0] + plan[1]]
-    counts += [Gather.semaphores(grid, AB), Gather.semaphores(grid, BA)]
+    counts = [Gather.semaphores(grid, grid.axes(p[3])) for p in plan[0] + plan[1]]
+    counts += [Gather.semaphores(grid, grid.axes(x)) for x in (AB, BA)]
     sends, takes = [sum(x) for x in zip(*counts)]
     shape = jax.ShapeDtypeStruct
     vmem = pl.BlockSpec(memory_space=pltpu.VMEM)
@@ -1416,8 +1402,8 @@
             ("v", 0, 2 * half_k, AFB + CORE),
         ),
         (
-            ("o", 0, width // 2, ABF + CORE),
-            ("o", width // 2, width, BAF + CORE),
+            ("o", 0, width // 2, FAB + CORE),
+            ("o", width // 2, width, FBA + CORE),
             ("g", 0, hidden_width, BFA + CORE),
             ("u", 0, hidden_width, AFB + CORE),
             ("d", 0, width // 2, BFA + CORE),
@@ -1437,7 +1423,7 @@
         query_low,
         inverse_one,
     ) = front(
-        grid,
+        Pairs(lax.axis_size("ctx"), lax.axis_size("fsdp")),
         plan,
         gain_pieces,
         (query_weight, key_weight, value_weight, output_weight, gate_weight, up_weight, down_weight),

time: 462 us -> 444 us (0.961)
  Pallas kernels: 448 us -> 430 us
    pallas_call x1, Pallas kernels: 172 us -> 156 us  [front(): pl.pallas_call(functools.partial(front_kernel, grid, plan, pieces), out_s...]
  transfers between devices with their start and end apart: 7 -> 7, of which waited for: 1 -> 1; matrix products, arithmetic and copies ran while one was open for 0% -> 0% of each run, Pallas kernels for 15% -> 16%
where the time goes in v6:
time: 444 us; the launch traced here: 443 us
  Pallas kernels  430 us (97%)
  local copies, waits for them, and re-layouts  6.03 us (1%)
    pallas_call x1, Pallas kernels, back(): pl.pallas_call(functools.partial(back_kernel, grid, plan), out_shape=[sha...  183 us
    pallas_call x1, Pallas kernels, front(): pl.pallas_call(functools.partial(front_kernel, grid, plan, pieces), out_s...  156 us
    pallas_call x1, Pallas kernels, attention_back(): pl.pallas_call(functools.partial(attention_back_kernel, pairs), grid_spec...  28.7 us
    pallas_call x4, Pallas kernels, chip_sums(): pl.pallas_call(functools.partial(sums_kernel, count), grid_spec=pltpu.Pre...  24.1 us
    pallas_call x1, Pallas kernels, middle_part(): pl.pallas_call(functools.partial(middle_kernel, steps), grid=(steps,), in...  22.3 us
    pallas_call x1, Pallas kernels, attention(): pl.pallas_call(functools.partial(attention_kernel, pairs), grid_spec=pltp...  13.2 us
  transfers between devices with their start and end apart: 7, of which 1 were waited for; matrix products, arithmetic and copies ran while one was open for 0% of the time, Pallas kernels for 16%

profile of v6, /device:TPU:0, one launch (start us, length us, event | category | flops | bytes accessed | tf_op | source)
XLA Modules:
  0.0 443.0 jit_solution(12420747053358827397)
XLA Ops:
  0.7 0.7 multiply_bitcast_fusion
  1.5 0.5 fusion
  2.0 0.8 pad_maximum_fusion
  2.9 1.3 fusion.9.refs_7_
  4.1 155.7 %front.1 = (bf16[2,2,2,2,2,32,4096]{6,5,4,3,2,1,0:T(8,128)(2,1)}, bf16[2,2,2,2,2,64,1024]{6,5,4,3,2,1,0:T(8,128)(2,1)}, bf16[2,2,2,2,2,32,6144]{6,5,4,3,2,1,0:T(...) custom-call(bf16[32,2048]{1,0:T(8,128)(2,1)} %refs_0_.1, ...), custom_call_target="tpu_custom_call" | custom-call | tf_op jit(solution)/shard_map/front/pallas_call | solution.py:776
  159.9 13.2 %attention.1 = (f32[256,2048]{1,0:T(8,128)}, bf16[256,2048]{1,0:T(8,128)(2,1)}, f32[256,2048]{1,0:T(8,128)}) custom-call(s32[16]{0:T(128)} %bitcast.48, bf16[256,2048]{1,0:T(8,128)(2,1)} %get-tuple-element.56.q_ref, bf16[2048,1024]{1,0:T(8,128)(2,1)} %bitcast.41, bf16[2048,1024]{1,0:T(8,128)(2,1)} %bitcast.43), custom_call_target="tpu_custom_call" | custom-call | tf_op jit(solution)/shard_map/attention/pallas_call | solution.py:475
  173.0 0.7 collective-permute-start.5
  173.7 22.3 %middle.1 = (bf16[256,1024]{1,0:T(8,128)(2,1)}, bf16[256,3072]{1,0:T(8,128)(2,1)}, bf16[256,3072]{1,0:T(8,128)(2,1)}, bf16[256,3072]{1,0:T(8,128)(2,1)}, bf16[25...) custom-call(bf16[256,2048]{1,0:T(8,128)(2,1)} %get-tuple-element.59., ...), custom_call_target="tpu_custom_call" | custom-call | tf_op jit(solution)/shard_map/middle/pallas_call | solution.py:1257
  196.1 0.5 collective-permute-start.2
  196.7 0.4 collective-permute-start.3
  197.1 1.1 collective-permute-done.6.right_other
  198.4 0.7 copy-done.4
  199.2 28.7 %attention_back.1 = (f32[256,2048]{1,0:T(8,128)}, bf16[2048,1024]{1,0:T(8,128)(2,1)}, bf16[2048,1024]{1,0:T(8,128)(2,1)}) custom-call(s32[16]{0:T(128)} %bitcast.49, bf16[256,2048]{1,0:T(8,128)(2,1)} %get-tuple-element.56.q_ref, bf16[2048,1024]{1,0:T(8,128)(2,1)} %bitcast.42, bf16[2048,1024]{1,0:T(8,128)(2,1)} %bitcast.44, ...), custom_call_target="tpu_custom_call" | custom-call | flops 12079595520 | bytes 24117248 | tf_op jit(solution)/shard_map/attention_back/pallas_call | solution.py:540
  227.8 4.5 %chip_sums.7 = bf16[1024,1024]{1,0:T(8,128)(2,1)} custom-call(s32[1]{0:T(128)} %bitcast.15.core, bf16[256,2048]{1,0:T(8,128)(2,1)} %get-tuple-element.59.alow_ref.left, bf16[256,2048]{1,0:T(8,128)(2,1)} %collective-permute-done.5.left_other, bf16[256,1024]{1,0:T(8,128)(2,1)} %get-tuple-element.70.right, bf16[256,1024]{1,0:T(8,128)(2,1)} %copy-done.4), custom_call_target="tpu_custom_call" | custom-call | tf_op jit(solution)/shard_map/chip_sums/pallas_call | solution.py:847
  232.4 0.8 copy-done.1
  233.2 6.9 %chip_sums.5 = bf16[512,3072]{1,0:T(8,128)(2,1)} custom-call(s32[1]{0:T(128)} %bitcast.15.core, bf16[256,1024]{1,0:T(8,128)(2,1)} %get-tuple-element.66.left, bf16[256,1024]{1,0:T(8,128)(2,1)} %copy-done.1, bf16[256,3072]{1,0:T(8,128)(2,1)} %get-tuple-element.68.right, bf16[256,3072]{1,0:T(8,128)(2,1)} %collective-permute-done.2.right_other), custom_call_target="tpu_custom_call" | custom-call | tf_op jit(solution)/shard_map/chip_sums/pallas_call | solution.py:847
  240.0 7.0 %chip_sums.4 = bf16[512,3072]{1,0:T(8,128)(2,1)} custom-call(s32[1]{0:T(128)} %bitcast.15.core, bf16[256,1024]{1,0:T(8,128)(2,1)} %get-tuple-element.66.left, bf16[256,1024]{1,0:T(8,128)(2,1)} %copy-done.1, bf16[256,3072]{1,0:T(8,128)(2,1)} %get-tuple-element.67.right, bf16[256,3072]{1,0:T(8,128)(2,1)} %collective-permute-done.1.right_other), custom_call_target="tpu_custom_call" | custom-call | tf_op jit(solution)/shard_map/chip_sums/pallas_call | solution.py:847
  247.0 0.8 copy-done.3
  247.8 1.2 copy-done.2
  249.0 5.7 %chip_sums.6 = bf16[1536,1024]{1,0:T(8,128)(2,1)} custom-call(s32[1]{0:T(128)} %bitcast.15.core, bf16[256,3072]{1,0:T(8,128)(2,1)} %get-tuple-element.69.left, bf16[256,3072]{1,0:T(8,128)(2,1)} %copy-done.2, bf16[256,1024]{1,0:T(8,128)(2,1)} %bitcast.46, bf16[256,1024]{1,0:T(8,128)(2,1)} %copy-done.3), custom_call_target="tpu_custom_call" | custom-call | tf_op jit(solution)/shard_map/chip_sums/pallas_call | solution.py:847
  254.7 182.5 %back.1 = (f32[32,3072]{1,0:T(8,128)}, f32[32,3072]{1,0:T(8,128)}, f32[96,1024]{1,0:T(8,128)}, f32[64,1024]{1,0:T(8,128)}, f32[32,2048]{1,0:T(8,128)}, /*index=5...) custom-call(bf16[2,2,4,32,3072]{4,3,2,1,0:T(8,128)(2,1)} %bitcast.30, ...), custom_call_target="tpu_custom_call" | custom-call | tf_op jit(solution)/shard_map/back/pallas_call | solution.py:1124
  437.3 1.3 fusion.12
  438.6 1.3 fusion.11
  439.9 3.1 handed.1
  (18 shorter events, 0.6 us)
Async XLA Ops:
  173.0 25.3 %collective-permute-start.5 = (bf16[256,2048]{1,0:T(8,128)(2,1)}, bf16[256,2048]{1,0:T(8,128)(2,1)}, u32[]{:S(2)}, u32[]{:S(2)}) collective-permute-start(bf16[256,2048]{1,0:T(8,128)(2,1)} %get-tuple-element.59.alow_ref.left), channel_id=1, source_target_pairs={{0,4},{4,0},{8,12},{12,8},{16,20},{20,16},{24,28},{28,24},{1,5},{5... | collective-permute-start | bytes 3145736 | tf_op jit(solution)/shard_map/ppermute | solution.py:1349
  173.7 24.5 %copy-start = (bf16[1,256,1024]{2,1,0:T(8,128)(2,1)S(1)}, bf16[1,256,1024]{2,1,0:T(8,128)(2,1)}, u32[]{:S(2)}) copy-start(bf16[1,256,1024]{2,1,0:T(8,128)(2,1)} %param.15) | copy-start | bytes 1572868
  196.0 2.2 collective-permute-start.6
  196.1 36.2 %collective-permute-start.2 = (bf16[256,3072]{1,0:T(8,128)(2,1)}, bf16[256,3072]{1,0:T(8,128)(2,1)}, u32[]{:S(2)}, u32[]{:S(2)}) collective-permute-start(bf16[256,3072]{1,0:T(8,128)(2,1)} %get-tuple-element.68.right), channel_id=1, source_target_pairs={{0,4},{4,0},{8,12},{12,8},{16,20},{20,16},{24,28},{28,24},{1,5},{5... | collective-permute-start | bytes 4718600 | tf_op jit(solution)/shard_map/ppermute | solution.py:1349
  196.6 43.4 %collective-permute-start.1 = (bf16[256,3072]{1,0:T(8,128)(2,1)}, bf16[256,3072]{1,0:T(8,128)(2,1)}, u32[]{:S(2)}, u32[]{:S(2)}) collective-permute-start(bf16[256,3072]{1,0:T(8,128)(2,1)} %get-tuple-element.67.right), channel_id=1, source_target_pairs={{0,4},{4,0},{8,12},{12,8},{16,20},{20,16},{24,28},{28,24},{1,5},{5... | collective-permute-start | bytes 4718600 | tf_op jit(solution)/shard_map/ppermute | solution.py:1349
  196.7 50.3 %collective-permute-start.3 = (bf16[256,3072]{1,0:T(8,128)(2,1)}, bf16[256,3072]{1,0:T(8,128)(2,1)S(1)}, u32[]{:S(2)}, u32[]{:S(2)}) collective-permute-start(bf16[256,3072]{1,0:T(8,128)(2,1)} %get-tuple-element.69.left), channel_id=1, source_target_pairs={{0,4},{4,0},{8,12},{12,8},{16,20},{20,16},{24,28},{28,24},{1,5},{5... | collective-permute-start | bytes 4718600 | tf_op jit(solution)/shard_map/ppermute | solution.py:1349
  198.2 0.8 copy-start.4
  198.2 48.8 %collective-permute-start.4 = (bf16[256,1024]{1,0:T(8,128)(2,1)S(1)}, bf16[256,1024]{1,0:T(8,128)(2,1)S(1)}, u32[]{:S(2)}, u32[]{:S(2)}) collective-permute-start(bf16[256,1024]{1,0:T(8,128)(2,1)S(1)} %bitcast.47), channel_id=1, source_target_pairs={{0,4},{4,0},{8,12},{12,8},{16,20},{20,16},{24,28},{28,24},{1,5},{5... | collective-permute-start | bytes 1572872 | tf_op jit(solution)/shard_map/ppermute | solution.py:1349
  199.0 33.3 %collective-permute-start = (bf16[256,1024]{1,0:T(8,128)(2,1)}, bf16[256,1024]{1,0:T(8,128)(2,1)S(1)}, u32[]{:S(2)}, u32[]{:S(2)}) collective-permute-start(bf16[256,1024]{1,0:T(8,128)(2,1)} %get-tuple-element.66.left), channel_id=1, source_target_pairs={{0,4},{4,0},{8,12},{12,8},{16,20},{20,16},{24,28},{28,24},{1,5},{5... | collective-permute-start | bytes 1572872 | tf_op jit(solution)/shard_map/ppermute | solution.py:1349
  232.4 0.8 copy-start.1
  247.0 0.8 copy-start.3
  247.8 1.2 copy-start.2

commit v7 on v6

--- a/solution.py
+++ b/solution.py
@@ -858,20 +858,28 @@
     )(core, left, left_other, right, right_other)
 
 
-def handed_kernel(*refs):
-    for source, out in zip(refs[: len(refs) // 2], refs[len(refs) // 2 :]):
+def handed_kernel(pieces, count, sums_ref, *refs):
+    results, outs = refs[: (len(refs) - len(pieces)) // 2], refs[(len(refs) - len(pieces)) // 2 :]
+    for source, out in zip(results, outs):
         out[...] = source[...]
-
-
-def handed(*results):
+    device = lax.axis_index("ctx") * count + lax.axis_index("fsdp")
+    for (at, size), out in zip(pieces, outs[len(results) :]):
+        spot = at + device * size
+        line = jnp.broadcast_to(sums_ref[pl.ds(spot // 128, 1), :], (8, 128))
+        line = pltpu.roll(line, lax.rem(128 - lax.rem(spot, 128), 128), 1)
+        out[...] = line[:1, :size]
+
+
+def handed(pieces, sums, *results):
     vmem = pl.BlockSpec(memory_space=pltpu.VMEM)
     return pl.pallas_call(
-        handed_kernel,
-        out_shape=[jax.ShapeDtypeStruct(x.shape, x.dtype) for x in results],
-        in_specs=[vmem] * len(results),
-        out_specs=[vmem] * len(results),
+        functools.partial(handed_kernel, pieces, lax.axis_size("fsdp")),
+        out_shape=[jax.ShapeDtypeStruct(x.shape, x.dtype) for x in results]
+        + [jax.ShapeDtypeStruct((1, size), jnp.float32) for _, size in pieces],
+        in_specs=[vmem] * (1 + len(results)),
+        out_specs=[vmem] * (len(results) + len(pieces)),
         name="handed",
-    )(*results)
+    )(sums, *results)
 
 
 BACK_SUMS = ("g", "u", "d", "o")
@@ -1406,8 +1414,8 @@
             ("o", width // 2, width, FBA + CORE),
             ("g", 0, hidden_width, BFA + CORE),
             ("u", 0, hidden_width, AFB + CORE),
-            ("d", 0, width // 2, BFA + CORE),
-            ("d", width // 2, width, AFB + CORE),
+            ("d", 0, width // 2, ABF + CORE),
+            ("d", width // 2, width, BFA + CORE),
         ),
     )
     (
@@ -1505,25 +1513,31 @@
             grad_middle,
             grad_gain_two.reshape(lanes, 128),
         )
-        out_g, out_u, out_down, out_output, out_q, out_k, out_v, grad_tokens = handed(
-            out_g, out_u, out_down, out_output, out_q, out_k, out_v, grad_tokens
+        (
+            out_g,
+            out_u,
+            out_down,
+            out_output,
+            out_q,
+            out_k,
+            out_v,
+            grad_tokens,
+            *own_gains,
+        ) = handed(
+            gain_pieces, gain_sums, out_g, out_u, out_down, out_output, out_q, out_k, out_v, grad_tokens
         )
-        flat_sums = gain_sums.reshape(-1)
-
-        def own_piece(at, x):
-            return lax.dynamic_slice_in_dim(flat_sums, at + device * x.shape[0], x.shape[0], 0)
-
+        own_attn, own_mlp, own_query, own_key = [x.reshape(-1) for x in own_gains]
         return (
             output,
             grad_tokens.reshape(groups, rows, width),
-            own_piece(0, attn_gain),
+            own_attn,
             out_q,
             out_k,
             out_v,
-            own_piece(2 * width, query_gain),
-            own_piece(2 * width + HD, key_gain),
+            own_query,
+            own_key,
             out_output,
-            own_piece(width, mlp_gain),
+            own_mlp,
             out_g,
             out_u,
             out_down,

time: 444 us -> 440 us (level)
  no operation moved by 1% of the time
where the time goes in v7:
time: 440 us; the launch traced here: 439 us
  Pallas kernels  428 us (97%)
    pallas_call x1, Pallas kernels, back(): pl.pallas_call(functools.partial(back_kernel, grid, plan), out_shape=[sha...  182 us
    pallas_call x1, Pallas kernels, front(): pl.pallas_call(functools.partial(front_kernel, grid, plan, pieces), out_s...  155 us
    pallas_call x1, Pallas kernels, attention_back(): pl.pallas_call(functools.partial(attention_back_kernel, pairs), grid_spec...  28.6 us
    pallas_call x4, Pallas kernels, chip_sums(): pl.pallas_call(functools.partial(sums_kernel, count), grid_spec=pltpu.Pre...  24 us
    pallas_call x1, Pallas kernels, middle_part(): pl.pallas_call(functools.partial(middle_kernel, steps), grid=(steps,), in...  22.2 us
    pallas_call x1, Pallas kernels, attention(): pl.pallas_call(functools.partial(attention_kernel, pairs), grid_spec=pltp...  13.2 us
  transfers between devices with their start and end apart: 7, of which 1 were waited for; matrix products, arithmetic and copies ran while one was open for 0% of the time, Pallas kernels for 16%

profile of v7, /device:TPU:0, one launch (start us, length us, event | category | flops | bytes accessed | tf_op | source)
XLA Modules:
  0.0 439.2 jit_solution(13331378642922771045)
XLA Ops:
  0.7 0.7 multiply_bitcast_fusion
  1.5 0.5 fusion
  2.0 0.8 pad_maximum_fusion
  2.9 1.3 fusion.9.refs_7_
  4.1 155.2 %front.1 = (bf16[2,2,2,2,2,32,4096]{6,5,4,3,2,1,0:T(8,128)(2,1)}, bf16[2,2,2,2,2,64,1024]{6,5,4,3,2,1,0:T(8,128)(2,1)}, bf16[2,2,2,2,2,32,6144]{6,5,4,3,2,1,0:T(...) custom-call(bf16[32,2048]{1,0:T(8,128)(2,1)} %refs_0_.1, ...), custom_call_target="tpu_custom_call" | custom-call | tf_op jit(solution)/shard_map/front/pallas_call | solution.py:776
  159.3 13.2 %attention.1 = (f32[256,2048]{1,0:T(8,128)}, bf16[256,2048]{1,0:T(8,128)(2,1)}, f32[256,2048]{1,0:T(8,128)}) custom-call(s32[16]{0:T(128)} %bitcast.51, bf16[256,2048]{1,0:T(8,128)(2,1)} %get-tuple-element.60.q_ref, bf16[2048,1024]{1,0:T(8,128)(2,1)} %bitcast.44, bf16[2048,1024]{1,0:T(8,128)(2,1)} %bitcast.46), custom_call_target="tpu_custom_call" | custom-call | tf_op jit(solution)/shard_map/attention/pallas_call | solution.py:475
  172.5 0.7 collective-permute-start.5
  173.1 22.2 %middle.1 = (bf16[256,1024]{1,0:T(8,128)(2,1)}, bf16[256,3072]{1,0:T(8,128)(2,1)}, bf16[256,3072]{1,0:T(8,128)(2,1)}, bf16[256,3072]{1,0:T(8,128)(2,1)}, bf16[25...) custom-call(bf16[256,2048]{1,0:T(8,128)(2,1)} %get-tuple-element.63., ...), custom_call_target="tpu_custom_call" | custom-call | tf_op jit(solution)/shard_map/middle/pallas_call | solution.py:1265
  195.4 0.5 collective-permute-start.2
  196.0 0.4 collective-permute-start.3
  196.5 1.1 collective-permute-done.6.right_other
  197.6 0.1 collective-permute-start.4
  197.7 0.7 copy-done.4
  198.4 0.1 collective-permute-start
  198.5 28.6 %attention_back.1 = (f32[256,2048]{1,0:T(8,128)}, bf16[2048,1024]{1,0:T(8,128)(2,1)}, bf16[2048,1024]{1,0:T(8,128)(2,1)}) custom-call(s32[16]{0:T(128)} %bitcast.52, bf16[256,2048]{1,0:T(8,128)(2,1)} %get-tuple-element.60.q_ref, bf16[2048,1024]{1,0:T(8,128)(2,1)} %bitcast.45, bf16[2048,1024]{1,0:T(8,128)(2,1)} %bitcast.47, ...), custom_call_target="tpu_custom_call" | custom-call | flops 12079595520 | bytes 24117248 | tf_op jit(solution)/shard_map/attention_back/pallas_call | solution.py:540
  227.1 4.5 %chip_sums.7 = bf16[1024,1024]{1,0:T(8,128)(2,1)} custom-call(s32[1]{0:T(128)} %bitcast.15.core, bf16[256,2048]{1,0:T(8,128)(2,1)} %get-tuple-element.63.alow_ref.left, bf16[256,2048]{1,0:T(8,128)(2,1)} %collective-permute-done.5.left_other, bf16[256,1024]{1,0:T(8,128)(2,1)} %get-tuple-element.74.right, bf16[256,1024]{1,0:T(8,128)(2,1)} %copy-done.4), custom_call_target="tpu_custom_call" | custom-call | tf_op jit(solution)/shard_map/chip_sums/pallas_call | solution.py:847
  231.7 0.8 copy-done.1
  232.4 6.9 %chip_sums.5 = bf16[512,3072]{1,0:T(8,128)(2,1)} custom-call(s32[1]{0:T(128)} %bitcast.15.core, bf16[256,1024]{1,0:T(8,128)(2,1)} %get-tuple-element.70.left, bf16[256,1024]{1,0:T(8,128)(2,1)} %copy-done.1, bf16[256,3072]{1,0:T(8,128)(2,1)} %get-tuple-element.72.right, bf16[256,3072]{1,0:T(8,128)(2,1)} %collective-permute-done.2.right_other), custom_call_target="tpu_custom_call" | custom-call | tf_op jit(solution)/shard_map/chip_sums/pallas_call | solution.py:847
  239.3 6.9 %chip_sums.4 = bf16[512,3072]{1,0:T(8,128)(2,1)} custom-call(s32[1]{0:T(128)} %bitcast.15.core, bf16[256,1024]{1,0:T(8,128)(2,1)} %get-tuple-element.70.left, bf16[256,1024]{1,0:T(8,128)(2,1)} %copy-done.1, bf16[256,3072]{1,0:T(8,128)(2,1)} %get-tuple-element.71.right, bf16[256,3072]{1,0:T(8,128)(2,1)} %collective-permute-done.1.right_other), custom_call_target="tpu_custom_call" | custom-call | tf_op jit(solution)/shard_map/chip_sums/pallas_call | solution.py:847
  246.2 0.8 copy-done.3
  247.0 1.2 copy-done.2
  248.3 5.7 %chip_sums.6 = bf16[1536,1024]{1,0:T(8,128)(2,1)} custom-call(s32[1]{0:T(128)} %bitcast.15.core, bf16[256,3072]{1,0:T(8,128)(2,1)} %get-tuple-element.73.left, bf16[256,3072]{1,0:T(8,128)(2,1)} %copy-done.2, bf16[256,1024]{1,0:T(8,128)(2,1)} %bitcast.49, bf16[256,1024]{1,0:T(8,128)(2,1)} %copy-done.3), custom_call_target="tpu_custom_call" | custom-call | tf_op jit(solution)/shard_map/chip_sums/pallas_call | solution.py:847
  254.0 181.9 %back.1 = (f32[32,3072]{1,0:T(8,128)}, f32[32,3072]{1,0:T(8,128)}, f32[96,1024]{1,0:T(8,128)}, f32[64,1024]{1,0:T(8,128)}, f32[32,2048]{1,0:T(8,128)}, /*index=5...) custom-call(bf16[2,2,4,32,3072]{4,3,2,1,0:T(8,128)(2,1)} %bitcast.33, ...), custom_call_target="tpu_custom_call" | custom-call | tf_op jit(solution)/shard_map/back/pallas_call | solution.py:1132
  435.9 3.2 handed.1
  (16 shorter events, 0.3 us)
Async XLA Ops:
  172.5 25.2 %collective-permute-start.5 = (bf16[256,2048]{1,0:T(8,128)(2,1)}, bf16[256,2048]{1,0:T(8,128)(2,1)}, u32[]{:S(2)}, u32[]{:S(2)}) collective-permute-start(bf16[256,2048]{1,0:T(8,128)(2,1)} %get-tuple-element.63.alow_ref.left), channel_id=1, source_target_pairs={{0,4},{4,0},{8,12},{12,8},{16,20},{20,16},{24,28},{28,24},{1,5},{5... | collective-permute-start | bytes 3145736 | tf_op jit(solution)/shard_map/ppermute | solution.py:1357
  173.1 24.4 %copy-start = (bf16[1,256,1024]{2,1,0:T(8,128)(2,1)S(1)}, bf16[1,256,1024]{2,1,0:T(8,128)(2,1)}, u32[]{:S(2)}) copy-start(bf16[1,256,1024]{2,1,0:T(8,128)(2,1)} %param.15) | copy-start | bytes 1572868
  195.4 2.2 collective-permute-start.6
  195.4 36.2 %collective-permute-start.2 = (bf16[256,3072]{1,0:T(8,128)(2,1)}, bf16[256,3072]{1,0:T(8,128)(2,1)}, u32[]{:S(2)}, u32[]{:S(2)}) collective-permute-start(bf16[256,3072]{1,0:T(8,128)(2,1)} %get-tuple-element.72.right), channel_id=1, source_target_pairs={{0,4},{4,0},{8,12},{12,8},{16,20},{20,16},{24,28},{28,24},{1,5},{5... | collective-permute-start | bytes 4718600 | tf_op jit(solution)/shard_map/ppermute | solution.py:1357
  195.9 43.4 %collective-permute-start.1 = (bf16[256,3072]{1,0:T(8,128)(2,1)}, bf16[256,3072]{1,0:T(8,128)(2,1)}, u32[]{:S(2)}, u32[]{:S(2)}) collective-permute-start(bf16[256,3072]{1,0:T(8,128)(2,1)} %get-tuple-element.71.right), channel_id=1, source_target_pairs={{0,4},{4,0},{8,12},{12,8},{16,20},{20,16},{24,28},{28,24},{1,5},{5... | collective-permute-start | bytes 4718600 | tf_op jit(solution)/shard_map/ppermute | solution.py:1357
  196.0 50.2 %collective-permute-start.3 = (bf16[256,3072]{1,0:T(8,128)(2,1)}, bf16[256,3072]{1,0:T(8,128)(2,1)S(1)}, u32[]{:S(2)}, u32[]{:S(2)}) collective-permute-start(bf16[256,3072]{1,0:T(8,128)(2,1)} %get-tuple-element.73.left), channel_id=1, source_target_pairs={{0,4},{4,0},{8,12},{12,8},{16,20},{20,16},{24,28},{28,24},{1,5},{5... | collective-permute-start | bytes 4718600 | tf_op jit(solution)/shard_map/ppermute | solution.py:1357
  197.6 0.8 copy-start.4
  197.6 48.7 %collective-permute-start.4 = (bf16[256,1024]{1,0:T(8,128)(2,1)S(1)}, bf16[256,1024]{1,0:T(8,128)(2,1)S(1)}, u32[]{:S(2)}, u32[]{:S(2)}) collective-permute-start(bf16[256,1024]{1,0:T(8,128)(2,1)S(1)} %bitcast.50), channel_id=1, source_target_pairs={{0,4},{4,0},{8,12},{12,8},{16,20},{20,16},{24,28},{28,24},{1,5},{5... | collective-permute-start | bytes 1572872 | tf_op jit(solution)/shard_map/ppermute | solution.py:1357
  198.4 33.3 %collective-permute-start = (bf16[256,1024]{1,0:T(8,128)(2,1)}, bf16[256,1024]{1,0:T(8,128)(2,1)S(1)}, u32[]{:S(2)}, u32[]{:S(2)}) collective-permute-start(bf16[256,1024]{1,0:T(8,128)(2,1)} %get-tuple-element.70.left), channel_id=1, source_target_pairs={{0,4},{4,0},{8,12},{12,8},{16,20},{20,16},{24,28},{28,24},{1,5},{5... | collective-permute-start | bytes 1572872 | tf_op jit(solution)/shard_map/ppermute | solution.py:1357
  231.6 0.8 copy-start.1
  246.2 0.8 copy-start.3
  247.0 1.2 copy-start.2

commit v8 on v7

--- a/solution.py
+++ b/solution.py
@@ -813,7 +813,8 @@
     return flat + [normed, gains, raw, qlow, inverse]
 
 
-def sums_kernel(count, core, left, left_other, right, right_other, out, turned):
+def sums_kernel(count, n, core, left, left_other, *refs):
+    rights, outs, turned = refs[: 2 * n], refs[2 * n : 3 * n], refs[-1]
     rows, width = left.shape
     block = width // count
 
@@ -824,11 +825,12 @@
             for k, ref in enumerate((left, left_other)):
                 turned[j * block : (j + 1) * block, k * rows : (k + 1) * rows] = ref[:, at].T
 
-    rhs = jnp.concatenate([right[...], right_other[...]], axis=0)
-    out[...] = jnp.dot(turned[...], rhs, preferred_element_type=jnp.float32).astype(out.dtype)
-
-
-def chip_sums(left, left_other, right, right_other):
+    for k, out in enumerate(outs):
+        rhs = jnp.concatenate([rights[2 * k][...], rights[2 * k + 1][...]], axis=0)
+        out[...] = jnp.dot(turned[...], rhs, preferred_element_type=jnp.float32).astype(out.dtype)
+
+
+def chip_sums(left, left_other, *rights):
     rows, width = left.shape
     count = lax.axis_size("ctx")
     block = width // count
@@ -840,22 +842,26 @@
             for x in (left, left_other)
         ]
         lhs = jnp.concatenate(halves, axis=0).reshape(2 * rows, width // 2)
-        return left_dot(lhs, jnp.concatenate([right, right_other], axis=0)).astype(jnp.bfloat16)
+        return [
+            left_dot(lhs, jnp.concatenate(rights[k : k + 2], axis=0)).astype(jnp.bfloat16)
+            for k in range(0, len(rights), 2)
+        ]
     core = (lax.axis_index("ctx") % 2).astype(jnp.int32)[None]
+    n, columns = len(rights) // 2, rights[0].shape[1]
     lhs = pl.BlockSpec((rows, width), lambda n, c: (0, 0))
     rhs = pl.BlockSpec((rows, tile), lambda n, c: (0, n))
     return pl.pallas_call(
-        functools.partial(sums_kernel, count),
+        functools.partial(sums_kernel, count, n),
         grid_spec=pltpu.PrefetchScalarGridSpec(
             num_scalar_prefetch=1,
-            grid=(right.shape[1] // tile,),
-            in_specs=[lhs, lhs, rhs, rhs],
-            out_specs=pl.BlockSpec((width // 2, tile), lambda n, c: (0, n)),
+            grid=(columns // tile,),
+            in_specs=[lhs, lhs] + [rhs] * (2 * n),
+            out_specs=[pl.BlockSpec((width // 2, tile), lambda n, c: (0, n))] * n,
             scratch_shapes=[pltpu.VMEM((width // 2, 2 * rows), jnp.bfloat16)],
         ),
-        out_shape=jax.ShapeDtypeStruct((width // 2, right.shape[1]), jnp.bfloat16),
+        out_shape=[jax.ShapeDtypeStruct((width // 2, columns), jnp.bfloat16)] * n,
         name="chip_sums",
-    )(core, left, left_other, right, right_other)
+    )(core, left, left_other, *rights)
 
 
 def handed_kernel(pieces, count, sums_ref, *refs):
@@ -1473,10 +1479,11 @@
     output = output.reshape(groups, rows, width)
     grad_gain_two = grad_gain_two.reshape(width)
     normed_other, upstream_other = swapped(normed_two), swapped(upstream)
-    grad_down = chip_sums(hidden, swapped(hidden), upstream, upstream_other)
-    grad_g = chip_sums(normed_two, normed_other, grad_gate, swapped(grad_gate))
-    grad_u = chip_sums(normed_two, normed_other, grad_upper, swapped(grad_upper))
-    grad_woutput = chip_sums(attended_low, swapped(attended_low), branch_grad, swapped(branch_grad))
+    (grad_down,) = chip_sums(hidden, swapped(hidden), upstream, upstream_other)
+    grad_g, grad_u = chip_sums(
+        normed_two, normed_other, grad_gate, swapped(grad_gate), grad_upper, swapped(grad_upper)
+    )
+    (grad_woutput,) = chip_sums(attended_low, swapped(attended_low), branch_grad, swapped(branch_grad))
     grad_query, grad_keys, grad_values = attention_back(
         blocks, pairs, query_low, key_all, value_all, grad_summed, attended
     )
@@ -1581,7 +1588,7 @@
         ],
         axis=1,
     )
-    grad_wqkv = chip_sums(normed, swapped(normed), grad_raw, swapped(grad_raw))
+    (grad_wqkv,) = chip_sums(normed, swapped(normed), grad_raw, swapped(grad_raw))
     grad_normed = right_dot(grad_raw, full_qkv)
     grad_gain_one = jnp.sum(grad_normed * normal_one, axis=0)
     grad_inputs = grad_middle + norm_back(grad_normed, normal_one, inverse_one, gain_one)

time: 440 us -> 433 us (0.984)
  Pallas kernels: 428 us -> 423 us
    pallas_call x4 -> x3, Pallas kernels: 24 us -> 18.8 us  [chip_sums(): pl.pallas_call(functools.partial(sums_kernel, count, n), grid_spec=pltpu....]
  transfers between devices with their start and end apart: 7 -> 7, of which waited for: 1 -> 1; matrix products, arithmetic and copies ran while one was open for 0% -> 0% of each run, Pallas kernels for 16% -> 14%
where the time goes in v8:
time: 433 us; the launch traced here: 432 us
  Pallas kernels  423 us (98%)
    pallas_call x1, Pallas kernels, back(): pl.pallas_call(functools.partial(back_kernel, grid, plan), out_shape=[sha...  182 us
    pallas_call x1, Pallas kernels, front(): pl.pallas_call(functools.partial(front_kernel, grid, plan, pieces), out_s...  155 us
    pallas_call x1, Pallas kernels, attention_back(): pl.pallas_call(functools.partial(attention_back_kernel, pairs), grid_spec...  28.6 us
    pallas_call x1, Pallas kernels, middle_part(): pl.pallas_call(functools.partial(middle_kernel, steps), grid=(steps,), in...  22.2 us
    pallas_call x3, Pallas kernels, chip_sums(): pl.pallas_call(functools.partial(sums_kernel, count, n), grid_spec=pltpu....  18.8 us
    pallas_call x1, Pallas kernels, attention(): pl.pallas_call(functools.partial(attention_kernel, pairs), grid_spec=pltp...  13.2 us
  transfers between devices with their start and end apart: 7, of which 1 were waited for; matrix products, arithmetic and copies ran while one was open for 0% of the time, Pallas kernels for 14%

profile of v8, /device:TPU:0, one launch (start us, length us, event | category | flops | bytes accessed | tf_op | source)
XLA Modules:
  0.0 432.2 jit_solution(8564413733713429926)
XLA Ops:
  0.7 0.7 multiply_bitcast_fusion
  1.4 0.1 convert_bitcast_fusion
  1.5 0.5 fusion
  2.0 0.8 pad_maximum_fusion
  2.9 1.3 fusion.9.refs_7_
  4.1 155.1 %front.1 = (bf16[2,2,2,2,2,32,4096]{6,5,4,3,2,1,0:T(8,128)(2,1)}, bf16[2,2,2,2,2,64,1024]{6,5,4,3,2,1,0:T(8,128)(2,1)}, bf16[2,2,2,2,2,32,6144]{6,5,4,3,2,1,0:T(...) custom-call(bf16[32,2048]{1,0:T(8,128)(2,1)} %refs_0_.1, ...), custom_call_target="tpu_custom_call" | custom-call | tf_op jit(solution)/shard_map/front/pallas_call | solution.py:776
  159.3 13.2 %attention.1 = (f32[256,2048]{1,0:T(8,128)}, bf16[256,2048]{1,0:T(8,128)(2,1)}, f32[256,2048]{1,0:T(8,128)}) custom-call(s32[16]{0:T(128)} %bitcast.51, bf16[256,2048]{1,0:T(8,128)(2,1)} %get-tuple-element.62.q_ref, bf16[2048,1024]{1,0:T(8,128)(2,1)} %bitcast.42, bf16[2048,1024]{1,0:T(8,128)(2,1)} %bitcast.44), custom_call_target="tpu_custom_call" | custom-call | tf_op jit(solution)/shard_map/attention/pallas_call | solution.py:475
  172.5 0.7 collective-permute-start.5
  173.1 22.2 %middle.1 = (bf16[256,1024]{1,0:T(8,128)(2,1)}, bf16[256,3072]{1,0:T(8,128)(2,1)}, bf16[256,3072]{1,0:T(8,128)(2,1)}, bf16[256,3072]{1,0:T(8,128)(2,1)}, bf16[25...) custom-call(bf16[256,2048]{1,0:T(8,128)(2,1)} %get-tuple-element.65., ...), custom_call_target="tpu_custom_call" | custom-call | tf_op jit(solution)/shard_map/middle/pallas_call | solution.py:1271
  195.3 0.1 collective-permute-start.6
  195.4 0.5 collective-permute-start.3
  195.8 0.1 collective-permute-start.1
  195.9 0.4 collective-permute-start.2
  196.4 1.1 collective-permute-done.6.refs_1_
  197.5 0.1 collective-permute-start.4
  197.6 0.6 copy-done.3
  198.3 0.1 collective-permute-start
  198.4 28.6 %attention_back.1 = (f32[256,2048]{1,0:T(8,128)}, bf16[2048,1024]{1,0:T(8,128)(2,1)}, bf16[2048,1024]{1,0:T(8,128)(2,1)}) custom-call(s32[16]{0:T(128)} %bitcast.52, bf16[256,2048]{1,0:T(8,128)(2,1)} %get-tuple-element.62.q_ref, bf16[2048,1024]{1,0:T(8,128)(2,1)} %bitcast.43, bf16[2048,1024]{1,0:T(8,128)(2,1)} %bitcast.45, ...), custom_call_target="tpu_custom_call" | custom-call | flops 12079595520 | bytes 24117248 | tf_op jit(solution)/shard_map/attention_back/pallas_call | solution.py:540
  227.0 4.5 %chip_sums.5 = bf16[1024,1024]{1,0:T(8,128)(2,1)} custom-call(s32[1]{0:T(128)} %bitcast.15.core, bf16[256,2048]{1,0:T(8,128)(2,1)} %get-tuple-element.65.alow_ref.left, bf16[256,2048]{1,0:T(8,128)(2,1)} %copy-done.2, bf16[256,1024]{1,0:T(8,128)(2,1)} %get-tuple-element.78.refs_0_, bf16[256,1024]{1,0:T(8,128)(2,1)} %copy-done.3), custom_call_target="tpu_custom_call" | custom-call | tf_op jit(solution)/shard_map/chip_sums/pallas_call | solution.py:853
  231.6 5.8 %chip_sums.4 = bf16[1536,1024]{1,0:T(8,128)(2,1)} custom-call(s32[1]{0:T(128)} %bitcast.15.core, bf16[256,3072]{1,0:T(8,128)(2,1)} %get-tuple-element.77.left, bf16[256,3072]{1,0:T(8,128)(2,1)} %collective-permute-done.3.left_other, bf16[256,1024]{1,0:T(8,128)(2,1)} %bitcast.49, bf16[256,1024]{1,0:T(8,128)(2,1)} %collective-permute-done.4.refs_1_), custom_call_target="tpu_custom_call" | custom-call | tf_op jit(solution)/shard_map/chip_sums/pallas_call | solution.py:853
  237.4 1.1 copy-done.1
  238.5 8.5 %chip_sums.3 = (bf16[512,3072]{1,0:T(8,128)(2,1)}, bf16[512,3072]{1,0:T(8,128)(2,1)}) custom-call(s32[1]{0:T(128)} %bitcast.15.core, bf16[256,1024]{1,0:T(8,128)(2,1)} %get-tuple-element.72.left, bf16[256,1024]{1,0:T(8,128)(2,1)} %collective-permute-done.left_other, bf16[256,3072]{1,0:T(8,128)(2,1)} %get-tuple-element.73.refs_0_, ...), custom_call_target="tpu_custom_call" | custom-call | tf_op jit(solution)/shard_map/chip_sums/pallas_call | solution.py:853
  247.0 181.9 %back.1 = (f32[32,3072]{1,0:T(8,128)}, f32[32,3072]{1,0:T(8,128)}, f32[96,1024]{1,0:T(8,128)}, f32[64,1024]{1,0:T(8,128)}, f32[32,2048]{1,0:T(8,128)}, /*index=5...) custom-call(bf16[2,2,4,32,3072]{4,3,2,1,0:T(8,128)(2,1)} %bitcast.46, ...), custom_call_target="tpu_custom_call" | custom-call | tf_op jit(solution)/shard_map/back/pallas_call | solution.py:1138
  428.9 3.2 handed.1
  (13 shorter events, 0.0 us)
Async XLA Ops:
  172.5 25.1 %collective-permute-start.5 = (bf16[256,2048]{1,0:T(8,128)(2,1)}, bf16[256,2048]{1,0:T(8,128)(2,1)S(1)}, u32[]{:S(2)}, u32[]{:S(2)}) collective-permute-start(bf16[256,2048]{1,0:T(8,128)(2,1)} %get-tuple-element.65.alow_ref.left), channel_id=1, source_target_pairs={{0,4},{4,0},{8,12},{12,8},{16,20},{20,16},{24,28},{28,24},{1,5},{5... | collective-permute-start | bytes 3145736 | tf_op jit(solution)/shard_map/ppermute | solution.py:1363
  173.1 24.4 %copy-start = (bf16[1,256,1024]{2,1,0:T(8,128)(2,1)S(1)}, bf16[1,256,1024]{2,1,0:T(8,128)(2,1)}, u32[]{:S(2)}) copy-start(bf16[1,256,1024]{2,1,0:T(8,128)(2,1)} %param.15) | copy-start | bytes 1572868
  195.3 2.2 collective-permute-start.6
  195.4 36.2 %collective-permute-start.3 = (bf16[256,3072]{1,0:T(8,128)(2,1)}, bf16[256,3072]{1,0:T(8,128)(2,1)}, u32[]{:S(2)}, u32[]{:S(2)}) collective-permute-start(bf16[256,3072]{1,0:T(8,128)(2,1)} %get-tuple-element.77.left), channel_id=1, source_target_pairs={{0,4},{4,0},{8,12},{12,8},{16,20},{20,16},{24,28},{28,24},{1,5},{5... | collective-permute-start | bytes 4718600 | tf_op jit(solution)/shard_map/ppermute | solution.py:1363
  195.8 41.5 %collective-permute-start.1 = (bf16[256,3072]{1,0:T(8,128)(2,1)}, bf16[256,3072]{1,0:T(8,128)(2,1)S(1)}, u32[]{:S(2)}, u32[]{:S(2)}) collective-permute-start(bf16[256,3072]{1,0:T(8,128)(2,1)} %get-tuple-element.73.refs_0_), channel_id=1, source_target_pairs={{0,4},{4,0},{8,12},{12,8},{16,20},{20,16},{24,28},{28,24},{1,5},{5... | collective-permute-start | bytes 4718600 | tf_op jit(solution)/shard_map/ppermute | solution.py:1363
  195.9 41.4 %collective-permute-start.2 = (bf16[256,3072]{1,0:T(8,128)(2,1)}, bf16[256,3072]{1,0:T(8,128)(2,1)}, u32[]{:S(2)}, u32[]{:S(2)}) collective-permute-start(bf16[256,3072]{1,0:T(8,128)(2,1)} %get-tuple-element.74.refs_2_), channel_id=1, source_target_pairs={{0,4},{4,0},{8,12},{12,8},{16,20},{20,16},{24,28},{28,24},{1,5},{5... | collective-permute-start | bytes 4718600 | tf_op jit(solution)/shard_map/ppermute | solution.py:1363
  197.5 0.8 copy-start.3
  197.5 34.1 %collective-permute-start.4 = (bf16[256,1024]{1,0:T(8,128)(2,1)S(1)}, bf16[256,1024]{1,0:T(8,128)(2,1)}, u32[]{:S(2)}, u32[]{:S(2)}) collective-permute-start(bf16[256,1024]{1,0:T(8,128)(2,1)S(1)} %bitcast.50), channel_id=1, source_target_pairs={{0,4},{4,0},{8,12},{12,8},{16,20},{20,16},{24,28},{28,24},{1,5},{5... | collective-permute-start | bytes 1572872 | tf_op jit(solution)/shard_map/ppermute | solution.py:1363
  198.2 28.8 %copy-start.2 = (bf16[256,2048]{1,0:T(8,128)(2,1)}, bf16[256,2048]{1,0:T(8,128)(2,1)S(1)}, u32[]{:S(2)}) copy-start(bf16[256,2048]{1,0:T(8,128)(2,1)S(1)} %collective-permute-done.5.left_other) | copy-start | bytes 3145732
  198.3 39.1 %collective-permute-start = (bf16[256,1024]{1,0:T(8,128)(2,1)}, bf16[256,1024]{1,0:T(8,128)(2,1)}, u32[]{:S(2)}, u32[]{:S(2)}) collective-permute-start(bf16[256,1024]{1,0:T(8,128)(2,1)} %get-tuple-element.72.left), channel_id=1, source_target_pairs={{0,4},{4,0},{8,12},{12,8},{16,20},{20,16},{24,28},{28,24},{1,5},{5... | collective-permute-start | bytes 1572872 | tf_op jit(solution)/shard_map/ppermute | solution.py:1363
  237.3 1.2 copy-start.1
